TPU v7x, 16 devices: a 4x2x1 block of a 4x4x8 slice. The times are simulated.
16 devices in a mesh: rep: 4 (over y, z, core), dp: 4 (over x).
Axes of the slice: x: 4, y: 2, z: 1, core: 2. Of those that a mesh axis runs over, the one named last changes fastest.
The devices are a block of a 4x4x8 slice.
Arguments:
- g_w_gate: bfloat16 [16, 2, 512, 8192], P(('rep', 'dp')), parts along dimension 0
- g_w_up: bfloat16 [16, 2, 512, 8192], P(('rep', 'dp')), parts along dimension 0
- g_w_down: bfloat16 [16, 2, 8192, 512], P(('rep', 'dp')), parts along dimension 0
- w_gate: bfloat16 [2, 512, 8192], replicated
- w_up: bfloat16 [2, 512, 8192], replicated
- w_down: bfloat16 [2, 8192, 512], replicated
- m_w_gate: float32 [2, 512, 8192], P(None, 'dp')
- m_w_up: float32 [2, 512, 8192], P(None, 'dp')
- m_w_down: float32 [2, 8192, 512], P(None, 'dp')
- v_w_gate: float32 [2, 512, 8192], P(None, 'dp')
- v_w_up: float32 [2, 512, 8192], P(None, 'dp')
- v_w_down: float32 [2, 8192, 512], P(None, 'dp')
Outputs:
- output 1: bfloat16 [8, 512, 8192], P('rep'), parts along dimension 0
- output 2: bfloat16 [8, 512, 8192], P('rep'), parts along dimension 0
- output 3: bfloat16 [8, 8192, 512], P('rep'), parts along dimension 0
- output 4: float32 [8, 512, 8192], P('rep', 'dp'), parts along dimension 0
- output 5: float32 [8, 512, 8192], P('rep', 'dp'), parts along dimension 0
- output 6: float32 [8, 8192, 512], P('rep', 'dp'), parts along dimension 0
- output 7: float32 [8, 512, 8192], P('rep', 'dp'), parts along dimension 0
- output 8: float32 [8, 512, 8192], P('rep', 'dp'), parts along dimension 0
- output 9: float32 [8, 8192, 512], P('rep', 'dp'), parts along dimension 0
There are 4 independent parts. A program takes and returns all parts, laid end to end along the dimension named above; an argument that names none is the same for every part.
All inputs are finite; a program needn't handle non-finite values.
Results may differ from a plain program's by a relative error of at most 0.022.
Values are sent between devices in bfloat16 or wider.
A program may use at most 768 MiB of HBM per device.

v0:
```python
import jax
import jax.numpy as jnp
from jax import lax
from jax.experimental import pallas as pl
from jax.experimental.pallas import tpu as pltpu
from jax.sharding import PartitionSpec as P


def adamw(w, m, v, g):
    m = 0.9 * m + 0.1 * g
    v = 0.95 * v + 0.05 * g * g
    step = m * lax.rsqrt(v + 1e-8) + 0.1 * w
    return (w - 0.02 * step).astype(jnp.bfloat16), m, v


def update(me, arrived, term, w, m, v):
    layers, rows, columns = m.shape
    half = rows // 2
    parts = max(1, half * columns * 4 // (1 << 20))
    tile = half // parts

    def kernel(me_ref, up_ref, down_ref, t_ref, w_ref, m_ref, v_ref, out_ref, m_out, v_out, up_out, down_out):
        for side, (in_ref, o_ref) in enumerate(((up_ref, up_out), (down_ref, down_out))):

            @pl.when(pl.program_id(1) == side)
            def _():
                g = (in_ref[0].astype(jnp.float32) + t_ref[0, 0].astype(jnp.float32)).astype(jnp.bfloat16)
                new, m_new, v_new = adamw(w_ref[0].astype(jnp.float32), m_ref[0], v_ref[0], g.astype(jnp.float32))
                out_ref[0], o_ref[0], m_out[0], v_out[0] = new, new, m_new, v_new

    def row(s, p):
        return s * parts + p

    up = pl.BlockSpec((1, tile, columns), lambda l, s, p, me: (l, jnp.where(s == 0, p, parts - 1), 0))
    down = pl.BlockSpec((1, tile, columns), lambda l, s, p, me: (l, jnp.where(s == 0, 0, p), 0))
    whole = pl.BlockSpec((1, tile, columns), lambda l, s, p, me: (l, me[0] * 2 * parts + row(s, p), 0))
    local = pl.BlockSpec((1, tile, columns), lambda l, s, p, me: (l, row(s, p), 0))
    t_spec = pl.BlockSpec((1, 1, tile, columns), lambda l, s, p, me: (0, l, me[0] * 2 * parts + row(s, p), 0))
    piece = jax.ShapeDtypeStruct((layers, half, columns), jnp.bfloat16)
    moment = jax.ShapeDtypeStruct(m.shape, jnp.float32)
    size = layers * rows * columns
    return pl.pallas_call(
        kernel,
        out_shape=(jax.ShapeDtypeStruct(w.shape, jnp.bfloat16), moment, moment, piece, piece),
        grid_spec=pltpu.PrefetchScalarGridSpec(
            num_scalar_prefetch=1,
            grid=(layers, 2, parts),
            in_specs=[up, down, t_spec, whole, local, local],
            out_specs=(whole, local, local, up, down),
        ),
        cost_estimate=pl.CostEstimate(flops=20 * size, bytes_accessed=26 * size, transcendentals=size),
        name="update",
    )(me, *arrived, term, w, m, v)


def place(axis, hops, whole, pieces, layer, row, half, last):
    layers, rows, columns = pieces[0].shape
    count = whole.shape[1] // (2 * half)

    def kernel(up_ref, down_ref, whole_ref, out_ref, held, in_sems, out_sems):
        del whole_ref
        me = lax.axis_index(axis)
        reads, writes = [], []
        for side, ref in enumerate((up_ref, down_ref)):
            block = lax.rem(me + (count - hops, hops)[side], count)
            start = pl.multiple_of((block * 2 + side) * half, half) + row
            for i in range(layers):
                source = ref.at[i] if last else held.at[side, i]
                if not last:
                    reads.append(pltpu.make_async_copy(ref.at[i], source, in_sems.at[side, i]))
                writes.append(pltpu.make_async_copy(source, out_ref.at[layer + i, pl.ds(start, rows)], out_sems.at[side, i]))
        for read in reads:
            read.start()
        for i, write in enumerate(writes):
            if not last:
                reads[i].wait()
            write.start()
        for write in writes:
            write.wait()

    size = 2 * layers * rows * columns
    return pl.pallas_call(
        kernel,
        out_shape=jax.ShapeDtypeStruct(whole.shape, whole.dtype),
        in_specs=[pl.BlockSpec(memory_space=pltpu.VMEM if last else pl.ANY)] * 2 + [pl.BlockSpec(memory_space=pl.ANY)],
        out_specs=pl.BlockSpec(memory_space=pl.ANY),
        scratch_shapes=[
            pltpu.VMEM((8, 128) if last else (2, layers, rows, columns), whole.dtype),
            pltpu.SemaphoreType.DMA((2, layers)),
            pltpu.SemaphoreType.DMA((2, layers)),
        ],
        input_output_aliases={2: 0},
        compiler_params=pltpu.CompilerParams(vmem_limit_bytes=1 << 20 if last else None),
        cost_estimate=pl.CostEstimate(flops=size, bytes_accessed=4 * size, transcendentals=0),
        name="place",
    )(*pieces, whole)


def solution(mesh):
    n = mesh.shape["dp"]
    ways = tuple(tuple((i, (i + to) % n) for i in range(n)) for to in (1, -1))

    def body(*arrays):
        terms, weights, m, v = (arrays[i : i + 3] for i in (0, 3, 6, 9))
        me = lax.axis_index("dp")
        sides = ((0, 1), (1, -1))

        def block(hops, to):
            return lax.rem(me - to * hops + 2 * n, n)

        def own(t, like, hops, part):
            half, (layer, layers, row, rows) = like.shape[1] // 2, part
            starts = [block(-hops, to) * 2 * half + side * half + row for side, to in sides]
            return [lax.dynamic_slice(t, (0, layer, start, 0), (1, layers, rows, t.shape[3]))[0] for start in starts]

        def send(pieces):
            moved = []
            for p, way in zip(pieces, ways, strict=True):
                moved.append(lax.ppermute(p, "dp", way))
            return moved

        def add(a, b):
            return (a.astype(jnp.float32) + b.astype(jnp.float32)).astype(jnp.bfloat16)

        def all_of_it(like):
            return [(0, like.shape[0], 0, like.shape[1] // 2)]

        def small_first(like):
            layers, half = like.shape[0], like.shape[1] // 2
            return [(0, 1, 0, half // 4), (0, 1, half // 4, half - half // 4)] + [(1, layers - 1, 0, half)] * (layers > 1)

        def small_last(like):
            layers, half = like.shape[0], like.shape[1] // 2
            quarter = half // 4
            ends = [(layers - 1, 1, 0, half - 2 * quarter)] + [(layers - 1, 1, half - i * quarter, quarter) for i in (2, 1)]
            return [(0, layers - 1, 0, half)] * (layers > 1) + ends

        def join(parts):
            first = jnp.concatenate(parts[:2], axis=1)
            return jnp.concatenate([first, *parts[2:]], axis=0) if len(parts) > 2 else first

        order = (2, 1, 0)
        moving = [None] * 3
        new_w, new_m, new_v = [None] * 3, [None] * 3, [None] * 3
        for k in order:
            if k == order[0]:
                sent = [send(own(terms[k], m[k], n - 1, part)) for part in small_first(m[k])]
                moving[k] = [join(parts) for parts in zip(*sent, strict=True)]
            else:
                moving[k] = send(own(terms[k], m[k], n - 1, all_of_it(m[k])[0]))
        for hop in range(1, n - 1):
            for k in order:
                moving[k] = send([add(a, b) for a, b in zip(moving[k], own(terms[k], m[k], n - 1 - hop, all_of_it(m[k])[0]), strict=True)])
        at = me[None].astype(jnp.int32)
        for k in order:
            new_w[k], new_m[k], new_v[k], *pieces = update(at, moving[k], terms[k], weights[k], m[k], v[k])
            moving[k] = [(part, send(pieces)) for part in all_of_it(m[k])]
        for hop in range(1, n):
            for k in order:
                here = moving[k]
                if hop < n - 1:
                    parts = small_last(m[k]) if (hop, k) == (n - 2, order[-1]) else all_of_it(m[k])
                    ((_, whole_piece),) = here
                    moving[k] = [
                        (part, send([p[part[0] : part[0] + part[1], part[2] : part[2] + part[3]] for p in whole_piece])) for part in parts
                    ]
                for i, (part, pieces) in enumerate(here):
                    last = (hop, k, i) == (n - 1, order[-1], len(here) - 1)
                    new_w[k] = place("dp", hop, new_w[k], pieces, part[0], part[2], m[k].shape[1] // 2, last)
        return (*new_w, *new_m, *new_v)

    all_of, cut = P(None, None, None), P(None, "dp", None)
    return jax.shard_map(
        body,
        mesh=mesh,
        in_specs=(P(("rep", "dp"), None, None, None),) * 3 + (all_of,) * 3 + (cut,) * 6,
        out_specs=(P("rep", None, None),) * 3 + (P("rep", "dp", None),) * 6,
        check_vma=False,
    )
```

profile of v0, /device:TPU:112, one launch (start us, length us, event | category | flops | bytes accessed | tf_op | source)
XLA Modules:
  0.0 878.1 jit_solution(17699166872439385447)
XLA Ops:
  0.7 2.6 dynamic-slice_bitcast_fusion.6
  3.3 2.3 collective-permute-start.31
  5.6 4.7 dynamic-slice_bitcast_fusion.2
  15.1 2.8 collective-permute-start.35
  17.9 2.6 dynamic-slice_bitcast_fusion.4
  20.6 55.0 %collective-permute-done.30 = bf16[1,256,512]{2,1,0:T(8,128)(2,1)S(1)} collective-permute-done((bf16[1,256,512]{2,1,0:T(8,128)(2,1)S(1)}, bf16[1,256,512]{2,1,0:T(8,128)(2,1)S(1)}, u32[]{:S(2)}, u32[]{:S(2)}) %collective-permute-start.30) | collective-permute-done | bytes 262176 | tf_op jit(solution)/shard_map/ppermute | solution.py:119
  76.5 3.0 collective-permute-start.37
  80.0 4.1 dynamic-slice_bitcast_fusion
  84.2 33.9 %collective-permute-done.36 = bf16[1,768,512]{2,1,0:T(8,128)(2,1)S(1)} collective-permute-done((bf16[1,768,512]{2,1,0:T(8,128)(2,1)}, bf16[1,768,512]{2,1,0:T(8,128)(2,1)S(1)}, u32[]{:S(2)}, u32[]{:S(2)}) %collective-permute-start.36) | collective-permute-done | bytes 786464 | tf_op jit(solution)/shard_map/ppermute | solution.py:119
  118.8 3.0 collective-permute-start.21
  121.8 4.6 fusion.1
  126.4 3.2 collective-permute-start.38
  129.6 6.4 fusion.9
  136.0 32.3 %collective-permute-done.18 = bf16[2,64,8192]{2,1,0:T(8,128)(2,1)S(1)} collective-permute-done((bf16[2,64,8192]{2,1,0:T(8,128)(2,1)}, bf16[2,64,8192]{2,1,0:T(8,128)(2,1)S(1)}, u32[]{:S(2)}, u32[]{:S(2)}) %collective-permute-start.18) | collective-permute-done | bytes 2097184 | tf_op jit(solution)/shard_map/ppermute | solution.py:119
  168.3 2.0 collective-permute-start.4
  170.4 5.2 fusion.5
  175.6 37.8 %collective-permute-done.33 = bf16[2,1024,512]{2,1,0:T(8,128)(2,1)} collective-permute-done((bf16[2,1024,512]{2,1,0:T(8,128)(2,1)}, bf16[2,1024,512]{2,1,0:T(8,128)(2,1)}, u32[]{:S(2)}, u32[]{:S(2)}) %collective-permute-start.33) | collective-permute-done | bytes 2097184 | tf_op jit(solution)/shard_map/ppermute | solution.py:119
  213.4 2.0 collective-permute-start.22
  215.4 6.1 fusion
  221.5 36.9 %collective-permute-done.1 = bf16[2,64,8192]{2,1,0:T(8,128)(2,1)} collective-permute-done((bf16[2,64,8192]{2,1,0:T(8,128)(2,1)}, bf16[2,64,8192]{2,1,0:T(8,128)(2,1)}, u32[]{:S(2)}, u32[]{:S(2)}) %collective-permute-start.1) | collective-permute-done | bytes 2097184 | tf_op jit(solution)/shard_map/ppermute | solution.py:119
  258.3 2.0 collective-permute-start.39
  260.4 7.0 fusion.8
  267.4 35.8 %collective-permute-done.19 = bf16[2,64,8192]{2,1,0:T(8,128)(2,1)S(1)} collective-permute-done((bf16[2,64,8192]{2,1,0:T(8,128)(2,1)}, bf16[2,64,8192]{2,1,0:T(8,128)(2,1)S(1)}, u32[]{:S(2)}, u32[]{:S(2)}) %collective-permute-start.19) | collective-permute-done | bytes 2097184 | tf_op jit(solution)/shard_map/ppermute | solution.py:119
  303.2 2.0 collective-permute-start.5
  305.2 5.2 fusion.4
  310.4 37.7 %collective-permute-done.34.up_ref = bf16[2,1024,512]{2,1,0:T(8,128)(2,1)S(1)} collective-permute-done((bf16[2,1024,512]{2,1,0:T(8,128)(2,1)}, bf16[2,1024,512]{2,1,0:T(8,128)(2,1)S(1)}, u32[]{:S(2)}, u32[]{:S(2)}) %collective-permute-start.34) | collective-permute-done | bytes 2097184 | tf_op jit(solution)/shard_map/ppermute | solution.py:119
  348.1 2.0 collective-permute-start.23
  351.5 20.4 %update.5 = (bf16[2,8192,512]{2,1,0:T(8,128)(2,1)}, f32[2,2048,512]{2,1,0:T(8,128)}, f32[2,2048,512]{2,1,0:T(8,128)}, bf16[2,1024,512]{2,1,0:T(8,128)(2,1)}, bf16[2,1024,512]{2,1,0:T(8,128)(2,1)}) custom-call(s32[1]{0:T(128)} %bitcast.me_ref, bf16[2,1024,512]{2,1,0:T(8,128)(2,1)} %copy-done.5, bf16[2,1024,512]{2,1,0:T(8,128)(2,1)} %copy-done.6, ...), custom_call_target="tpu_custom_call" | custom-call | flops 41943040 | bytes 54525952 | tf_op jit(solution)/shard_map/update/pallas_call | solution.py:42
  371.9 21.2 %collective-permute-done.2.up_ref = bf16[2,64,8192]{2,1,0:T(8,128)(2,1)} collective-permute-done((bf16[2,64,8192]{2,1,0:T(8,128)(2,1)}, bf16[2,64,8192]{2,1,0:T(8,128)(2,1)}, u32[]{:S(2)}, u32[]{:S(2)}) %collective-permute-start.2) | collective-permute-done | bytes 2097184 | tf_op jit(solution)/shard_map/ppermute | solution.py:119
  393.2 20.7 %update.3 = (bf16[2,512,8192]{2,1,0:T(8,128)(2,1)}, f32[2,128,8192]{2,1,0:T(8,128)}, f32[2,128,8192]{2,1,0:T(8,128)}, bf16[2,64,8192]{2,1,0:T(8,128)(2,1)}, bf16[2,64,8192]{2,1,0:T(8,128)(2,1)}) custom-call(s32[1]{0:T(128)} %bitcast.me_ref, bf16[2,64,8192]{2,1,0:T(8,128)(2,1)} %collective-permute-done.2.up_ref, ...), custom_call_target="tpu_custom_call" | custom-call | flops 41943040 | bytes 54525952 | tf_op jit(solution)/shard_map/update/pallas_call | solution.py:42
  415.1 2.0 collective-permute-start.43
  417.1 21.0 %collective-permute-done.20.up_ref = bf16[2,64,8192]{2,1,0:T(8,128)(2,1)} collective-permute-done((bf16[2,64,8192]{2,1,0:T(8,128)(2,1)}, bf16[2,64,8192]{2,1,0:T(8,128)(2,1)}, u32[]{:S(2)}, u32[]{:S(2)}) %collective-permute-start.20) | collective-permute-done | bytes 2097184 | tf_op jit(solution)/shard_map/ppermute | solution.py:119
  438.1 2.0 collective-permute-start.9
  440.1 20.5 %update.4 = (bf16[2,512,8192]{2,1,0:T(8,128)(2,1)}, f32[2,128,8192]{2,1,0:T(8,128)}, f32[2,128,8192]{2,1,0:T(8,128)}, bf16[2,64,8192]{2,1,0:T(8,128)(2,1)}, bf16[2,64,8192]{2,1,0:T(8,128)(2,1)}) custom-call(s32[1]{0:T(128)} %bitcast.me_ref, bf16[2,64,8192]{2,1,0:T(8,128)(2,1)} %collective-permute-done.20.up_ref, ...), custom_call_target="tpu_custom_call" | custom-call | flops 41943040 | bytes 54525952 | tf_op jit(solution)/shard_map/update/pallas_call | solution.py:42
  460.6 22.3 %collective-permute-done.40.up_ref = bf16[2,1024,512]{2,1,0:T(8,128)(2,1)S(1)} collective-permute-done((bf16[2,1024,512]{2,1,0:T(8,128)(2,1)}, bf16[2,1024,512]{2,1,0:T(8,128)(2,1)S(1)}, u32[]{:S(2)}, u32[]{:S(2)}) %collective-permute-start.40) | collective-permute-done | bytes 2097184 | tf_op jit(solution)/shard_map/ppermute | solution.py:119
  482.9 2.0 collective-permute-start.27
  485.0 43.0 %collective-permute-done.6.up_ref = bf16[2,64,8192]{2,1,0:T(8,128)(2,1)} collective-permute-done((bf16[2,64,8192]{2,1,0:T(8,128)(2,1)}, bf16[2,64,8192]{2,1,0:T(8,128)(2,1)}, u32[]{:S(2)}, u32[]{:S(2)}) %collective-permute-start.6) | collective-permute-done | bytes 2097184 | tf_op jit(solution)/shard_map/ppermute | solution.py:119
  528.0 3.2 collective-permute-start.10
  531.2 41.6 %collective-permute-done.24.up_ref = bf16[2,64,8192]{2,1,0:T(8,128)(2,1)S(1)} collective-permute-done((bf16[2,64,8192]{2,1,0:T(8,128)(2,1)}, bf16[2,64,8192]{2,1,0:T(8,128)(2,1)S(1)}, u32[]{:S(2)}, u32[]{:S(2)}) %collective-permute-start.24) | collective-permute-done | bytes 2097184 | tf_op jit(solution)/shard_map/ppermute | solution.py:119
  572.8 2.0 collective-permute-start.44
  574.9 42.9 %collective-permute-done.7.up_ref = bf16[2,64,8192]{2,1,0:T(8,128)(2,1)S(1)} collective-permute-done((bf16[2,64,8192]{2,1,0:T(8,128)(2,1)}, bf16[2,64,8192]{2,1,0:T(8,128)(2,1)S(1)}, u32[]{:S(2)}, u32[]{:S(2)}) %collective-permute-start.7) | collective-permute-done | bytes 2097184 | tf_op jit(solution)/shard_map/ppermute | solution.py:119
  617.8 2.0 collective-permute-start.28
  620.7 42.1 %collective-permute-done.41.up_ref = bf16[2,1024,512]{2,1,0:T(8,128)(2,1)} collective-permute-done((bf16[2,1024,512]{2,1,0:T(8,128)(2,1)S(1)}, bf16[2,1024,512]{2,1,0:T(8,128)(2,1)}, u32[]{:S(2)}, u32[]{:S(2)}) %collective-permute-start.41) | collective-permute-done | bytes 2097184 | tf_op jit(solution)/shard_map/ppermute | solution.py:119
  662.8 2.0 collective-permute-start.15
  665.0 42.8 %collective-permute-done.25.up_ref = bf16[2,64,8192]{2,1,0:T(8,128)(2,1)} collective-permute-done((bf16[2,64,8192]{2,1,0:T(8,128)(2,1)S(1)}, bf16[2,64,8192]{2,1,0:T(8,128)(2,1)}, u32[]{:S(2)}, u32[]{:S(2)}) %collective-permute-start.25) | collective-permute-done | bytes 2097184 | tf_op jit(solution)/shard_map/ppermute | solution.py:119
  707.8 3.2 collective-permute-start.13
  711.0 13.5 %collective-permute-done.12.up_ref = bf16[1,16,8192]{2,1,0:T(8,128)(2,1)S(1)} collective-permute-done((bf16[1,16,8192]{2,1,0:T(8,128)(2,1)S(1)}, bf16[1,16,8192]{2,1,0:T(8,128)(2,1)S(1)}, u32[]{:S(2)}, u32[]{:S(2)}) %collective-permute-start.12) | collective-permute-done | bytes 262176 | tf_op jit(solution)/shard_map/ppermute | solution.py:119
  724.5 2.0 collective-permute-start.11
  726.5 7.1 collective-permute-done.11.down_ref
  733.7 3.0 collective-permute-start.45
  737.5 3.2 collective-permute-start.29
  740.8 6.2 collective-permute-done.16.up_ref
  747.0 2.0 collective-permute-start.17
  749.0 94.1 %collective-permute-done.17.down_ref = bf16[1,64,8192]{2,1,0:T(8,128)(2,1)S(1)} collective-permute-done((bf16[1,64,8192]{2,1,0:T(8,128)(2,1)S(1)}, bf16[1,64,8192]{2,1,0:T(8,128)(2,1)S(1)}, u32[]{:S(2)}, u32[]{:S(2)}) %collective-permute-start.17) | collective-permute-done | bytes 1048608 | tf_op jit(solution)/shard_map/ppermute | solution.py:119
  844.1 3.3 place.21.whole_ref
  847.4 3.3 place.18.whole_ref
  850.7 3.3 place.12.whole_ref
  854.0 3.3 place.22.whole_ref
  857.4 3.3 place.13.whole_ref
  860.7 2.6 place.14.whole_ref
  863.3 2.0 place.15.whole_ref
  865.3 3.3 place.19.whole_ref
  871.3 3.3 place.23
  874.6 3.3 place.20
  (99 shorter events, 15.2 us)
Async XLA Ops:
  3.3 76.2 %collective-permute-start.31 = (bf16[1,768,512]{2,1,0:T(8,128)(2,1)}, bf16[1,768,512]{2,1,0:T(8,128)(2,1)}, u32[]{:S(2)}, u32[]{:S(2)}) collective-permute-start(bf16[1,768,512]{2,1,0:T(8,128)(2,1)} %get-tuple-element.46), channel_id=1, source_target_pairs={{0,1},{1,2},{2,3},{3,0},{4,5},{5,6},{6,7},{7,4},{8,9},{9,10},{10,1... | collective-permute-start | bytes 2359304 | tf_op jit(solution)/shard_map/ppermute | solution.py:119
  10.3 116.1 %collective-permute-start = (bf16[2,64,8192]{2,1,0:T(8,128)(2,1)}, bf16[2,64,8192]{2,1,0:T(8,128)(2,1)S(1)}, u32[]{:S(2)}, u32[]{:S(2)}) collective-permute-start(bf16[2,64,8192]{2,1,0:T(8,128)(2,1)} %get-tuple-element.60), channel_id=1, source_target_pairs={{0,1},{1,2},{2,3},{3,0},{4,5},{5,6},{6,7},{7,4},{8,9},{9,10},{10,1... | collective-permute-start | bytes 6291464 | tf_op jit(solution)/shard_map/ppermute | solution.py:119
  11.9 117.7 %collective-permute-start.3 = (bf16[2,64,8192]{2,1,0:T(8,128)(2,1)}, bf16[2,64,8192]{2,1,0:T(8,128)(2,1)}, u32[]{:S(2)}, u32[]{:S(2)}) collective-permute-start(bf16[2,64,8192]{2,1,0:T(8,128)(2,1)} %get-tuple-element.59), channel_id=1, source_target_pairs={{0,3},{1,0},{2,1},{3,2},{4,7},{5,4},{6,5},{7,6},{8,11},{9,8},{10,9... | collective-permute-start | bytes 6291464 | tf_op jit(solution)/shard_map/ppermute | solution.py:119
  14.6 60.9 %collective-permute-start.30 = (bf16[1,256,512]{2,1,0:T(8,128)(2,1)S(1)}, bf16[1,256,512]{2,1,0:T(8,128)(2,1)S(1)}, u32[]{:S(2)}, u32[]{:S(2)}) collective-permute-start(bf16[1,256,512]{2,1,0:T(8,128)(2,1)S(1)} %get-tuple-element.44), channel_id=1, source_target_pairs={{0,1},{1,2},{2,3},{3,0},{4,5},{5,6},{6,7},{7,4},{8,9},{9,10},{10,1... | collective-permute-start | bytes 786440 | tf_op jit(solution)/shard_map/ppermute | solution.py:119
  15.1 60.7 %collective-permute-start.35 = (bf16[1,256,512]{2,1,0:T(8,128)(2,1)S(1)}, bf16[1,256,512]{2,1,0:T(8,128)(2,1)S(1)}, u32[]{:S(2)}, u32[]{:S(2)}) collective-permute-start(bf16[1,256,512]{2,1,0:T(8,128)(2,1)S(1)} %get-tuple-element.43), channel_id=1, source_target_pairs={{0,3},{1,0},{2,1},{3,2},{4,7},{5,4},{6,5},{7,6},{8,11},{9,8},{10,9... | collective-permute-start | bytes 786440 | tf_op jit(solution)/shard_map/ppermute | solution.py:119
  75.5 43.2 %collective-permute-start.32 = (bf16[1,1024,512]{2,1,0:T(8,128)(2,1)}, bf16[1,1024,512]{2,1,0:T(8,128)(2,1)}, u32[]{:S(2)}, u32[]{:S(2)}) collective-permute-start(bf16[1,1024,512]{2,1,0:T(8,128)(2,1)} %get-tuple-element.48), channel_id=1, source_target_pairs={{0,1},{1,2},{2,3},{3,0},{4,5},{5,6},{6,7},{7,4},{8,9},{9,10},{10,1... | collective-permute-start | bytes 3145736 | tf_op jit(solution)/shard_map/ppermute | solution.py:119
  76.5 45.3 %collective-permute-start.37 = (bf16[1,1024,512]{2,1,0:T(8,128)(2,1)S(1)}, bf16[1,1024,512]{2,1,0:T(8,128)(2,1)}, u32[]{:S(2)}, u32[]{:S(2)}) collective-permute-start(bf16[1,1024,512]{2,1,0:T(8,128)(2,1)S(1)} %get-tuple-element.47), channel_id=1, source_target_pairs={{0,3},{1,0},{2,1},{3,2},{4,7},{5,4},{6,5},{7,6},{8,11},{9,8},{10,9... | collective-permute-start | bytes 3145736 | tf_op jit(solution)/shard_map/ppermute | solution.py:119
  79.5 42.3 %copy-start.14 = (bf16[1,256,512]{2,1,0:T(8,128)(2,1)S(1)}, bf16[1,256,512]{2,1,0:T(8,128)(2,1)}, u32[]{:S(2)}) copy-start(bf16[1,256,512]{2,1,0:T(8,128)(2,1)} %copy-done.13) | copy-start | bytes 786436
  79.5 38.6 %collective-permute-start.36 = (bf16[1,768,512]{2,1,0:T(8,128)(2,1)}, bf16[1,768,512]{2,1,0:T(8,128)(2,1)S(1)}, u32[]{:S(2)}, u32[]{:S(2)}) collective-permute-start(bf16[1,768,512]{2,1,0:T(8,128)(2,1)} %get-tuple-element.45), channel_id=1, source_target_pairs={{0,3},{1,0},{2,1},{3,2},{4,7},{5,4},{6,5},{7,6},{8,11},{9,8},{10,9... | collective-permute-start | bytes 2359304 | tf_op jit(solution)/shard_map/ppermute | solution.py:119
  80.0 90.4 %slice-start = ((s8[16777216]{0:T(1024)(128)(4,1)}), s8[4194304]{0:T(1024)(128)(4,1)S(1)}, s32[]{:S(2)}) async-start(s8[16777216]{0:T(1024)(128)(4,1)} %bitcast.57), calls=%async_computation | async-start | bytes 8388608
  118.1 52.3 %slice-start.1 = ((s8[16777216]{0:T(1024)(128)(4,1)}), s8[4194304]{0:T(1024)(128)(4,1)S(1)}, s32[]{:S(2)}) async-start(s8[16777216]{0:T(1024)(128)(4,1)} %bitcast.57), calls=%async_computation.1 | async-start | bytes 8388608
  118.1 50.3 %collective-permute-start.18 = (bf16[2,64,8192]{2,1,0:T(8,128)(2,1)}, bf16[2,64,8192]{2,1,0:T(8,128)(2,1)S(1)}, u32[]{:S(2)}, u32[]{:S(2)}) collective-permute-start(bf16[2,64,8192]{2,1,0:T(8,128)(2,1)} %get-tuple-element.54), channel_id=1, source_target_pairs={{0,1},{1,2},{2,3},{3,0},{4,5},{5,6},{6,7},{7,4},{8,9},{9,10},{10,1... | collective-permute-start | bytes 6291464 | tf_op jit(solution)/shard_map/ppermute | solution.py:119
  118.8 51.6 %slice-start.2 = ((s8[16777216]{0:T(1024)(128)(4,1)}), s8[4194304]{0:T(1024)(128)(4,1)S(1)}, s32[]{:S(2)}) async-start(s8[16777216]{0:T(1024)(128)(4,1)} %bitcast.57), calls=%async_computation.2 | async-start | bytes 8388608
  118.8 51.6 %collective-permute-start.21 = (bf16[2,64,8192]{2,1,0:T(8,128)(2,1)S(1)}, bf16[2,64,8192]{2,1,0:T(8,128)(2,1)}, u32[]{:S(2)}, u32[]{:S(2)}) collective-permute-start(bf16[2,64,8192]{2,1,0:T(8,128)(2,1)S(1)} %get-tuple-element.53), channel_id=1, source_target_pairs={{0,3},{1,0},{2,1},{3,2},{4,7},{5,4},{6,5},{7,6},{8,11},{9,8},{10,9... | collective-permute-start | bytes 6291464 | tf_op jit(solution)/shard_map/ppermute | solution.py:119
  126.4 87.0 %collective-permute-start.33 = (bf16[2,1024,512]{2,1,0:T(8,128)(2,1)}, bf16[2,1024,512]{2,1,0:T(8,128)(2,1)}, u32[]{:S(2)}, u32[]{:S(2)}) collective-permute-start(bf16[2,1024,512]{2,1,0:T(8,128)(2,1)} %get-tuple-element.42), channel_id=1, source_target_pairs={{0,1},{1,2},{2,3},{3,0},{4,5},{5,6},{6,7},{7,4},{8,9},{9,10},{10,1... | collective-permute-start | bytes 6291464 | tf_op jit(solution)/shard_map/ppermute | solution.py:119
  126.4 44.0 %slice-start.3 = ((s8[16777216]{0:T(1024)(128)(4,1)}), s8[4194304]{0:T(1024)(128)(4,1)S(1)}, s32[]{:S(2)}) async-start(s8[16777216]{0:T(1024)(128)(4,1)} %bitcast.57), calls=%async_computation.3 | async-start | bytes 8388608
  126.4 89.0 %collective-permute-start.38 = (bf16[2,1024,512]{2,1,0:T(8,128)(2,1)S(1)}, bf16[2,1024,512]{2,1,0:T(8,128)(2,1)}, u32[]{:S(2)}, u32[]{:S(2)}) collective-permute-start(bf16[2,1024,512]{2,1,0:T(8,128)(2,1)S(1)} %get-tuple-element.41), channel_id=1, source_target_pairs={{0,3},{1,0},{2,1},{3,2},{4,7},{5,4},{6,5},{7,6},{8,11},{9,8},{10,9... | collective-permute-start | bytes 6291464 | tf_op jit(solution)/shard_map/ppermute | solution.py:119
  136.0 122.3 %collective-permute-start.1 = (bf16[2,64,8192]{2,1,0:T(8,128)(2,1)}, bf16[2,64,8192]{2,1,0:T(8,128)(2,1)}, u32[]{:S(2)}, u32[]{:S(2)}) collective-permute-start(bf16[2,64,8192]{2,1,0:T(8,128)(2,1)} %get-tuple-element.58), channel_id=1, source_target_pairs={{0,1},{1,2},{2,3},{3,0},{4,5},{5,6},{6,7},{7,4},{8,9},{9,10},{10,1... | collective-permute-start | bytes 6291464 | tf_op jit(solution)/shard_map/ppermute | solution.py:119
  168.3 92.0 %collective-permute-start.4 = (bf16[2,64,8192]{2,1,0:T(8,128)(2,1)}, bf16[2,64,8192]{2,1,0:T(8,128)(2,1)}, u32[]{:S(2)}, u32[]{:S(2)}) collective-permute-start(bf16[2,64,8192]{2,1,0:T(8,128)(2,1)} %get-tuple-element.57), channel_id=1, source_target_pairs={{0,3},{1,0},{2,1},{3,2},{4,7},{5,4},{6,5},{7,6},{8,11},{9,8},{10,9... | collective-permute-start | bytes 6291464 | tf_op jit(solution)/shard_map/ppermute | solution.py:119
  175.6 127.6 %collective-permute-start.19 = (bf16[2,64,8192]{2,1,0:T(8,128)(2,1)}, bf16[2,64,8192]{2,1,0:T(8,128)(2,1)S(1)}, u32[]{:S(2)}, u32[]{:S(2)}) collective-permute-start(bf16[2,64,8192]{2,1,0:T(8,128)(2,1)} %get-tuple-element.52), channel_id=1, source_target_pairs={{0,1},{1,2},{2,3},{3,0},{4,5},{5,6},{6,7},{7,4},{8,9},{9,10},{10,1... | collective-permute-start | bytes 6291464 | tf_op jit(solution)/shard_map/ppermute | solution.py:119
  213.4 91.8 %collective-permute-start.22 = (bf16[2,64,8192]{2,1,0:T(8,128)(2,1)}, bf16[2,64,8192]{2,1,0:T(8,128)(2,1)}, u32[]{:S(2)}, u32[]{:S(2)}) collective-permute-start(bf16[2,64,8192]{2,1,0:T(8,128)(2,1)} %get-tuple-element.51), channel_id=1, source_target_pairs={{0,3},{1,0},{2,1},{3,2},{4,7},{5,4},{6,5},{7,6},{8,11},{9,8},{10,9... | collective-permute-start | bytes 6291464 | tf_op jit(solution)/shard_map/ppermute | solution.py:119
  221.5 126.6 %collective-permute-start.34 = (bf16[2,1024,512]{2,1,0:T(8,128)(2,1)}, bf16[2,1024,512]{2,1,0:T(8,128)(2,1)S(1)}, u32[]{:S(2)}, u32[]{:S(2)}) collective-permute-start(bf16[2,1024,512]{2,1,0:T(8,128)(2,1)} %get-tuple-element.40), channel_id=1, source_target_pairs={{0,1},{1,2},{2,3},{3,0},{4,5},{5,6},{6,7},{7,4},{8,9},{9,10},{10,1... | collective-permute-start | bytes 6291464 | tf_op jit(solution)/shard_map/ppermute | solution.py:119
  258.3 91.8 %collective-permute-start.39 = (bf16[2,1024,512]{2,1,0:T(8,128)(2,1)S(1)}, bf16[2,1024,512]{2,1,0:T(8,128)(2,1)S(1)}, u32[]{:S(2)}, u32[]{:S(2)}) collective-permute-start(bf16[2,1024,512]{2,1,0:T(8,128)(2,1)S(1)} %get-tuple-element.39), channel_id=1, source_target_pairs={{0,3},{1,0},{2,1},{3,2},{4,7},{5,4},{6,5},{7,6},{8,11},{9,8},{10,9... | collective-permute-start | bytes 6291464 | tf_op jit(solution)/shard_map/ppermute | solution.py:119
  267.4 125.8 %collective-permute-start.2 = (bf16[2,64,8192]{2,1,0:T(8,128)(2,1)}, bf16[2,64,8192]{2,1,0:T(8,128)(2,1)}, u32[]{:S(2)}, u32[]{:S(2)}) collective-permute-start(bf16[2,64,8192]{2,1,0:T(8,128)(2,1)} %get-tuple-element.56), channel_id=1, source_target_pairs={{0,1},{1,2},{2,3},{3,0},{4,5},{5,6},{6,7},{7,4},{8,9},{9,10},{10,1... | collective-permute-start | bytes 6291464 | tf_op jit(solution)/shard_map/ppermute | solution.py:119
  303.2 90.0 %collective-permute-start.5 = (bf16[2,64,8192]{2,1,0:T(8,128)(2,1)}, bf16[2,64,8192]{2,1,0:T(8,128)(2,1)}, u32[]{:S(2)}, u32[]{:S(2)}) collective-permute-start(bf16[2,64,8192]{2,1,0:T(8,128)(2,1)} %get-tuple-element.55), channel_id=1, source_target_pairs={{0,3},{1,0},{2,1},{3,2},{4,7},{5,4},{6,5},{7,6},{8,11},{9,8},{10,9... | collective-permute-start | bytes 6291464 | tf_op jit(solution)/shard_map/ppermute | solution.py:119
  310.4 127.7 %collective-permute-start.20 = (bf16[2,64,8192]{2,1,0:T(8,128)(2,1)}, bf16[2,64,8192]{2,1,0:T(8,128)(2,1)}, u32[]{:S(2)}, u32[]{:S(2)}) collective-permute-start(bf16[2,64,8192]{2,1,0:T(8,128)(2,1)} %get-tuple-element.50), channel_id=1, source_target_pairs={{0,1},{1,2},{2,3},{3,0},{4,5},{5,6},{6,7},{7,4},{8,9},{9,10},{10,1... | collective-permute-start | bytes 6291464 | tf_op jit(solution)/shard_map/ppermute | solution.py:119
  348.1 3.4 copy-start.5
  348.1 92.0 %collective-permute-start.23 = (bf16[2,64,8192]{2,1,0:T(8,128)(2,1)}, bf16[2,64,8192]{2,1,0:T(8,128)(2,1)}, u32[]{:S(2)}, u32[]{:S(2)}) collective-permute-start(bf16[2,64,8192]{2,1,0:T(8,128)(2,1)} %get-tuple-element.49), channel_id=1, source_target_pairs={{0,3},{1,0},{2,1},{3,2},{4,7},{5,4},{6,5},{7,6},{8,11},{9,8},{10,9... | collective-permute-start | bytes 6291464 | tf_op jit(solution)/shard_map/ppermute | solution.py:119
  350.1 1.3 copy-start.6
  371.9 111.0 %collective-permute-start.40 = (bf16[2,1024,512]{2,1,0:T(8,128)(2,1)}, bf16[2,1024,512]{2,1,0:T(8,128)(2,1)S(1)}, u32[]{:S(2)}, u32[]{:S(2)}) collective-permute-start(bf16[2,1024,512]{2,1,0:T(8,128)(2,1)} %get-tuple-element.30), channel_id=1, source_target_pairs={{0,1},{1,2},{2,3},{3,0},{4,5},{5,6},{6,7},{7,4},{8,9},{9,10},{10,1... | collective-permute-start | bytes 6291464 | tf_op jit(solution)/shard_map/ppermute | solution.py:119
  413.8 114.1 %collective-permute-start.6 = (bf16[2,64,8192]{2,1,0:T(8,128)(2,1)}, bf16[2,64,8192]{2,1,0:T(8,128)(2,1)}, u32[]{:S(2)}, u32[]{:S(2)}) collective-permute-start(bf16[2,64,8192]{2,1,0:T(8,128)(2,1)} %get-tuple-element.24), channel_id=1, source_target_pairs={{0,1},{1,2},{2,3},{3,0},{4,5},{5,6},{6,7},{7,4},{8,9},{9,10},{10,1... | collective-permute-start | bytes 6291464 | tf_op jit(solution)/shard_map/ppermute | solution.py:119
  415.1 116.2 %collective-permute-start.43 = (bf16[2,1024,512]{2,1,0:T(8,128)(2,1)}, bf16[2,1024,512]{2,1,0:T(8,128)(2,1)}, u32[]{:S(2)}, u32[]{:S(2)}) collective-permute-start(bf16[2,1024,512]{2,1,0:T(8,128)(2,1)} %get-tuple-element.31), channel_id=1, source_target_pairs={{0,3},{1,0},{2,1},{3,2},{4,7},{5,4},{6,5},{7,6},{8,11},{9,8},{10,9... | collective-permute-start | bytes 6291464 | tf_op jit(solution)/shard_map/ppermute | solution.py:119
  438.1 89.9 %collective-permute-start.9 = (bf16[2,64,8192]{2,1,0:T(8,128)(2,1)}, bf16[2,64,8192]{2,1,0:T(8,128)(2,1)}, u32[]{:S(2)}, u32[]{:S(2)}) collective-permute-start(bf16[2,64,8192]{2,1,0:T(8,128)(2,1)} %get-tuple-element.25), channel_id=1, source_target_pairs={{0,3},{1,0},{2,1},{3,2},{4,7},{5,4},{6,5},{7,6},{8,11},{9,8},{10,9... | collective-permute-start | bytes 6291464 | tf_op jit(solution)/shard_map/ppermute | solution.py:119
  460.6 112.2 %collective-permute-start.24 = (bf16[2,64,8192]{2,1,0:T(8,128)(2,1)}, bf16[2,64,8192]{2,1,0:T(8,128)(2,1)S(1)}, u32[]{:S(2)}, u32[]{:S(2)}) collective-permute-start(bf16[2,64,8192]{2,1,0:T(8,128)(2,1)} %get-tuple-element.27), channel_id=1, source_target_pairs={{0,1},{1,2},{2,3},{3,0},{4,5},{5,6},{6,7},{7,4},{8,9},{9,10},{10,1... | collective-permute-start | bytes 6291464 | tf_op jit(solution)/shard_map/ppermute | solution.py:119
  482.9 361.2 %copy-start.2 = (bf16[2,1024,512]{2,1,0:T(8,128)(2,1)}, bf16[2,1024,512]{2,1,0:T(8,128)(2,1)S(1)}, u32[]{:S(2)}) copy-start(bf16[2,1024,512]{2,1,0:T(8,128)(2,1)S(1)} %collective-permute-done.40.up_ref) | copy-start | bytes 6291460
  482.9 91.9 %collective-permute-start.27 = (bf16[2,64,8192]{2,1,0:T(8,128)(2,1)}, bf16[2,64,8192]{2,1,0:T(8,128)(2,1)S(1)}, u32[]{:S(2)}, u32[]{:S(2)}) collective-permute-start(bf16[2,64,8192]{2,1,0:T(8,128)(2,1)} %get-tuple-element.28), channel_id=1, source_target_pairs={{0,3},{1,0},{2,1},{3,2},{4,7},{5,4},{6,5},{7,6},{8,11},{9,8},{10,9... | collective-permute-start | bytes 6291464 | tf_op jit(solution)/shard_map/ppermute | solution.py:119
  528.0 89.8 %collective-permute-start.7 = (bf16[2,64,8192]{2,1,0:T(8,128)(2,1)}, bf16[2,64,8192]{2,1,0:T(8,128)(2,1)S(1)}, u32[]{:S(2)}, u32[]{:S(2)}) collective-permute-start(bf16[2,64,8192]{2,1,0:T(8,128)(2,1)} %collective-permute-done.6.up_ref), channel_id=1, source_target_pairs={{0,1},{1,2},{2,3},{3,0},{4,5},{5,6},{6,7},{7,4},{8,9},{9,10},{10,1... | collective-permute-start | bytes 6291464 | tf_op jit(solution)/shard_map/ppermute | solution.py:119
  528.0 92.6 %collective-permute-start.10 = (bf16[2,64,8192]{2,1,0:T(8,128)(2,1)}, bf16[2,64,8192]{2,1,0:T(8,128)(2,1)S(1)}, u32[]{:S(2)}, u32[]{:S(2)}) collective-permute-start(bf16[2,64,8192]{2,1,0:T(8,128)(2,1)} %collective-permute-done.9.down_ref), channel_id=1, source_target_pairs={{0,3},{1,0},{2,1},{3,2},{4,7},{5,4},{6,5},{7,6},{8,11},{9,8},{10,9... | collective-permute-start | bytes 6291464 | tf_op jit(solution)/shard_map/ppermute | solution.py:119
  531.2 131.6 %collective-permute-start.41 = (bf16[2,1024,512]{2,1,0:T(8,128)(2,1)S(1)}, bf16[2,1024,512]{2,1,0:T(8,128)(2,1)}, u32[]{:S(2)}, u32[]{:S(2)}) collective-permute-start(bf16[2,1024,512]{2,1,0:T(8,128)(2,1)S(1)} %collective-permute-done.40.up_ref), channel_id=1, source_target_pairs={{0,1},{1,2},{2,3},{3,0},{4,5},{5,6},{6,7},{7,4},{8,9},{9,10},{10,1... | collective-permute-start | bytes 6291464 | tf_op jit(solution)/shard_map/ppermute | solution.py:119
  572.8 270.3 %copy-start.3 = (bf16[2,64,8192]{2,1,0:T(8,128)(2,1)}, bf16[2,64,8192]{2,1,0:T(8,128)(2,1)S(1)}, u32[]{:S(2)}) copy-start(bf16[2,64,8192]{2,1,0:T(8,128)(2,1)S(1)} %collective-permute-done.24.up_ref) | copy-start | bytes 6291460
  572.8 92.0 %collective-permute-start.44 = (bf16[2,1024,512]{2,1,0:T(8,128)(2,1)}, bf16[2,1024,512]{2,1,0:T(8,128)(2,1)}, u32[]{:S(2)}, u32[]{:S(2)}) collective-permute-start(bf16[2,1024,512]{2,1,0:T(8,128)(2,1)} %collective-permute-done.43.down_ref), channel_id=1, source_target_pairs={{0,3},{1,0},{2,1},{3,2},{4,7},{5,4},{6,5},{7,6},{8,11},{9,8},{10,9... | collective-permute-start | bytes 6291464 | tf_op jit(solution)/shard_map/ppermute | solution.py:119
  574.9 268.3 %copy-start.4 = (bf16[2,64,8192]{2,1,0:T(8,128)(2,1)}, bf16[2,64,8192]{2,1,0:T(8,128)(2,1)S(1)}, u32[]{:S(2)}) copy-start(bf16[2,64,8192]{2,1,0:T(8,128)(2,1)S(1)} %collective-permute-done.27.down_ref) | copy-start | bytes 6291460
  574.9 132.9 %collective-permute-start.25 = (bf16[2,64,8192]{2,1,0:T(8,128)(2,1)S(1)}, bf16[2,64,8192]{2,1,0:T(8,128)(2,1)}, u32[]{:S(2)}, u32[]{:S(2)}) collective-permute-start(bf16[2,64,8192]{2,1,0:T(8,128)(2,1)S(1)} %collective-permute-done.24.up_ref), channel_id=1, source_target_pairs={{0,1},{1,2},{2,3},{3,0},{4,5},{5,6},{6,7},{7,4},{8,9},{9,10},{10,1... | collective-permute-start | bytes 6291464 | tf_op jit(solution)/shard_map/ppermute | solution.py:119
  617.8 47.1 %copy-start = (bf16[2,64,8192]{2,1,0:T(8,128)(2,1)}, bf16[2,64,8192]{2,1,0:T(8,128)(2,1)S(1)}, u32[]{:S(2)}) copy-start(bf16[2,64,8192]{2,1,0:T(8,128)(2,1)S(1)} %collective-permute-done.7.up_ref) | copy-start | bytes 6291460
  617.8 90.0 %collective-permute-start.28 = (bf16[2,64,8192]{2,1,0:T(8,128)(2,1)S(1)}, bf16[2,64,8192]{2,1,0:T(8,128)(2,1)}, u32[]{:S(2)}, u32[]{:S(2)}) collective-permute-start(bf16[2,64,8192]{2,1,0:T(8,128)(2,1)S(1)} %collective-permute-done.27.down_ref), channel_id=1, source_target_pairs={{0,3},{1,0},{2,1},{3,2},{4,7},{5,4},{6,5},{7,6},{8,11},{9,8},{10,9... | collective-permute-start | bytes 6291464 | tf_op jit(solution)/shard_map/ppermute | solution.py:119
  620.6 120.2 %copy-start.1 = (bf16[2,64,8192]{2,1,0:T(8,128)(2,1)}, bf16[2,64,8192]{2,1,0:T(8,128)(2,1)S(1)}, u32[]{:S(2)}) copy-start(bf16[2,64,8192]{2,1,0:T(8,128)(2,1)S(1)} %collective-permute-done.10.down_ref) | copy-start | bytes 6291460
  620.6 116.1 %collective-permute-start.14 = (bf16[1,32,8192]{2,1,0:T(8,128)(2,1)S(1)}, bf16[1,32,8192]{2,1,0:T(8,128)(2,1)S(1)}, u32[]{:S(2)}, u32[]{:S(2)}) collective-permute-start(bf16[1,32,8192]{2,1,0:T(8,128)(2,1)S(1)} %slice.36), channel_id=1, source_target_pairs={{0,1},{1,2},{2,3},{3,0},{4,5},{5,6},{6,7},{7,4},{8,9},{9,10},{10,1... | collective-permute-start | bytes 1572872 | tf_op jit(solution)/shard_map/ppermute | solution.py:119
  662.8 73.9 %collective-permute-start.15 = (bf16[1,32,8192]{2,1,0:T(8,128)(2,1)S(1)}, bf16[1,32,8192]{2,1,0:T(8,128)(2,1)S(1)}, u32[]{:S(2)}, u32[]{:S(2)}) collective-permute-start(bf16[1,32,8192]{2,1,0:T(8,128)(2,1)S(1)} %slice.37), channel_id=1, source_target_pairs={{0,3},{1,0},{2,1},{3,2},{4,7},{5,4},{6,5},{7,6},{8,11},{9,8},{10,9... | collective-permute-start | bytes 1572872 | tf_op jit(solution)/shard_map/ppermute | solution.py:119
  664.8 59.7 %collective-permute-start.12 = (bf16[1,16,8192]{2,1,0:T(8,128)(2,1)S(1)}, bf16[1,16,8192]{2,1,0:T(8,128)(2,1)S(1)}, u32[]{:S(2)}, u32[]{:S(2)}) collective-permute-start(bf16[1,16,8192]{2,1,0:T(8,128)(2,1)S(1)} %get-tuple-element.63), channel_id=1, source_target_pairs={{0,1},{1,2},{2,3},{3,0},{4,5},{5,6},{6,7},{7,4},{8,9},{9,10},{10,1... | collective-permute-start | bytes 786440 | tf_op jit(solution)/shard_map/ppermute | solution.py:119
  707.8 39.2 %collective-permute-start.16 = (bf16[1,64,8192]{2,1,0:T(8,128)(2,1)S(1)}, bf16[1,64,8192]{2,1,0:T(8,128)(2,1)S(1)}, u32[]{:S(2)}, u32[]{:S(2)}) collective-permute-start(bf16[1,64,8192]{2,1,0:T(8,128)(2,1)S(1)} %slice.38), channel_id=1, source_target_pairs={{0,1},{1,2},{2,3},{3,0},{4,5},{5,6},{6,7},{7,4},{8,9},{9,10},{10,1... | collective-permute-start | bytes 3145736 | tf_op jit(solution)/shard_map/ppermute | solution.py:119
  707.8 18.8 %collective-permute-start.13 = (bf16[1,16,8192]{2,1,0:T(8,128)(2,1)S(1)}, bf16[1,16,8192]{2,1,0:T(8,128)(2,1)S(1)}, u32[]{:S(2)}, u32[]{:S(2)}) collective-permute-start(bf16[1,16,8192]{2,1,0:T(8,128)(2,1)S(1)} %get-tuple-element.61), channel_id=1, source_target_pairs={{0,3},{1,0},{2,1},{3,2},{4,7},{5,4},{6,5},{7,6},{8,11},{9,8},{10,9... | collective-permute-start | bytes 786440 | tf_op jit(solution)/shard_map/ppermute | solution.py:119
  724.5 122.9 %copy-start.11 = (bf16[1,16,8192]{2,1,0:T(8,128)(2,1)}, bf16[1,16,8192]{2,1,0:T(8,128)(2,1)S(1)}, u32[]{:S(2)}) copy-start(bf16[1,16,8192]{2,1,0:T(8,128)(2,1)S(1)} %collective-permute-done.12.up_ref) | copy-start | bytes 786436
  724.5 9.2 %collective-permute-start.11 = (bf16[1,16,8192]{2,1,0:T(8,128)(2,1)S(1)}, bf16[1,16,8192]{2,1,0:T(8,128)(2,1)S(1)}, u32[]{:S(2)}, u32[]{:S(2)}) collective-permute-start(bf16[1,16,8192]{2,1,0:T(8,128)(2,1)S(1)} %get-tuple-element.62), channel_id=1, source_target_pairs={{0,3},{1,0},{2,1},{3,2},{4,7},{5,4},{6,5},{7,6},{8,11},{9,8},{10,9... | collective-permute-start | bytes 786440 | tf_op jit(solution)/shard_map/ppermute | solution.py:119
  726.5 116.6 %copy-start.12 = (bf16[1,16,8192]{2,1,0:T(8,128)(2,1)}, bf16[1,16,8192]{2,1,0:T(8,128)(2,1)S(1)}, u32[]{:S(2)}) copy-start(bf16[1,16,8192]{2,1,0:T(8,128)(2,1)S(1)} %collective-permute-done.13.down_ref) | copy-start | bytes 786436
  726.5 144.7 %collective-permute-start.42 = (bf16[2,1024,512]{2,1,0:T(8,128)(2,1)}, bf16[2,1024,512]{2,1,0:T(8,128)(2,1)}, u32[]{:S(2)}, u32[]{:S(2)}) collective-permute-start(bf16[2,1024,512]{2,1,0:T(8,128)(2,1)} %collective-permute-done.41.up_ref), channel_id=1, source_target_pairs={{0,1},{1,2},{2,3},{3,0},{4,5},{5,6},{6,7},{7,4},{8,9},{9,10},{10,1... | collective-permute-start | bytes 6291464 | tf_op jit(solution)/shard_map/ppermute | solution.py:119
  733.7 137.6 %collective-permute-start.45 = (bf16[2,1024,512]{2,1,0:T(8,128)(2,1)}, bf16[2,1024,512]{2,1,0:T(8,128)(2,1)}, u32[]{:S(2)}, u32[]{:S(2)}) collective-permute-start(bf16[2,1024,512]{2,1,0:T(8,128)(2,1)} %collective-permute-done.44.down_ref), channel_id=1, source_target_pairs={{0,3},{1,0},{2,1},{3,2},{4,7},{5,4},{6,5},{7,6},{8,11},{9,8},{10,9... | collective-permute-start | bytes 6291464 | tf_op jit(solution)/shard_map/ppermute | solution.py:119
  736.7 110.7 %copy-start.9 = (bf16[1,32,8192]{2,1,0:T(8,128)(2,1)}, bf16[1,32,8192]{2,1,0:T(8,128)(2,1)S(1)}, u32[]{:S(2)}) copy-start(bf16[1,32,8192]{2,1,0:T(8,128)(2,1)S(1)} %collective-permute-done.14.up_ref) | copy-start | bytes 1572868
  736.7 137.9 %collective-permute-start.26 = (bf16[2,64,8192]{2,1,0:T(8,128)(2,1)}, bf16[2,64,8192]{2,1,0:T(8,128)(2,1)}, u32[]{:S(2)}, u32[]{:S(2)}) collective-permute-start(bf16[2,64,8192]{2,1,0:T(8,128)(2,1)} %collective-permute-done.25.up_ref), channel_id=1, source_target_pairs={{0,1},{1,2},{2,3},{3,0},{4,5},{5,6},{6,7},{7,4},{8,9},{9,10},{10,1... | collective-permute-start | bytes 6291464 | tf_op jit(solution)/shard_map/ppermute | solution.py:119
  736.7 0.8 copy-start.10
  737.5 137.1 %collective-permute-start.29 = (bf16[2,64,8192]{2,1,0:T(8,128)(2,1)}, bf16[2,64,8192]{2,1,0:T(8,128)(2,1)}, u32[]{:S(2)}, u32[]{:S(2)}) collective-permute-start(bf16[2,64,8192]{2,1,0:T(8,128)(2,1)} %collective-permute-done.28.down_ref), channel_id=1, source_target_pairs={{0,3},{1,0},{2,1},{3,2},{4,7},{5,4},{6,5},{7,6},{8,11},{9,8},{10,9... | collective-permute-start | bytes 6291464 | tf_op jit(solution)/shard_map/ppermute | solution.py:119
  747.0 96.3 %copy-start.7 = (bf16[1,64,8192]{2,1,0:T(8,128)(2,1)}, bf16[1,64,8192]{2,1,0:T(8,128)(2,1)S(1)}, u32[]{:S(2)}) copy-start(bf16[1,64,8192]{2,1,0:T(8,128)(2,1)S(1)} %collective-permute-done.16.up_ref) | copy-start | bytes 3145732
  747.0 96.1 %collective-permute-start.17 = (bf16[1,64,8192]{2,1,0:T(8,128)(2,1)S(1)}, bf16[1,64,8192]{2,1,0:T(8,128)(2,1)S(1)}, u32[]{:S(2)}, u32[]{:S(2)}) collective-permute-start(bf16[1,64,8192]{2,1,0:T(8,128)(2,1)S(1)} %slice.39), channel_id=1, source_target_pairs={{0,3},{1,0},{2,1},{3,2},{4,7},{5,4},{6,5},{7,6},{8,11},{9,8},{10,9... | collective-permute-start | bytes 3145736 | tf_op jit(solution)/shard_map/ppermute | solution.py:119
  843.1 1.0 copy-start.8
  843.1 27.3 %collective-permute-start.8 = (bf16[1,16,8192]{2,1,0:T(8,128)(2,1)}, bf16[1,16,8192]{2,1,0:T(8,128)(2,1)S(1)}, u32[]{:S(2)}, u32[]{:S(2)}) collective-permute-start(bf16[1,16,8192]{2,1,0:T(8,128)(2,1)} %get-tuple-element.64), channel_id=1, source_target_pairs={{0,1},{1,2},{2,3},{3,0},{4,5},{5,6},{6,7},{7,4},{8,9},{9,10},{10,1... | collective-permute-start | bytes 786440 | tf_op jit(solution)/shard_map/ppermute | solution.py:119
  (1 other events, 0.7 us)
where the time goes:
time: 878 us
  waiting for transfers between devices  667 us (76%)
  Pallas kernels  95.2 us (11%)
  starting transfers between devices  60 us (7%)
  other arithmetic  34.5 us (4%)
  local copies, waits for them, and re-layouts  19.9 us (2%)
    ppermute x46, waiting for transfers between devices, send(): moved.append(lax.ppermute(p, 'dp', way))  667 us
    pallas_call x3, Pallas kernels, update(): pl.pallas_call(kernel, out_shape=(jax.ShapeDtypeStruct(w.shape, jnp.bfloa...  61.6 us
    ppermute x46, starting transfers between devices, send(): moved.append(lax.ppermute(p, 'dp', way))  60 us
    convert_element_type x6, other arithmetic, add(): return (a.astype(jnp.float32) + b.astype(jnp.float32)).astype(jnp.bfloat16)  34.5 us
    pallas_call x12, Pallas kernels, place(): pl.pallas_call(kernel, out_shape=jax.ShapeDtypeStruct(whole.shape, whole....  33.7 us
  transfers between devices with their start and end apart: 46, of which 19 were waited for; matrix products, arithmetic and copies ran while one was open for 5% of the time, Pallas kernels for 10%

commit v1 on v0

--- a/solution.py
+++ b/solution.py
@@ -96,6 +96,35 @@
     )(*pieces, whole)
 
 
+def first_slice(axis, hops, term, half, rows):
+    columns = term.shape[3]
+    count = term.shape[2] // (2 * half)
+
+    def kernel(term_ref, up_ref, down_ref, sems):
+        me = lax.axis_index(axis)
+        copies = []
+        for side, ref in enumerate((up_ref, down_ref)):
+            block = lax.rem(me + (hops, count - hops)[side], count)
+            start = pl.multiple_of((block * 2 + side) * half, half)
+            copies.append(pltpu.make_async_copy(term_ref.at[0, 0, pl.ds(start, rows)], ref.at[0], sems.at[side]))
+        for copy in copies:
+            copy.start()
+        for copy in copies:
+            copy.wait()
+
+    piece = jax.ShapeDtypeStruct((1, rows, columns), term.dtype)
+    return pl.pallas_call(
+        kernel,
+        out_shape=(piece, piece),
+        in_specs=[pl.BlockSpec(memory_space=pl.ANY)],
+        out_specs=(pl.BlockSpec(memory_space=pltpu.VMEM),) * 2,
+        scratch_shapes=[pltpu.SemaphoreType.DMA((2,))],
+        compiler_params=pltpu.CompilerParams(vmem_limit_bytes=52 << 20),
+        cost_estimate=pl.CostEstimate(flops=rows * columns, bytes_accessed=8 * rows * columns, transcendentals=0),
+        name="first_slice",
+    )(term)
+
+
 def solution(mesh):
     n = mesh.shape["dp"]
     ways = tuple(tuple((i, (i + to) % n) for i in range(n)) for to in (1, -1))
@@ -144,7 +173,9 @@
         new_w, new_m, new_v = [None] * 3, [None] * 3, [None] * 3
         for k in order:
             if k == order[0]:
-                sent = [send(own(terms[k], m[k], n - 1, part)) for part in small_first(m[k])]
+                half, parts = m[k].shape[1] // 2, small_first(m[k])
+                sent = [send(first_slice("dp", n - 1, terms[k], half, parts[0][3]))]
+                sent += [send(own(terms[k], m[k], n - 1, part)) for part in parts[1:]]
                 moving[k] = [join(parts) for parts in zip(*sent, strict=True)]
             else:
                 moving[k] = send(own(terms[k], m[k], n - 1, all_of_it(m[k])[0]))

time: 878 us -> 879 us (level)
  transfers between devices with their start and end apart: 46 -> 46, of which waited for: 19 -> 19; matrix products, arithmetic and copies ran while one was open for 5% -> 5% of each run, Pallas kernels for 10% -> 11%
where the time goes in v1:
time: 879 us; the launch traced here: 878 us
  waiting for transfers between devices  667 us (76%)
  Pallas kernels  96.3 us (11%)
  starting transfers between devices  60 us (7%)
  other arithmetic  34.3 us (4%)
  local copies, waits for them, and re-layouts  19.2 us (2%)
    ppermute x46, waiting for transfers between devices, send(): moved.append(lax.ppermute(p, 'dp', way))  667 us
    pallas_call x3, Pallas kernels, update(): pl.pallas_call(kernel, out_shape=(jax.ShapeDtypeStruct(w.shape, jnp.bfloa...  61.6 us
    ppermute x46, starting transfers between devices, send(): moved.append(lax.ppermute(p, 'dp', way))  60 us
    convert_element_type x6, other arithmetic, add(): return (a.astype(jnp.float32) + b.astype(jnp.float32)).astype(jnp.bfloat16)  34.3 us
    pallas_call x12, Pallas kernels, place(): pl.pallas_call(kernel, out_shape=jax.ShapeDtypeStruct(whole.shape, whole....  33.7 us
  transfers between devices with their start and end apart: 46, of which 19 were waited for; matrix products, arithmetic and copies ran while one was open for 5% of the time, Pallas kernels for 11%

profile of v1, /device:TPU:112, one launch (start us, length us, event | category | flops | bytes accessed | tf_op | source)
XLA Modules:
  0.0 878.3 jit_solution(664155267880742642)
XLA Ops:
  0.7 2.6 dynamic-slice_bitcast_fusion.6
  3.3 2.3 collective-permute-start.31
  5.6 4.7 dynamic-slice_bitcast_fusion.2
  15.1 2.8 collective-permute-start.35
  17.9 3.0 dynamic-slice_bitcast_fusion.4
  20.9 54.6 %collective-permute-done.30 = bf16[1,256,512]{2,1,0:T(8,128)(2,1)S(1)} collective-permute-done((bf16[1,256,512]{2,1,0:T(8,128)(2,1)S(1)}, bf16[1,256,512]{2,1,0:T(8,128)(2,1)S(1)}, u32[]{:S(2)}, u32[]{:S(2)}) %collective-permute-start.30) | collective-permute-done | bytes 262176 | tf_op jit(solution)/shard_map/ppermute | solution.py:148
  76.5 3.0 collective-permute-start.37
  80.0 4.1 dynamic-slice_bitcast_fusion
  84.2 34.1 %collective-permute-done.36 = bf16[1,768,512]{2,1,0:T(8,128)(2,1)S(1)} collective-permute-done((bf16[1,768,512]{2,1,0:T(8,128)(2,1)}, bf16[1,768,512]{2,1,0:T(8,128)(2,1)S(1)}, u32[]{:S(2)}, u32[]{:S(2)}) %collective-permute-start.36) | collective-permute-done | bytes 786464 | tf_op jit(solution)/shard_map/ppermute | solution.py:148
  119.0 3.0 collective-permute-start.21
  122.0 4.4 fusion.1
  126.4 3.2 collective-permute-start.38
  129.6 6.4 fusion.9
  136.1 32.5 %collective-permute-done.18 = bf16[2,64,8192]{2,1,0:T(8,128)(2,1)S(1)} collective-permute-done((bf16[2,64,8192]{2,1,0:T(8,128)(2,1)}, bf16[2,64,8192]{2,1,0:T(8,128)(2,1)S(1)}, u32[]{:S(2)}, u32[]{:S(2)}) %collective-permute-start.18) | collective-permute-done | bytes 2097184 | tf_op jit(solution)/shard_map/ppermute | solution.py:148
  168.6 2.0 collective-permute-start.4
  170.6 5.2 fusion.5
  175.8 37.8 %collective-permute-done.33 = bf16[2,1024,512]{2,1,0:T(8,128)(2,1)} collective-permute-done((bf16[2,1024,512]{2,1,0:T(8,128)(2,1)}, bf16[2,1024,512]{2,1,0:T(8,128)(2,1)}, u32[]{:S(2)}, u32[]{:S(2)}) %collective-permute-start.33) | collective-permute-done | bytes 2097184 | tf_op jit(solution)/shard_map/ppermute | solution.py:148
  213.6 2.0 collective-permute-start.22
  215.6 6.1 fusion
  221.7 36.9 %collective-permute-done.1 = bf16[2,64,8192]{2,1,0:T(8,128)(2,1)} collective-permute-done((bf16[2,64,8192]{2,1,0:T(8,128)(2,1)}, bf16[2,64,8192]{2,1,0:T(8,128)(2,1)}, u32[]{:S(2)}, u32[]{:S(2)}) %collective-permute-start.1) | collective-permute-done | bytes 2097184 | tf_op jit(solution)/shard_map/ppermute | solution.py:148
  258.5 2.0 collective-permute-start.39
  260.6 7.0 fusion.8
  267.6 35.8 %collective-permute-done.19 = bf16[2,64,8192]{2,1,0:T(8,128)(2,1)S(1)} collective-permute-done((bf16[2,64,8192]{2,1,0:T(8,128)(2,1)}, bf16[2,64,8192]{2,1,0:T(8,128)(2,1)S(1)}, u32[]{:S(2)}, u32[]{:S(2)}) %collective-permute-start.19) | collective-permute-done | bytes 2097184 | tf_op jit(solution)/shard_map/ppermute | solution.py:148
  303.4 2.0 collective-permute-start.5
  305.4 5.2 fusion.4
  310.6 37.7 %collective-permute-done.34.up_ref = bf16[2,1024,512]{2,1,0:T(8,128)(2,1)S(1)} collective-permute-done((bf16[2,1024,512]{2,1,0:T(8,128)(2,1)}, bf16[2,1024,512]{2,1,0:T(8,128)(2,1)S(1)}, u32[]{:S(2)}, u32[]{:S(2)}) %collective-permute-start.34) | collective-permute-done | bytes 2097184 | tf_op jit(solution)/shard_map/ppermute | solution.py:148
  348.3 2.0 collective-permute-start.23
  351.7 20.4 %update.5 = (bf16[2,8192,512]{2,1,0:T(8,128)(2,1)}, f32[2,2048,512]{2,1,0:T(8,128)}, f32[2,2048,512]{2,1,0:T(8,128)}, bf16[2,1024,512]{2,1,0:T(8,128)(2,1)}, bf16[2,1024,512]{2,1,0:T(8,128)(2,1)}) custom-call(s32[1]{0:T(128)} %bitcast.me_ref, bf16[2,1024,512]{2,1,0:T(8,128)(2,1)} %copy-done.5, bf16[2,1024,512]{2,1,0:T(8,128)(2,1)} %copy-done.6, ...), custom_call_target="tpu_custom_call" | custom-call | flops 41943040 | bytes 54525952 | tf_op jit(solution)/shard_map/update/pallas_call | solution.py:42
  372.1 21.2 %collective-permute-done.2.up_ref = bf16[2,64,8192]{2,1,0:T(8,128)(2,1)} collective-permute-done((bf16[2,64,8192]{2,1,0:T(8,128)(2,1)}, bf16[2,64,8192]{2,1,0:T(8,128)(2,1)}, u32[]{:S(2)}, u32[]{:S(2)}) %collective-permute-start.2) | collective-permute-done | bytes 2097184 | tf_op jit(solution)/shard_map/ppermute | solution.py:148
  393.4 20.7 %update.3 = (bf16[2,512,8192]{2,1,0:T(8,128)(2,1)}, f32[2,128,8192]{2,1,0:T(8,128)}, f32[2,128,8192]{2,1,0:T(8,128)}, bf16[2,64,8192]{2,1,0:T(8,128)(2,1)}, bf16[2,64,8192]{2,1,0:T(8,128)(2,1)}) custom-call(s32[1]{0:T(128)} %bitcast.me_ref, bf16[2,64,8192]{2,1,0:T(8,128)(2,1)} %collective-permute-done.2.up_ref, ...), custom_call_target="tpu_custom_call" | custom-call | flops 41943040 | bytes 54525952 | tf_op jit(solution)/shard_map/update/pallas_call | solution.py:42
  415.3 2.0 collective-permute-start.43
  417.3 21.0 %collective-permute-done.20.up_ref = bf16[2,64,8192]{2,1,0:T(8,128)(2,1)} collective-permute-done((bf16[2,64,8192]{2,1,0:T(8,128)(2,1)}, bf16[2,64,8192]{2,1,0:T(8,128)(2,1)}, u32[]{:S(2)}, u32[]{:S(2)}) %collective-permute-start.20) | collective-permute-done | bytes 2097184 | tf_op jit(solution)/shard_map/ppermute | solution.py:148
  438.3 2.0 collective-permute-start.9
  440.3 20.5 %update.4 = (bf16[2,512,8192]{2,1,0:T(8,128)(2,1)}, f32[2,128,8192]{2,1,0:T(8,128)}, f32[2,128,8192]{2,1,0:T(8,128)}, bf16[2,64,8192]{2,1,0:T(8,128)(2,1)}, bf16[2,64,8192]{2,1,0:T(8,128)(2,1)}) custom-call(s32[1]{0:T(128)} %bitcast.me_ref, bf16[2,64,8192]{2,1,0:T(8,128)(2,1)} %collective-permute-done.20.up_ref, ...), custom_call_target="tpu_custom_call" | custom-call | flops 41943040 | bytes 54525952 | tf_op jit(solution)/shard_map/update/pallas_call | solution.py:42
  460.8 22.3 %collective-permute-done.40.up_ref = bf16[2,1024,512]{2,1,0:T(8,128)(2,1)S(1)} collective-permute-done((bf16[2,1024,512]{2,1,0:T(8,128)(2,1)}, bf16[2,1024,512]{2,1,0:T(8,128)(2,1)S(1)}, u32[]{:S(2)}, u32[]{:S(2)}) %collective-permute-start.40) | collective-permute-done | bytes 2097184 | tf_op jit(solution)/shard_map/ppermute | solution.py:148
  483.2 2.0 collective-permute-start.27
  485.2 43.0 %collective-permute-done.6.up_ref = bf16[2,64,8192]{2,1,0:T(8,128)(2,1)} collective-permute-done((bf16[2,64,8192]{2,1,0:T(8,128)(2,1)}, bf16[2,64,8192]{2,1,0:T(8,128)(2,1)}, u32[]{:S(2)}, u32[]{:S(2)}) %collective-permute-start.6) | collective-permute-done | bytes 2097184 | tf_op jit(solution)/shard_map/ppermute | solution.py:148
  528.2 3.2 collective-permute-start.10
  531.4 41.6 %collective-permute-done.24.up_ref = bf16[2,64,8192]{2,1,0:T(8,128)(2,1)S(1)} collective-permute-done((bf16[2,64,8192]{2,1,0:T(8,128)(2,1)}, bf16[2,64,8192]{2,1,0:T(8,128)(2,1)S(1)}, u32[]{:S(2)}, u32[]{:S(2)}) %collective-permute-start.24) | collective-permute-done | bytes 2097184 | tf_op jit(solution)/shard_map/ppermute | solution.py:148
  573.0 2.0 collective-permute-start.44
  575.1 42.9 %collective-permute-done.7.up_ref = bf16[2,64,8192]{2,1,0:T(8,128)(2,1)S(1)} collective-permute-done((bf16[2,64,8192]{2,1,0:T(8,128)(2,1)}, bf16[2,64,8192]{2,1,0:T(8,128)(2,1)S(1)}, u32[]{:S(2)}, u32[]{:S(2)}) %collective-permute-start.7) | collective-permute-done | bytes 2097184 | tf_op jit(solution)/shard_map/ppermute | solution.py:148
  618.0 2.0 collective-permute-start.28
  620.9 42.1 %collective-permute-done.41.up_ref = bf16[2,1024,512]{2,1,0:T(8,128)(2,1)} collective-permute-done((bf16[2,1024,512]{2,1,0:T(8,128)(2,1)S(1)}, bf16[2,1024,512]{2,1,0:T(8,128)(2,1)}, u32[]{:S(2)}, u32[]{:S(2)}) %collective-permute-start.41) | collective-permute-done | bytes 2097184 | tf_op jit(solution)/shard_map/ppermute | solution.py:148
  663.0 2.0 collective-permute-start.15
  665.2 42.8 %collective-permute-done.25.up_ref = bf16[2,64,8192]{2,1,0:T(8,128)(2,1)} collective-permute-done((bf16[2,64,8192]{2,1,0:T(8,128)(2,1)S(1)}, bf16[2,64,8192]{2,1,0:T(8,128)(2,1)}, u32[]{:S(2)}, u32[]{:S(2)}) %collective-permute-start.25) | collective-permute-done | bytes 2097184 | tf_op jit(solution)/shard_map/ppermute | solution.py:148
  708.0 3.2 collective-permute-start.13
  711.2 13.5 %collective-permute-done.12.up_ref = bf16[1,16,8192]{2,1,0:T(8,128)(2,1)S(1)} collective-permute-done((bf16[1,16,8192]{2,1,0:T(8,128)(2,1)S(1)}, bf16[1,16,8192]{2,1,0:T(8,128)(2,1)S(1)}, u32[]{:S(2)}, u32[]{:S(2)}) %collective-permute-start.12) | collective-permute-done | bytes 262176 | tf_op jit(solution)/shard_map/ppermute | solution.py:148
  724.7 2.0 collective-permute-start.11
  726.7 7.1 collective-permute-done.11.down_ref
  733.9 3.0 collective-permute-start.45
  737.8 3.2 collective-permute-start.29
  741.0 6.2 collective-permute-done.16.up_ref
  747.2 2.0 collective-permute-start.17
  749.2 94.1 %collective-permute-done.17.down_ref = bf16[1,64,8192]{2,1,0:T(8,128)(2,1)S(1)} collective-permute-done((bf16[1,64,8192]{2,1,0:T(8,128)(2,1)S(1)}, bf16[1,64,8192]{2,1,0:T(8,128)(2,1)S(1)}, u32[]{:S(2)}, u32[]{:S(2)}) %collective-permute-start.17) | collective-permute-done | bytes 1048608 | tf_op jit(solution)/shard_map/ppermute | solution.py:148
  844.3 3.3 place.21.whole_ref
  847.6 3.3 place.18.whole_ref
  850.9 3.3 place.12.whole_ref
  854.3 3.3 place.22.whole_ref
  857.6 3.3 place.13.whole_ref
  860.9 2.6 place.14.whole_ref
  863.5 2.0 place.15.whole_ref
  865.5 3.3 place.19.whole_ref
  871.5 3.3 place.23
  874.8 3.3 place.20
  (99 shorter events, 15.1 us)
Async XLA Ops:
  3.3 76.2 %collective-permute-start.31 = (bf16[1,768,512]{2,1,0:T(8,128)(2,1)}, bf16[1,768,512]{2,1,0:T(8,128)(2,1)}, u32[]{:S(2)}, u32[]{:S(2)}) collective-permute-start(bf16[1,768,512]{2,1,0:T(8,128)(2,1)} %get-tuple-element.48), channel_id=1, source_target_pairs={{0,1},{1,2},{2,3},{3,0},{4,5},{5,6},{6,7},{7,4},{8,9},{9,10},{10,1... | collective-permute-start | bytes 2359304 | tf_op jit(solution)/shard_map/ppermute | solution.py:148
  10.3 116.1 %collective-permute-start = (bf16[2,64,8192]{2,1,0:T(8,128)(2,1)}, bf16[2,64,8192]{2,1,0:T(8,128)(2,1)S(1)}, u32[]{:S(2)}, u32[]{:S(2)}) collective-permute-start(bf16[2,64,8192]{2,1,0:T(8,128)(2,1)} %get-tuple-element.62), channel_id=1, source_target_pairs={{0,1},{1,2},{2,3},{3,0},{4,5},{5,6},{6,7},{7,4},{8,9},{9,10},{10,1... | collective-permute-start | bytes 6291464 | tf_op jit(solution)/shard_map/ppermute | solution.py:148
  11.9 117.7 %collective-permute-start.3 = (bf16[2,64,8192]{2,1,0:T(8,128)(2,1)}, bf16[2,64,8192]{2,1,0:T(8,128)(2,1)}, u32[]{:S(2)}, u32[]{:S(2)}) collective-permute-start(bf16[2,64,8192]{2,1,0:T(8,128)(2,1)} %get-tuple-element.61), channel_id=1, source_target_pairs={{0,3},{1,0},{2,1},{3,2},{4,7},{5,4},{6,5},{7,6},{8,11},{9,8},{10,9... | collective-permute-start | bytes 6291464 | tf_op jit(solution)/shard_map/ppermute | solution.py:148
  14.6 61.0 %collective-permute-start.30 = (bf16[1,256,512]{2,1,0:T(8,128)(2,1)S(1)}, bf16[1,256,512]{2,1,0:T(8,128)(2,1)S(1)}, u32[]{:S(2)}, u32[]{:S(2)}) collective-permute-start(bf16[1,256,512]{2,1,0:T(8,128)(2,1)S(1)} %get-tuple-element.32), channel_id=1, source_target_pairs={{0,1},{1,2},{2,3},{3,0},{4,5},{5,6},{6,7},{7,4},{8,9},{9,10},{10,1... | collective-permute-start | bytes 786440 | tf_op jit(solution)/shard_map/ppermute | solution.py:148
  15.1 61.4 %collective-permute-start.35 = (bf16[1,256,512]{2,1,0:T(8,128)(2,1)S(1)}, bf16[1,256,512]{2,1,0:T(8,128)(2,1)}, u32[]{:S(2)}, u32[]{:S(2)}) collective-permute-start(bf16[1,256,512]{2,1,0:T(8,128)(2,1)S(1)} %get-tuple-element.33), channel_id=1, source_target_pairs={{0,3},{1,0},{2,1},{3,2},{4,7},{5,4},{6,5},{7,6},{8,11},{9,8},{10,9... | collective-permute-start | bytes 786440 | tf_op jit(solution)/shard_map/ppermute | solution.py:148
  76.2 42.7 %collective-permute-start.32 = (bf16[1,1024,512]{2,1,0:T(8,128)(2,1)}, bf16[1,1024,512]{2,1,0:T(8,128)(2,1)S(1)}, u32[]{:S(2)}, u32[]{:S(2)}) collective-permute-start(bf16[1,1024,512]{2,1,0:T(8,128)(2,1)} %get-tuple-element.50), channel_id=1, source_target_pairs={{0,1},{1,2},{2,3},{3,0},{4,5},{5,6},{6,7},{7,4},{8,9},{9,10},{10,1... | collective-permute-start | bytes 3145736 | tf_op jit(solution)/shard_map/ppermute | solution.py:148
  76.5 45.5 %collective-permute-start.37 = (bf16[1,1024,512]{2,1,0:T(8,128)(2,1)}, bf16[1,1024,512]{2,1,0:T(8,128)(2,1)}, u32[]{:S(2)}, u32[]{:S(2)}) collective-permute-start(bf16[1,1024,512]{2,1,0:T(8,128)(2,1)} %get-tuple-element.49), channel_id=1, source_target_pairs={{0,3},{1,0},{2,1},{3,2},{4,7},{5,4},{6,5},{7,6},{8,11},{9,8},{10,9... | collective-permute-start | bytes 3145736 | tf_op jit(solution)/shard_map/ppermute | solution.py:148
  79.5 42.5 %copy-start.14 = (bf16[1,256,512]{2,1,0:T(8,128)(2,1)S(1)}, bf16[1,256,512]{2,1,0:T(8,128)(2,1)}, u32[]{:S(2)}) copy-start(bf16[1,256,512]{2,1,0:T(8,128)(2,1)} %copy-done.13) | copy-start | bytes 786436
  79.5 38.8 %collective-permute-start.36 = (bf16[1,768,512]{2,1,0:T(8,128)(2,1)}, bf16[1,768,512]{2,1,0:T(8,128)(2,1)S(1)}, u32[]{:S(2)}, u32[]{:S(2)}) collective-permute-start(bf16[1,768,512]{2,1,0:T(8,128)(2,1)} %get-tuple-element.47), channel_id=1, source_target_pairs={{0,3},{1,0},{2,1},{3,2},{4,7},{5,4},{6,5},{7,6},{8,11},{9,8},{10,9... | collective-permute-start | bytes 2359304 | tf_op jit(solution)/shard_map/ppermute | solution.py:148
  80.0 90.6 %slice-start = ((s8[16777216]{0:T(1024)(128)(4,1)}), s8[4194304]{0:T(1024)(128)(4,1)S(1)}, s32[]{:S(2)}) async-start(s8[16777216]{0:T(1024)(128)(4,1)} %bitcast.53), calls=%async_computation | async-start | bytes 8388608
  118.3 52.3 %slice-start.1 = ((s8[16777216]{0:T(1024)(128)(4,1)}), s8[4194304]{0:T(1024)(128)(4,1)S(1)}, s32[]{:S(2)}) async-start(s8[16777216]{0:T(1024)(128)(4,1)} %bitcast.53), calls=%async_computation.1 | async-start | bytes 8388608
  118.3 50.3 %collective-permute-start.18 = (bf16[2,64,8192]{2,1,0:T(8,128)(2,1)}, bf16[2,64,8192]{2,1,0:T(8,128)(2,1)S(1)}, u32[]{:S(2)}, u32[]{:S(2)}) collective-permute-start(bf16[2,64,8192]{2,1,0:T(8,128)(2,1)} %get-tuple-element.56), channel_id=1, source_target_pairs={{0,1},{1,2},{2,3},{3,0},{4,5},{5,6},{6,7},{7,4},{8,9},{9,10},{10,1... | collective-permute-start | bytes 6291464 | tf_op jit(solution)/shard_map/ppermute | solution.py:148
  119.0 51.6 %slice-start.2 = ((s8[16777216]{0:T(1024)(128)(4,1)}), s8[4194304]{0:T(1024)(128)(4,1)S(1)}, s32[]{:S(2)}) async-start(s8[16777216]{0:T(1024)(128)(4,1)} %bitcast.53), calls=%async_computation.2 | async-start | bytes 8388608
  119.0 51.6 %collective-permute-start.21 = (bf16[2,64,8192]{2,1,0:T(8,128)(2,1)S(1)}, bf16[2,64,8192]{2,1,0:T(8,128)(2,1)}, u32[]{:S(2)}, u32[]{:S(2)}) collective-permute-start(bf16[2,64,8192]{2,1,0:T(8,128)(2,1)S(1)} %get-tuple-element.55), channel_id=1, source_target_pairs={{0,3},{1,0},{2,1},{3,2},{4,7},{5,4},{6,5},{7,6},{8,11},{9,8},{10,9... | collective-permute-start | bytes 6291464 | tf_op jit(solution)/shard_map/ppermute | solution.py:148
  126.4 87.2 %collective-permute-start.33 = (bf16[2,1024,512]{2,1,0:T(8,128)(2,1)}, bf16[2,1024,512]{2,1,0:T(8,128)(2,1)}, u32[]{:S(2)}, u32[]{:S(2)}) collective-permute-start(bf16[2,1024,512]{2,1,0:T(8,128)(2,1)} %get-tuple-element.46), channel_id=1, source_target_pairs={{0,1},{1,2},{2,3},{3,0},{4,5},{5,6},{6,7},{7,4},{8,9},{9,10},{10,1... | collective-permute-start | bytes 6291464 | tf_op jit(solution)/shard_map/ppermute | solution.py:148
  126.4 44.2 %slice-start.3 = ((s8[16777216]{0:T(1024)(128)(4,1)}), s8[4194304]{0:T(1024)(128)(4,1)S(1)}, s32[]{:S(2)}) async-start(s8[16777216]{0:T(1024)(128)(4,1)} %bitcast.53), calls=%async_computation.3 | async-start | bytes 8388608
  126.4 89.2 %collective-permute-start.38 = (bf16[2,1024,512]{2,1,0:T(8,128)(2,1)S(1)}, bf16[2,1024,512]{2,1,0:T(8,128)(2,1)}, u32[]{:S(2)}, u32[]{:S(2)}) collective-permute-start(bf16[2,1024,512]{2,1,0:T(8,128)(2,1)S(1)} %get-tuple-element.45), channel_id=1, source_target_pairs={{0,3},{1,0},{2,1},{3,2},{4,7},{5,4},{6,5},{7,6},{8,11},{9,8},{10,9... | collective-permute-start | bytes 6291464 | tf_op jit(solution)/shard_map/ppermute | solution.py:148
  136.1 122.5 %collective-permute-start.1 = (bf16[2,64,8192]{2,1,0:T(8,128)(2,1)}, bf16[2,64,8192]{2,1,0:T(8,128)(2,1)}, u32[]{:S(2)}, u32[]{:S(2)}) collective-permute-start(bf16[2,64,8192]{2,1,0:T(8,128)(2,1)} %get-tuple-element.60), channel_id=1, source_target_pairs={{0,1},{1,2},{2,3},{3,0},{4,5},{5,6},{6,7},{7,4},{8,9},{9,10},{10,1... | collective-permute-start | bytes 6291464 | tf_op jit(solution)/shard_map/ppermute | solution.py:148
  168.6 92.0 %collective-permute-start.4 = (bf16[2,64,8192]{2,1,0:T(8,128)(2,1)}, bf16[2,64,8192]{2,1,0:T(8,128)(2,1)}, u32[]{:S(2)}, u32[]{:S(2)}) collective-permute-start(bf16[2,64,8192]{2,1,0:T(8,128)(2,1)} %get-tuple-element.59), channel_id=1, source_target_pairs={{0,3},{1,0},{2,1},{3,2},{4,7},{5,4},{6,5},{7,6},{8,11},{9,8},{10,9... | collective-permute-start | bytes 6291464 | tf_op jit(solution)/shard_map/ppermute | solution.py:148
  175.8 127.6 %collective-permute-start.19 = (bf16[2,64,8192]{2,1,0:T(8,128)(2,1)}, bf16[2,64,8192]{2,1,0:T(8,128)(2,1)S(1)}, u32[]{:S(2)}, u32[]{:S(2)}) collective-permute-start(bf16[2,64,8192]{2,1,0:T(8,128)(2,1)} %get-tuple-element.54), channel_id=1, source_target_pairs={{0,1},{1,2},{2,3},{3,0},{4,5},{5,6},{6,7},{7,4},{8,9},{9,10},{10,1... | collective-permute-start | bytes 6291464 | tf_op jit(solution)/shard_map/ppermute | solution.py:148
  213.6 91.8 %collective-permute-start.22 = (bf16[2,64,8192]{2,1,0:T(8,128)(2,1)}, bf16[2,64,8192]{2,1,0:T(8,128)(2,1)}, u32[]{:S(2)}, u32[]{:S(2)}) collective-permute-start(bf16[2,64,8192]{2,1,0:T(8,128)(2,1)} %get-tuple-element.53), channel_id=1, source_target_pairs={{0,3},{1,0},{2,1},{3,2},{4,7},{5,4},{6,5},{7,6},{8,11},{9,8},{10,9... | collective-permute-start | bytes 6291464 | tf_op jit(solution)/shard_map/ppermute | solution.py:148
  221.7 126.6 %collective-permute-start.34 = (bf16[2,1024,512]{2,1,0:T(8,128)(2,1)}, bf16[2,1024,512]{2,1,0:T(8,128)(2,1)S(1)}, u32[]{:S(2)}, u32[]{:S(2)}) collective-permute-start(bf16[2,1024,512]{2,1,0:T(8,128)(2,1)} %get-tuple-element.44), channel_id=1, source_target_pairs={{0,1},{1,2},{2,3},{3,0},{4,5},{5,6},{6,7},{7,4},{8,9},{9,10},{10,1... | collective-permute-start | bytes 6291464 | tf_op jit(solution)/shard_map/ppermute | solution.py:148
  258.5 91.8 %collective-permute-start.39 = (bf16[2,1024,512]{2,1,0:T(8,128)(2,1)S(1)}, bf16[2,1024,512]{2,1,0:T(8,128)(2,1)S(1)}, u32[]{:S(2)}, u32[]{:S(2)}) collective-permute-start(bf16[2,1024,512]{2,1,0:T(8,128)(2,1)S(1)} %get-tuple-element.43), channel_id=1, source_target_pairs={{0,3},{1,0},{2,1},{3,2},{4,7},{5,4},{6,5},{7,6},{8,11},{9,8},{10,9... | collective-permute-start | bytes 6291464 | tf_op jit(solution)/shard_map/ppermute | solution.py:148
  267.6 125.8 %collective-permute-start.2 = (bf16[2,64,8192]{2,1,0:T(8,128)(2,1)}, bf16[2,64,8192]{2,1,0:T(8,128)(2,1)}, u32[]{:S(2)}, u32[]{:S(2)}) collective-permute-start(bf16[2,64,8192]{2,1,0:T(8,128)(2,1)} %get-tuple-element.58), channel_id=1, source_target_pairs={{0,1},{1,2},{2,3},{3,0},{4,5},{5,6},{6,7},{7,4},{8,9},{9,10},{10,1... | collective-permute-start | bytes 6291464 | tf_op jit(solution)/shard_map/ppermute | solution.py:148
  303.4 90.0 %collective-permute-start.5 = (bf16[2,64,8192]{2,1,0:T(8,128)(2,1)}, bf16[2,64,8192]{2,1,0:T(8,128)(2,1)}, u32[]{:S(2)}, u32[]{:S(2)}) collective-permute-start(bf16[2,64,8192]{2,1,0:T(8,128)(2,1)} %get-tuple-element.57), channel_id=1, source_target_pairs={{0,3},{1,0},{2,1},{3,2},{4,7},{5,4},{6,5},{7,6},{8,11},{9,8},{10,9... | collective-permute-start | bytes 6291464 | tf_op jit(solution)/shard_map/ppermute | solution.py:148
  310.6 127.7 %collective-permute-start.20 = (bf16[2,64,8192]{2,1,0:T(8,128)(2,1)}, bf16[2,64,8192]{2,1,0:T(8,128)(2,1)}, u32[]{:S(2)}, u32[]{:S(2)}) collective-permute-start(bf16[2,64,8192]{2,1,0:T(8,128)(2,1)} %get-tuple-element.52), channel_id=1, source_target_pairs={{0,1},{1,2},{2,3},{3,0},{4,5},{5,6},{6,7},{7,4},{8,9},{9,10},{10,1... | collective-permute-start | bytes 6291464 | tf_op jit(solution)/shard_map/ppermute | solution.py:148
  348.3 3.4 copy-start.5
  348.3 92.0 %collective-permute-start.23 = (bf16[2,64,8192]{2,1,0:T(8,128)(2,1)}, bf16[2,64,8192]{2,1,0:T(8,128)(2,1)}, u32[]{:S(2)}, u32[]{:S(2)}) collective-permute-start(bf16[2,64,8192]{2,1,0:T(8,128)(2,1)} %get-tuple-element.51), channel_id=1, source_target_pairs={{0,3},{1,0},{2,1},{3,2},{4,7},{5,4},{6,5},{7,6},{8,11},{9,8},{10,9... | collective-permute-start | bytes 6291464 | tf_op jit(solution)/shard_map/ppermute | solution.py:148
  350.4 1.3 copy-start.6
  372.1 111.0 %collective-permute-start.40 = (bf16[2,1024,512]{2,1,0:T(8,128)(2,1)}, bf16[2,1024,512]{2,1,0:T(8,128)(2,1)S(1)}, u32[]{:S(2)}, u32[]{:S(2)}) collective-permute-start(bf16[2,1024,512]{2,1,0:T(8,128)(2,1)} %get-tuple-element.34), channel_id=1, source_target_pairs={{0,1},{1,2},{2,3},{3,0},{4,5},{5,6},{6,7},{7,4},{8,9},{9,10},{10,1... | collective-permute-start | bytes 6291464 | tf_op jit(solution)/shard_map/ppermute | solution.py:148
  414.1 114.1 %collective-permute-start.6 = (bf16[2,64,8192]{2,1,0:T(8,128)(2,1)}, bf16[2,64,8192]{2,1,0:T(8,128)(2,1)}, u32[]{:S(2)}, u32[]{:S(2)}) collective-permute-start(bf16[2,64,8192]{2,1,0:T(8,128)(2,1)} %get-tuple-element.26), channel_id=1, source_target_pairs={{0,1},{1,2},{2,3},{3,0},{4,5},{5,6},{6,7},{7,4},{8,9},{9,10},{10,1... | collective-permute-start | bytes 6291464 | tf_op jit(solution)/shard_map/ppermute | solution.py:148
  415.3 116.2 %collective-permute-start.43 = (bf16[2,1024,512]{2,1,0:T(8,128)(2,1)}, bf16[2,1024,512]{2,1,0:T(8,128)(2,1)}, u32[]{:S(2)}, u32[]{:S(2)}) collective-permute-start(bf16[2,1024,512]{2,1,0:T(8,128)(2,1)} %get-tuple-element.35), channel_id=1, source_target_pairs={{0,3},{1,0},{2,1},{3,2},{4,7},{5,4},{6,5},{7,6},{8,11},{9,8},{10,9... | collective-permute-start | bytes 6291464 | tf_op jit(solution)/shard_map/ppermute | solution.py:148
  438.3 89.9 %collective-permute-start.9 = (bf16[2,64,8192]{2,1,0:T(8,128)(2,1)}, bf16[2,64,8192]{2,1,0:T(8,128)(2,1)}, u32[]{:S(2)}, u32[]{:S(2)}) collective-permute-start(bf16[2,64,8192]{2,1,0:T(8,128)(2,1)} %get-tuple-element.27), channel_id=1, source_target_pairs={{0,3},{1,0},{2,1},{3,2},{4,7},{5,4},{6,5},{7,6},{8,11},{9,8},{10,9... | collective-permute-start | bytes 6291464 | tf_op jit(solution)/shard_map/ppermute | solution.py:148
  460.8 112.2 %collective-permute-start.24 = (bf16[2,64,8192]{2,1,0:T(8,128)(2,1)}, bf16[2,64,8192]{2,1,0:T(8,128)(2,1)S(1)}, u32[]{:S(2)}, u32[]{:S(2)}) collective-permute-start(bf16[2,64,8192]{2,1,0:T(8,128)(2,1)} %get-tuple-element.29), channel_id=1, source_target_pairs={{0,1},{1,2},{2,3},{3,0},{4,5},{5,6},{6,7},{7,4},{8,9},{9,10},{10,1... | collective-permute-start | bytes 6291464 | tf_op jit(solution)/shard_map/ppermute | solution.py:148
  483.1 361.2 %copy-start.2 = (bf16[2,1024,512]{2,1,0:T(8,128)(2,1)}, bf16[2,1024,512]{2,1,0:T(8,128)(2,1)S(1)}, u32[]{:S(2)}) copy-start(bf16[2,1024,512]{2,1,0:T(8,128)(2,1)S(1)} %collective-permute-done.40.up_ref) | copy-start | bytes 6291460
  483.2 91.9 %collective-permute-start.27 = (bf16[2,64,8192]{2,1,0:T(8,128)(2,1)}, bf16[2,64,8192]{2,1,0:T(8,128)(2,1)S(1)}, u32[]{:S(2)}, u32[]{:S(2)}) collective-permute-start(bf16[2,64,8192]{2,1,0:T(8,128)(2,1)} %get-tuple-element.30), channel_id=1, source_target_pairs={{0,3},{1,0},{2,1},{3,2},{4,7},{5,4},{6,5},{7,6},{8,11},{9,8},{10,9... | collective-permute-start | bytes 6291464 | tf_op jit(solution)/shard_map/ppermute | solution.py:148
  528.2 89.8 %collective-permute-start.7 = (bf16[2,64,8192]{2,1,0:T(8,128)(2,1)}, bf16[2,64,8192]{2,1,0:T(8,128)(2,1)S(1)}, u32[]{:S(2)}, u32[]{:S(2)}) collective-permute-start(bf16[2,64,8192]{2,1,0:T(8,128)(2,1)} %collective-permute-done.6.up_ref), channel_id=1, source_target_pairs={{0,1},{1,2},{2,3},{3,0},{4,5},{5,6},{6,7},{7,4},{8,9},{9,10},{10,1... | collective-permute-start | bytes 6291464 | tf_op jit(solution)/shard_map/ppermute | solution.py:148
  528.2 92.6 %collective-permute-start.10 = (bf16[2,64,8192]{2,1,0:T(8,128)(2,1)}, bf16[2,64,8192]{2,1,0:T(8,128)(2,1)S(1)}, u32[]{:S(2)}, u32[]{:S(2)}) collective-permute-start(bf16[2,64,8192]{2,1,0:T(8,128)(2,1)} %collective-permute-done.9.down_ref), channel_id=1, source_target_pairs={{0,3},{1,0},{2,1},{3,2},{4,7},{5,4},{6,5},{7,6},{8,11},{9,8},{10,9... | collective-permute-start | bytes 6291464 | tf_op jit(solution)/shard_map/ppermute | solution.py:148
  531.4 131.6 %collective-permute-start.41 = (bf16[2,1024,512]{2,1,0:T(8,128)(2,1)S(1)}, bf16[2,1024,512]{2,1,0:T(8,128)(2,1)}, u32[]{:S(2)}, u32[]{:S(2)}) collective-permute-start(bf16[2,1024,512]{2,1,0:T(8,128)(2,1)S(1)} %collective-permute-done.40.up_ref), channel_id=1, source_target_pairs={{0,1},{1,2},{2,3},{3,0},{4,5},{5,6},{6,7},{7,4},{8,9},{9,10},{10,1... | collective-permute-start | bytes 6291464 | tf_op jit(solution)/shard_map/ppermute | solution.py:148
  573.0 270.3 %copy-start.3 = (bf16[2,64,8192]{2,1,0:T(8,128)(2,1)}, bf16[2,64,8192]{2,1,0:T(8,128)(2,1)S(1)}, u32[]{:S(2)}) copy-start(bf16[2,64,8192]{2,1,0:T(8,128)(2,1)S(1)} %collective-permute-done.24.up_ref) | copy-start | bytes 6291460
  573.0 92.0 %collective-permute-start.44 = (bf16[2,1024,512]{2,1,0:T(8,128)(2,1)}, bf16[2,1024,512]{2,1,0:T(8,128)(2,1)}, u32[]{:S(2)}, u32[]{:S(2)}) collective-permute-start(bf16[2,1024,512]{2,1,0:T(8,128)(2,1)} %collective-permute-done.43.down_ref), channel_id=1, source_target_pairs={{0,3},{1,0},{2,1},{3,2},{4,7},{5,4},{6,5},{7,6},{8,11},{9,8},{10,9... | collective-permute-start | bytes 6291464 | tf_op jit(solution)/shard_map/ppermute | solution.py:148
  575.1 268.3 %copy-start.4 = (bf16[2,64,8192]{2,1,0:T(8,128)(2,1)}, bf16[2,64,8192]{2,1,0:T(8,128)(2,1)S(1)}, u32[]{:S(2)}) copy-start(bf16[2,64,8192]{2,1,0:T(8,128)(2,1)S(1)} %collective-permute-done.27.down_ref) | copy-start | bytes 6291460
  575.1 132.9 %collective-permute-start.25 = (bf16[2,64,8192]{2,1,0:T(8,128)(2,1)S(1)}, bf16[2,64,8192]{2,1,0:T(8,128)(2,1)}, u32[]{:S(2)}, u32[]{:S(2)}) collective-permute-start(bf16[2,64,8192]{2,1,0:T(8,128)(2,1)S(1)} %collective-permute-done.24.up_ref), channel_id=1, source_target_pairs={{0,1},{1,2},{2,3},{3,0},{4,5},{5,6},{6,7},{7,4},{8,9},{9,10},{10,1... | collective-permute-start | bytes 6291464 | tf_op jit(solution)/shard_map/ppermute | solution.py:148
  618.0 47.1 %copy-start = (bf16[2,64,8192]{2,1,0:T(8,128)(2,1)}, bf16[2,64,8192]{2,1,0:T(8,128)(2,1)S(1)}, u32[]{:S(2)}) copy-start(bf16[2,64,8192]{2,1,0:T(8,128)(2,1)S(1)} %collective-permute-done.7.up_ref) | copy-start | bytes 6291460
  618.0 90.0 %collective-permute-start.28 = (bf16[2,64,8192]{2,1,0:T(8,128)(2,1)S(1)}, bf16[2,64,8192]{2,1,0:T(8,128)(2,1)}, u32[]{:S(2)}, u32[]{:S(2)}) collective-permute-start(bf16[2,64,8192]{2,1,0:T(8,128)(2,1)S(1)} %collective-permute-done.27.down_ref), channel_id=1, source_target_pairs={{0,3},{1,0},{2,1},{3,2},{4,7},{5,4},{6,5},{7,6},{8,11},{9,8},{10,9... | collective-permute-start | bytes 6291464 | tf_op jit(solution)/shard_map/ppermute | solution.py:148
  620.8 120.2 %copy-start.1 = (bf16[2,64,8192]{2,1,0:T(8,128)(2,1)}, bf16[2,64,8192]{2,1,0:T(8,128)(2,1)S(1)}, u32[]{:S(2)}) copy-start(bf16[2,64,8192]{2,1,0:T(8,128)(2,1)S(1)} %collective-permute-done.10.down_ref) | copy-start | bytes 6291460
  620.8 116.1 %collective-permute-start.14 = (bf16[1,32,8192]{2,1,0:T(8,128)(2,1)S(1)}, bf16[1,32,8192]{2,1,0:T(8,128)(2,1)S(1)}, u32[]{:S(2)}, u32[]{:S(2)}) collective-permute-start(bf16[1,32,8192]{2,1,0:T(8,128)(2,1)S(1)} %slice.36), channel_id=1, source_target_pairs={{0,1},{1,2},{2,3},{3,0},{4,5},{5,6},{6,7},{7,4},{8,9},{9,10},{10,1... | collective-permute-start | bytes 1572872 | tf_op jit(solution)/shard_map/ppermute | solution.py:148
  663.0 73.9 %collective-permute-start.15 = (bf16[1,32,8192]{2,1,0:T(8,128)(2,1)S(1)}, bf16[1,32,8192]{2,1,0:T(8,128)(2,1)S(1)}, u32[]{:S(2)}, u32[]{:S(2)}) collective-permute-start(bf16[1,32,8192]{2,1,0:T(8,128)(2,1)S(1)} %slice.37), channel_id=1, source_target_pairs={{0,3},{1,0},{2,1},{3,2},{4,7},{5,4},{6,5},{7,6},{8,11},{9,8},{10,9... | collective-permute-start | bytes 1572872 | tf_op jit(solution)/shard_map/ppermute | solution.py:148
  665.0 59.7 %collective-permute-start.12 = (bf16[1,16,8192]{2,1,0:T(8,128)(2,1)S(1)}, bf16[1,16,8192]{2,1,0:T(8,128)(2,1)S(1)}, u32[]{:S(2)}, u32[]{:S(2)}) collective-permute-start(bf16[1,16,8192]{2,1,0:T(8,128)(2,1)S(1)} %get-tuple-element.65), channel_id=1, source_target_pairs={{0,1},{1,2},{2,3},{3,0},{4,5},{5,6},{6,7},{7,4},{8,9},{9,10},{10,1... | collective-permute-start | bytes 786440 | tf_op jit(solution)/shard_map/ppermute | solution.py:148
  708.0 39.2 %collective-permute-start.16 = (bf16[1,64,8192]{2,1,0:T(8,128)(2,1)S(1)}, bf16[1,64,8192]{2,1,0:T(8,128)(2,1)S(1)}, u32[]{:S(2)}, u32[]{:S(2)}) collective-permute-start(bf16[1,64,8192]{2,1,0:T(8,128)(2,1)S(1)} %slice.38), channel_id=1, source_target_pairs={{0,1},{1,2},{2,3},{3,0},{4,5},{5,6},{6,7},{7,4},{8,9},{9,10},{10,1... | collective-permute-start | bytes 3145736 | tf_op jit(solution)/shard_map/ppermute | solution.py:148
  708.0 18.8 %collective-permute-start.13 = (bf16[1,16,8192]{2,1,0:T(8,128)(2,1)S(1)}, bf16[1,16,8192]{2,1,0:T(8,128)(2,1)S(1)}, u32[]{:S(2)}, u32[]{:S(2)}) collective-permute-start(bf16[1,16,8192]{2,1,0:T(8,128)(2,1)S(1)} %get-tuple-element.63), channel_id=1, source_target_pairs={{0,3},{1,0},{2,1},{3,2},{4,7},{5,4},{6,5},{7,6},{8,11},{9,8},{10,9... | collective-permute-start | bytes 786440 | tf_op jit(solution)/shard_map/ppermute | solution.py:148
  724.7 122.9 %copy-start.11 = (bf16[1,16,8192]{2,1,0:T(8,128)(2,1)}, bf16[1,16,8192]{2,1,0:T(8,128)(2,1)S(1)}, u32[]{:S(2)}) copy-start(bf16[1,16,8192]{2,1,0:T(8,128)(2,1)S(1)} %collective-permute-done.12.up_ref) | copy-start | bytes 786436
  724.7 9.2 %collective-permute-start.11 = (bf16[1,16,8192]{2,1,0:T(8,128)(2,1)S(1)}, bf16[1,16,8192]{2,1,0:T(8,128)(2,1)S(1)}, u32[]{:S(2)}, u32[]{:S(2)}) collective-permute-start(bf16[1,16,8192]{2,1,0:T(8,128)(2,1)S(1)} %get-tuple-element.64), channel_id=1, source_target_pairs={{0,3},{1,0},{2,1},{3,2},{4,7},{5,4},{6,5},{7,6},{8,11},{9,8},{10,9... | collective-permute-start | bytes 786440 | tf_op jit(solution)/shard_map/ppermute | solution.py:148
  726.7 116.6 %copy-start.12 = (bf16[1,16,8192]{2,1,0:T(8,128)(2,1)}, bf16[1,16,8192]{2,1,0:T(8,128)(2,1)S(1)}, u32[]{:S(2)}) copy-start(bf16[1,16,8192]{2,1,0:T(8,128)(2,1)S(1)} %collective-permute-done.13.down_ref) | copy-start | bytes 786436
  726.7 144.7 %collective-permute-start.42 = (bf16[2,1024,512]{2,1,0:T(8,128)(2,1)}, bf16[2,1024,512]{2,1,0:T(8,128)(2,1)}, u32[]{:S(2)}, u32[]{:S(2)}) collective-permute-start(bf16[2,1024,512]{2,1,0:T(8,128)(2,1)} %collective-permute-done.41.up_ref), channel_id=1, source_target_pairs={{0,1},{1,2},{2,3},{3,0},{4,5},{5,6},{6,7},{7,4},{8,9},{9,10},{10,1... | collective-permute-start | bytes 6291464 | tf_op jit(solution)/shard_map/ppermute | solution.py:148
  733.9 137.6 %collective-permute-start.45 = (bf16[2,1024,512]{2,1,0:T(8,128)(2,1)}, bf16[2,1024,512]{2,1,0:T(8,128)(2,1)}, u32[]{:S(2)}, u32[]{:S(2)}) collective-permute-start(bf16[2,1024,512]{2,1,0:T(8,128)(2,1)} %collective-permute-done.44.down_ref), channel_id=1, source_target_pairs={{0,3},{1,0},{2,1},{3,2},{4,7},{5,4},{6,5},{7,6},{8,11},{9,8},{10,9... | collective-permute-start | bytes 6291464 | tf_op jit(solution)/shard_map/ppermute | solution.py:148
  736.9 110.7 %copy-start.9 = (bf16[1,32,8192]{2,1,0:T(8,128)(2,1)}, bf16[1,32,8192]{2,1,0:T(8,128)(2,1)S(1)}, u32[]{:S(2)}) copy-start(bf16[1,32,8192]{2,1,0:T(8,128)(2,1)S(1)} %collective-permute-done.14.up_ref) | copy-start | bytes 1572868
  736.9 137.9 %collective-permute-start.26 = (bf16[2,64,8192]{2,1,0:T(8,128)(2,1)}, bf16[2,64,8192]{2,1,0:T(8,128)(2,1)}, u32[]{:S(2)}, u32[]{:S(2)}) collective-permute-start(bf16[2,64,8192]{2,1,0:T(8,128)(2,1)} %collective-permute-done.25.up_ref), channel_id=1, source_target_pairs={{0,1},{1,2},{2,3},{3,0},{4,5},{5,6},{6,7},{7,4},{8,9},{9,10},{10,1... | collective-permute-start | bytes 6291464 | tf_op jit(solution)/shard_map/ppermute | solution.py:148
  736.9 0.8 copy-start.10
  737.8 137.1 %collective-permute-start.29 = (bf16[2,64,8192]{2,1,0:T(8,128)(2,1)}, bf16[2,64,8192]{2,1,0:T(8,128)(2,1)}, u32[]{:S(2)}, u32[]{:S(2)}) collective-permute-start(bf16[2,64,8192]{2,1,0:T(8,128)(2,1)} %collective-permute-done.28.down_ref), channel_id=1, source_target_pairs={{0,3},{1,0},{2,1},{3,2},{4,7},{5,4},{6,5},{7,6},{8,11},{9,8},{10,9... | collective-permute-start | bytes 6291464 | tf_op jit(solution)/shard_map/ppermute | solution.py:148
  747.2 96.3 %copy-start.7 = (bf16[1,64,8192]{2,1,0:T(8,128)(2,1)}, bf16[1,64,8192]{2,1,0:T(8,128)(2,1)S(1)}, u32[]{:S(2)}) copy-start(bf16[1,64,8192]{2,1,0:T(8,128)(2,1)S(1)} %collective-permute-done.16.up_ref) | copy-start | bytes 3145732
  747.2 96.1 %collective-permute-start.17 = (bf16[1,64,8192]{2,1,0:T(8,128)(2,1)S(1)}, bf16[1,64,8192]{2,1,0:T(8,128)(2,1)S(1)}, u32[]{:S(2)}, u32[]{:S(2)}) collective-permute-start(bf16[1,64,8192]{2,1,0:T(8,128)(2,1)S(1)} %slice.39), channel_id=1, source_target_pairs={{0,3},{1,0},{2,1},{3,2},{4,7},{5,4},{6,5},{7,6},{8,11},{9,8},{10,9... | collective-permute-start | bytes 3145736 | tf_op jit(solution)/shard_map/ppermute | solution.py:148
  843.3 1.0 copy-start.8
  843.3 27.3 %collective-permute-start.8 = (bf16[1,16,8192]{2,1,0:T(8,128)(2,1)}, bf16[1,16,8192]{2,1,0:T(8,128)(2,1)S(1)}, u32[]{:S(2)}, u32[]{:S(2)}) collective-permute-start(bf16[1,16,8192]{2,1,0:T(8,128)(2,1)} %get-tuple-element.66), channel_id=1, source_target_pairs={{0,1},{1,2},{2,3},{3,0},{4,5},{5,6},{6,7},{7,4},{8,9},{9,10},{10,1... | collective-permute-start | bytes 786440 | tf_op jit(solution)/shard_map/ppermute | solution.py:148
  (1 other events, 0.7 us)

commit v2 on v1

--- a/solution.py
+++ b/solution.py
@@ -161,14 +161,15 @@
         def small_last(like):
             layers, half = like.shape[0], like.shape[1] // 2
             quarter = half // 4
-            ends = [(layers - 1, 1, 0, half - 2 * quarter)] + [(layers - 1, 1, half - i * quarter, quarter) for i in (2, 1)]
+            small = quarter // 2
+            ends = [(layers - 1, 1, 0, half - 3 * small), (layers - 1, 1, half - 3 * small, 2 * small), (layers - 1, 1, half - small, small)]
             return [(0, layers - 1, 0, half)] * (layers > 1) + ends
 
         def join(parts):
             first = jnp.concatenate(parts[:2], axis=1)
             return jnp.concatenate([first, *parts[2:]], axis=0) if len(parts) > 2 else first
 
-        order = (2, 1, 0)
+        order = (0, 1, 2)
         moving = [None] * 3
         new_w, new_m, new_v = [None] * 3, [None] * 3, [None] * 3
         for k in order:
@@ -196,7 +197,7 @@
                         (part, send([p[part[0] : part[0] + part[1], part[2] : part[2] + part[3]] for p in whole_piece])) for part in parts
                     ]
                 for i, (part, pieces) in enumerate(here):
-                    last = (hop, k, i) == (n - 1, order[-1], len(here) - 1)
+                    last = (hop, k) == (n - 1, order[-1]) and i >= len(here) - 2
                     new_w[k] = place("dp", hop, new_w[k], pieces, part[0], part[2], m[k].shape[1] // 2, last)
         return (*new_w, *new_m, *new_v)
 

time: 879 us -> 876 us (level)
  no operation moved by 1% of the time
where the time goes in v2:
time: 876 us
  waiting for transfers between devices  674 us (77%)
  Pallas kernels  95.4 us (11%)
  starting transfers between devices  58.5 us (7%)
  other arithmetic  29.3 us (3%)
  local copies, waits for them, and re-layouts  17.9 us (2%)
    ppermute x46, waiting for transfers between devices, send(): moved.append(lax.ppermute(p, 'dp', way))  674 us
    pallas_call x3, Pallas kernels, update(): pl.pallas_call(kernel, out_shape=(jax.ShapeDtypeStruct(w.shape, jnp.bfloa...  61.6 us
    ppermute x46, starting transfers between devices, send(): moved.append(lax.ppermute(p, 'dp', way))  58.5 us
    pallas_call x12, Pallas kernels, place(): pl.pallas_call(kernel, out_shape=jax.ShapeDtypeStruct(whole.shape, whole....  32.8 us
    convert_element_type x6, other arithmetic, add(): return (a.astype(jnp.float32) + b.astype(jnp.float32)).astype(jnp.bfloat16)  29.3 us
  transfers between devices with their start and end apart: 46, of which 19 were waited for; matrix products, arithmetic and copies ran while one was open for 5% of the time, Pallas kernels for 11%

profile of v2, /device:TPU:112, one launch (start us, length us, event | category | flops | bytes accessed | tf_op | source)
XLA Modules:
  0.0 876.2 jit_solution(12548934000182944814)
XLA Ops:
  0.7 2.6 dynamic-slice_bitcast_fusion.6
  3.3 2.3 collective-permute-start.1
  6.7 1.7 collective-permute-start
  8.4 1.6 collective-permute-start.5
  10.0 3.0 dynamic-slice_bitcast_fusion.4
  13.5 4.6 dynamic-slice_bitcast_fusion
  19.4 12.0 %collective-permute-done = bf16[1,16,8192]{2,1,0:T(8,128)(2,1)S(1)} collective-permute-done((bf16[1,16,8192]{2,1,0:T(8,128)(2,1)S(1)}, bf16[1,16,8192]{2,1,0:T(8,128)(2,1)S(1)}, u32[]{:S(2)}, u32[]{:S(2)}) %collective-permute-start) | collective-permute-done | bytes 262176 | tf_op jit(solution)/shard_map/ppermute | solution.py:148
  31.4 2.0 collective-permute-start.31
  35.2 4.7 dynamic-slice_bitcast_fusion.2
  39.9 77.2 %collective-permute-done.6 = bf16[1,48,8192]{2,1,0:T(8,128)(2,1)} collective-permute-done((bf16[1,48,8192]{2,1,0:T(8,128)(2,1)S(1)}, bf16[1,48,8192]{2,1,0:T(8,128)(2,1)}, u32[]{:S(2)}, u32[]{:S(2)}) %collective-permute-start.6) | collective-permute-done | bytes 786464 | tf_op jit(solution)/shard_map/ppermute | solution.py:148
  117.1 3.2 collective-permute-start.19
  120.3 3.8 fusion.9
  124.3 3.2 collective-permute-start.8
  127.5 4.1 fusion.1
  131.7 35.5 %collective-permute-done.16 = bf16[2,64,8192]{2,1,0:T(8,128)(2,1)} collective-permute-done((bf16[2,64,8192]{2,1,0:T(8,128)(2,1)}, bf16[2,64,8192]{2,1,0:T(8,128)(2,1)}, u32[]{:S(2)}, u32[]{:S(2)}) %collective-permute-start.16) | collective-permute-done | bytes 2097184 | tf_op jit(solution)/shard_map/ppermute | solution.py:148
  167.1 1.5 collective-permute-start.32
  168.6 5.0 fusion.5
  174.3 37.7 %collective-permute-done.3 = bf16[2,64,8192]{2,1,0:T(8,128)(2,1)S(1)} collective-permute-done((bf16[2,64,8192]{2,1,0:T(8,128)(2,1)S(1)}, bf16[2,64,8192]{2,1,0:T(8,128)(2,1)S(1)}, u32[]{:S(2)}, u32[]{:S(2)}) %collective-permute-start.3) | collective-permute-done | bytes 2097184 | tf_op jit(solution)/shard_map/ppermute | solution.py:148
  212.0 1.5 collective-permute-start.20
  213.4 5.1 fusion.8
  219.1 37.8 %collective-permute-done.29 = bf16[2,1024,512]{2,1,0:T(8,128)(2,1)S(1)} collective-permute-done((bf16[2,1024,512]{2,1,0:T(8,128)(2,1)S(1)}, bf16[2,1024,512]{2,1,0:T(8,128)(2,1)S(1)}, u32[]{:S(2)}, u32[]{:S(2)}) %collective-permute-start.29) | collective-permute-done | bytes 2097184 | tf_op jit(solution)/shard_map/ppermute | solution.py:148
  256.9 1.5 collective-permute-start.9
  258.4 5.5 fusion
  264.4 37.4 %collective-permute-done.17 = bf16[2,64,8192]{2,1,0:T(8,128)(2,1)S(1)} collective-permute-done((bf16[2,64,8192]{2,1,0:T(8,128)(2,1)S(1)}, bf16[2,64,8192]{2,1,0:T(8,128)(2,1)S(1)}, u32[]{:S(2)}, u32[]{:S(2)}) %collective-permute-start.17) | collective-permute-done | bytes 2097184 | tf_op jit(solution)/shard_map/ppermute | solution.py:148
  301.8 1.5 collective-permute-start.33
  303.3 5.8 fusion.4
  309.7 37.1 %collective-permute-done.4.up_ref = bf16[2,64,8192]{2,1,0:T(8,128)(2,1)S(1)} collective-permute-done((bf16[2,64,8192]{2,1,0:T(8,128)(2,1)}, bf16[2,64,8192]{2,1,0:T(8,128)(2,1)S(1)}, u32[]{:S(2)}, u32[]{:S(2)}) %collective-permute-start.4) | collective-permute-done | bytes 2097184 | tf_op jit(solution)/shard_map/ppermute | solution.py:148
  346.8 1.5 collective-permute-start.21
  349.6 20.5 %update.3 = (bf16[2,512,8192]{2,1,0:T(8,128)(2,1)}, f32[2,128,8192]{2,1,0:T(8,128)}, f32[2,128,8192]{2,1,0:T(8,128)}, bf16[2,64,8192]{2,1,0:T(8,128)(2,1)}, bf16[2,64,8192]{2,1,0:T(8,128)(2,1)}) custom-call(s32[1]{0:T(128)} %bitcast.me_ref, bf16[2,64,8192]{2,1,0:T(8,128)(2,1)} %copy-done.5, bf16[2,64,8192]{2,1,0:T(8,128)(2,1)} %copy-done.6, ...), custom_call_target="tpu_custom_call" | custom-call | flops 41943040 | bytes 54525952 | tf_op jit(solution)/shard_map/update/pallas_call | solution.py:42
  370.6 21.2 %collective-permute-done.30.up_ref = bf16[2,1024,512]{2,1,0:T(8,128)(2,1)} collective-permute-done((bf16[2,1024,512]{2,1,0:T(8,128)(2,1)}, bf16[2,1024,512]{2,1,0:T(8,128)(2,1)}, u32[]{:S(2)}, u32[]{:S(2)}) %collective-permute-start.30) | collective-permute-done | bytes 2097184 | tf_op jit(solution)/shard_map/ppermute | solution.py:148
  391.8 20.6 %update.5 = (bf16[2,8192,512]{2,1,0:T(8,128)(2,1)}, f32[2,2048,512]{2,1,0:T(8,128)}, f32[2,2048,512]{2,1,0:T(8,128)}, bf16[2,1024,512]{2,1,0:T(8,128)(2,1)}, bf16[2,1024,512]{2,1,0:T(8,128)(2,1)}) custom-call(s32[1]{0:T(128)} %bitcast.me_ref, bf16[2,1024,512]{2,1,0:T(8,128)(2,1)} %collective-permute-done.30.up_ref, ...), custom_call_target="tpu_custom_call" | custom-call | flops 41943040 | bytes 54525952 | tf_op jit(solution)/shard_map/update/pallas_call | solution.py:42
  413.3 2.5 collective-permute-start.37
  415.8 21.0 %collective-permute-done.18.up_ref = bf16[2,64,8192]{2,1,0:T(8,128)(2,1)} collective-permute-done((bf16[2,64,8192]{2,1,0:T(8,128)(2,1)}, bf16[2,64,8192]{2,1,0:T(8,128)(2,1)}, u32[]{:S(2)}, u32[]{:S(2)}) %collective-permute-start.18) | collective-permute-done | bytes 2097184 | tf_op jit(solution)/shard_map/ppermute | solution.py:148
  436.8 1.5 collective-permute-start.13
  438.2 20.5 %update.4 = (bf16[2,512,8192]{2,1,0:T(8,128)(2,1)}, f32[2,128,8192]{2,1,0:T(8,128)}, f32[2,128,8192]{2,1,0:T(8,128)}, bf16[2,64,8192]{2,1,0:T(8,128)(2,1)}, bf16[2,64,8192]{2,1,0:T(8,128)(2,1)}) custom-call(s32[1]{0:T(128)} %bitcast.me_ref, bf16[2,64,8192]{2,1,0:T(8,128)(2,1)} %collective-permute-done.18.up_ref, ...), custom_call_target="tpu_custom_call" | custom-call | flops 41943040 | bytes 54525952 | tf_op jit(solution)/shard_map/update/pallas_call | solution.py:42
  459.3 22.3 %collective-permute-done.10.up_ref = bf16[2,64,8192]{2,1,0:T(8,128)(2,1)S(1)} collective-permute-done((bf16[2,64,8192]{2,1,0:T(8,128)(2,1)}, bf16[2,64,8192]{2,1,0:T(8,128)(2,1)S(1)}, u32[]{:S(2)}, u32[]{:S(2)}) %collective-permute-start.10) | collective-permute-done | bytes 2097184 | tf_op jit(solution)/shard_map/ppermute | solution.py:148
  481.6 1.5 collective-permute-start.25
  483.1 43.6 %collective-permute-done.34.up_ref = bf16[2,1024,512]{2,1,0:T(8,128)(2,1)} collective-permute-done((bf16[2,1024,512]{2,1,0:T(8,128)(2,1)}, bf16[2,1024,512]{2,1,0:T(8,128)(2,1)}, u32[]{:S(2)}, u32[]{:S(2)}) %collective-permute-start.34) | collective-permute-done | bytes 2097184 | tf_op jit(solution)/shard_map/ppermute | solution.py:148
  526.7 3.2 collective-permute-start.38
  529.9 41.6 %collective-permute-done.22.up_ref = bf16[2,64,8192]{2,1,0:T(8,128)(2,1)S(1)} collective-permute-done((bf16[2,64,8192]{2,1,0:T(8,128)(2,1)}, bf16[2,64,8192]{2,1,0:T(8,128)(2,1)S(1)}, u32[]{:S(2)}, u32[]{:S(2)}) %collective-permute-start.22) | collective-permute-done | bytes 2097184 | tf_op jit(solution)/shard_map/ppermute | solution.py:148
  571.5 1.5 collective-permute-start.14
  573.5 42.9 %collective-permute-done.35.up_ref = bf16[2,1024,512]{2,1,0:T(8,128)(2,1)S(1)} collective-permute-done((bf16[2,1024,512]{2,1,0:T(8,128)(2,1)}, bf16[2,1024,512]{2,1,0:T(8,128)(2,1)S(1)}, u32[]{:S(2)}, u32[]{:S(2)}) %collective-permute-start.35) | collective-permute-done | bytes 2097184 | tf_op jit(solution)/shard_map/ppermute | solution.py:148
  616.4 1.5 collective-permute-start.26
  618.7 42.8 %collective-permute-done.11.up_ref = bf16[2,64,8192]{2,1,0:T(8,128)(2,1)} collective-permute-done((bf16[2,64,8192]{2,1,0:T(8,128)(2,1)S(1)}, bf16[2,64,8192]{2,1,0:T(8,128)(2,1)}, u32[]{:S(2)}, u32[]{:S(2)}) %collective-permute-start.11) | collective-permute-done | bytes 2097184 | tf_op jit(solution)/shard_map/ppermute | solution.py:148
  661.5 1.5 collective-permute-start.43
  663.7 42.8 %collective-permute-done.23.up_ref = bf16[2,64,8192]{2,1,0:T(8,128)(2,1)} collective-permute-done((bf16[2,64,8192]{2,1,0:T(8,128)(2,1)S(1)}, bf16[2,64,8192]{2,1,0:T(8,128)(2,1)}, u32[]{:S(2)}, u32[]{:S(2)}) %collective-permute-start.23) | collective-permute-done | bytes 2097184 | tf_op jit(solution)/shard_map/ppermute | solution.py:148
  706.4 3.2 collective-permute-start.41
  709.7 13.4 %collective-permute-done.36.up_ref = bf16[1,128,512]{2,1,0:T(8,128)(2,1)S(1)} collective-permute-done((bf16[1,128,512]{2,1,0:T(8,128)(2,1)S(1)}, bf16[1,128,512]{2,1,0:T(8,128)(2,1)S(1)}, u32[]{:S(2)}, u32[]{:S(2)}) %collective-permute-start.36) | collective-permute-done | bytes 131104 | tf_op jit(solution)/shard_map/ppermute | solution.py:148
  723.2 5.6 collective-permute-done.40.up_ref
  728.8 3.2 collective-permute-start.15
  732.1 3.2 collective-permute-start.27
  735.4 15.9 %collective-permute-done.44.up_ref = bf16[1,1024,512]{2,1,0:T(8,128)(2,1)S(1)} collective-permute-done((bf16[1,1024,512]{2,1,0:T(8,128)(2,1)S(1)}, bf16[1,1024,512]{2,1,0:T(8,128)(2,1)S(1)}, u32[]{:S(2)}, u32[]{:S(2)}) %collective-permute-start.44) | collective-permute-done | bytes 1048608 | tf_op jit(solution)/shard_map/ppermute | solution.py:148
  753.4 86.0 %collective-permute-done.45.down_ref = bf16[1,1024,512]{2,1,0:T(8,128)(2,1)S(1)} collective-permute-done((bf16[1,1024,512]{2,1,0:T(8,128)(2,1)S(1)}, bf16[1,1024,512]{2,1,0:T(8,128)(2,1)S(1)}, u32[]{:S(2)}, u32[]{:S(2)}) %collective-permute-start.45) | collective-permute-done | bytes 1048608 | tf_op jit(solution)/shard_map/ppermute | solution.py:148
  839.4 3.7 collective-permute-start.39
  843.1 3.3 place.12.whole_ref
  846.4 3.3 place.18.whole_ref
  849.7 3.3 place.15.whole_ref
  853.0 3.3 place.13.whole_ref
  856.3 3.3 place.19.whole_ref
  859.7 2.6 place.20.whole_ref
  862.2 2.2 place.21.whole_ref
  864.4 3.3 place.16.whole_ref
  869.4 3.3 place.14
  872.7 3.3 place.17
  (88 shorter events, 16.4 us)
Async XLA Ops:
  3.3 31.5 %collective-permute-start.1 = (bf16[1,48,8192]{2,1,0:T(8,128)(2,1)}, bf16[1,48,8192]{2,1,0:T(8,128)(2,1)}, u32[]{:S(2)}, u32[]{:S(2)}) collective-permute-start(bf16[1,48,8192]{2,1,0:T(8,128)(2,1)} %get-tuple-element.60), channel_id=1, source_target_pairs={{0,1},{1,2},{2,3},{3,0},{4,5},{5,6},{6,7},{7,4},{8,9},{9,10},{10,1... | collective-permute-start | bytes 2359304 | tf_op jit(solution)/shard_map/ppermute | solution.py:148
  6.7 24.7 %collective-permute-start = (bf16[1,16,8192]{2,1,0:T(8,128)(2,1)S(1)}, bf16[1,16,8192]{2,1,0:T(8,128)(2,1)S(1)}, u32[]{:S(2)}, u32[]{:S(2)}) collective-permute-start(bf16[1,16,8192]{2,1,0:T(8,128)(2,1)S(1)} %get-tuple-element.26), channel_id=1, source_target_pairs={{0,1},{1,2},{2,3},{3,0},{4,5},{5,6},{6,7},{7,4},{8,9},{9,10},{10,1... | collective-permute-start | bytes 786440 | tf_op jit(solution)/shard_map/ppermute | solution.py:148
  8.4 25.0 %collective-permute-start.5 = (bf16[1,16,8192]{2,1,0:T(8,128)(2,1)S(1)}, bf16[1,16,8192]{2,1,0:T(8,128)(2,1)S(1)}, u32[]{:S(2)}, u32[]{:S(2)}) collective-permute-start(bf16[1,16,8192]{2,1,0:T(8,128)(2,1)S(1)} %get-tuple-element.27), channel_id=1, source_target_pairs={{0,3},{1,0},{2,1},{3,2},{4,7},{5,4},{6,5},{7,6},{8,11},{9,8},{10,9... | collective-permute-start | bytes 786440 | tf_op jit(solution)/shard_map/ppermute | solution.py:148
  13.0 104.1 %collective-permute-start.2 = (bf16[1,64,8192]{2,1,0:T(8,128)(2,1)}, bf16[1,64,8192]{2,1,0:T(8,128)(2,1)}, u32[]{:S(2)}, u32[]{:S(2)}) collective-permute-start(bf16[1,64,8192]{2,1,0:T(8,128)(2,1)} %get-tuple-element.62), channel_id=1, source_target_pairs={{0,1},{1,2},{2,3},{3,0},{4,5},{5,6},{6,7},{7,4},{8,9},{9,10},{10,1... | collective-permute-start | bytes 3145736 | tf_op jit(solution)/shard_map/ppermute | solution.py:148
  13.5 21.4 %copy-start.9 = (bf16[1,48,8192]{2,1,0:T(8,128)(2,1)S(1)}, bf16[1,48,8192]{2,1,0:T(8,128)(2,1)}, u32[]{:S(2)}) copy-start(bf16[1,48,8192]{2,1,0:T(8,128)(2,1)} %get-tuple-element.59) | copy-start | bytes 2359300
  18.0 106.2 %collective-permute-start.28 = (bf16[2,1024,512]{2,1,0:T(8,128)(2,1)}, bf16[2,1024,512]{2,1,0:T(8,128)(2,1)S(1)}, u32[]{:S(2)}, u32[]{:S(2)}) collective-permute-start(bf16[2,1024,512]{2,1,0:T(8,128)(2,1)} %get-tuple-element.48), channel_id=1, source_target_pairs={{0,1},{1,2},{2,3},{3,0},{4,5},{5,6},{6,7},{7,4},{8,9},{9,10},{10,1... | collective-permute-start | bytes 6291464 | tf_op jit(solution)/shard_map/ppermute | solution.py:148
  31.4 96.1 %collective-permute-start.31 = (bf16[2,1024,512]{2,1,0:T(8,128)(2,1)}, bf16[2,1024,512]{2,1,0:T(8,128)(2,1)}, u32[]{:S(2)}, u32[]{:S(2)}) collective-permute-start(bf16[2,1024,512]{2,1,0:T(8,128)(2,1)} %get-tuple-element.47), channel_id=1, source_target_pairs={{0,3},{1,0},{2,1},{3,2},{4,7},{5,4},{6,5},{7,6},{8,11},{9,8},{10,9... | collective-permute-start | bytes 6291464 | tf_op jit(solution)/shard_map/ppermute | solution.py:148
  33.4 0.7 copy-start.12
  34.1 86.2 %collective-permute-start.7 = (bf16[1,64,8192]{2,1,0:T(8,128)(2,1)}, bf16[1,64,8192]{2,1,0:T(8,128)(2,1)S(1)}, u32[]{:S(2)}, u32[]{:S(2)}) collective-permute-start(bf16[1,64,8192]{2,1,0:T(8,128)(2,1)} %get-tuple-element.61), channel_id=1, source_target_pairs={{0,3},{1,0},{2,1},{3,2},{4,7},{5,4},{6,5},{7,6},{8,11},{9,8},{10,9... | collective-permute-start | bytes 3145736 | tf_op jit(solution)/shard_map/ppermute | solution.py:148
  34.8 82.3 %collective-permute-start.6 = (bf16[1,48,8192]{2,1,0:T(8,128)(2,1)S(1)}, bf16[1,48,8192]{2,1,0:T(8,128)(2,1)}, u32[]{:S(2)}, u32[]{:S(2)}) collective-permute-start(bf16[1,48,8192]{2,1,0:T(8,128)(2,1)S(1)} %copy-done.9), channel_id=1, source_target_pairs={{0,3},{1,0},{2,1},{3,2},{4,7},{5,4},{6,5},{7,6},{8,11},{9,8},{10,9... | collective-permute-start | bytes 2359304 | tf_op jit(solution)/shard_map/ppermute | solution.py:148
  117.1 50.0 %collective-permute-start.16 = (bf16[2,64,8192]{2,1,0:T(8,128)(2,1)}, bf16[2,64,8192]{2,1,0:T(8,128)(2,1)}, u32[]{:S(2)}, u32[]{:S(2)}) collective-permute-start(bf16[2,64,8192]{2,1,0:T(8,128)(2,1)} %get-tuple-element.54), channel_id=1, source_target_pairs={{0,1},{1,2},{2,3},{3,0},{4,5},{5,6},{6,7},{7,4},{8,9},{9,10},{10,1... | collective-permute-start | bytes 6291464 | tf_op jit(solution)/shard_map/ppermute | solution.py:148
  117.1 51.5 %collective-permute-start.19 = (bf16[2,64,8192]{2,1,0:T(8,128)(2,1)}, bf16[2,64,8192]{2,1,0:T(8,128)(2,1)}, u32[]{:S(2)}, u32[]{:S(2)}) collective-permute-start(bf16[2,64,8192]{2,1,0:T(8,128)(2,1)} %get-tuple-element.53), channel_id=1, source_target_pairs={{0,3},{1,0},{2,1},{3,2},{4,7},{5,4},{6,5},{7,6},{8,11},{9,8},{10,9... | collective-permute-start | bytes 6291464 | tf_op jit(solution)/shard_map/ppermute | solution.py:148
  124.2 87.8 %collective-permute-start.3 = (bf16[2,64,8192]{2,1,0:T(8,128)(2,1)S(1)}, bf16[2,64,8192]{2,1,0:T(8,128)(2,1)S(1)}, u32[]{:S(2)}, u32[]{:S(2)}) collective-permute-start(bf16[2,64,8192]{2,1,0:T(8,128)(2,1)S(1)} %get-tuple-element.58), channel_id=1, source_target_pairs={{0,1},{1,2},{2,3},{3,0},{4,5},{5,6},{6,7},{7,4},{8,9},{9,10},{10,1... | collective-permute-start | bytes 6291464 | tf_op jit(solution)/shard_map/ppermute | solution.py:148
  124.3 89.1 %collective-permute-start.8 = (bf16[2,64,8192]{2,1,0:T(8,128)(2,1)S(1)}, bf16[2,64,8192]{2,1,0:T(8,128)(2,1)S(1)}, u32[]{:S(2)}, u32[]{:S(2)}) collective-permute-start(bf16[2,64,8192]{2,1,0:T(8,128)(2,1)S(1)} %get-tuple-element.57), channel_id=1, source_target_pairs={{0,3},{1,0},{2,1},{3,2},{4,7},{5,4},{6,5},{7,6},{8,11},{9,8},{10,9... | collective-permute-start | bytes 6291464 | tf_op jit(solution)/shard_map/ppermute | solution.py:148
  131.5 125.4 %collective-permute-start.29 = (bf16[2,1024,512]{2,1,0:T(8,128)(2,1)S(1)}, bf16[2,1024,512]{2,1,0:T(8,128)(2,1)S(1)}, u32[]{:S(2)}, u32[]{:S(2)}) collective-permute-start(bf16[2,1024,512]{2,1,0:T(8,128)(2,1)S(1)} %get-tuple-element.46), channel_id=1, source_target_pairs={{0,1},{1,2},{2,3},{3,0},{4,5},{5,6},{6,7},{7,4},{8,9},{9,10},{10,1... | collective-permute-start | bytes 6291464 | tf_op jit(solution)/shard_map/ppermute | solution.py:148
  167.1 91.2 %collective-permute-start.32 = (bf16[2,1024,512]{2,1,0:T(8,128)(2,1)S(1)}, bf16[2,1024,512]{2,1,0:T(8,128)(2,1)S(1)}, u32[]{:S(2)}, u32[]{:S(2)}) collective-permute-start(bf16[2,1024,512]{2,1,0:T(8,128)(2,1)S(1)} %get-tuple-element.45), channel_id=1, source_target_pairs={{0,3},{1,0},{2,1},{3,2},{4,7},{5,4},{6,5},{7,6},{8,11},{9,8},{10,9... | collective-permute-start | bytes 6291464 | tf_op jit(solution)/shard_map/ppermute | solution.py:148
  173.6 128.2 %collective-permute-start.17 = (bf16[2,64,8192]{2,1,0:T(8,128)(2,1)S(1)}, bf16[2,64,8192]{2,1,0:T(8,128)(2,1)S(1)}, u32[]{:S(2)}, u32[]{:S(2)}) collective-permute-start(bf16[2,64,8192]{2,1,0:T(8,128)(2,1)S(1)} %get-tuple-element.52), channel_id=1, source_target_pairs={{0,1},{1,2},{2,3},{3,0},{4,5},{5,6},{6,7},{7,4},{8,9},{9,10},{10,1... | collective-permute-start | bytes 6291464 | tf_op jit(solution)/shard_map/ppermute | solution.py:148
  212.0 91.3 %collective-permute-start.20 = (bf16[2,64,8192]{2,1,0:T(8,128)(2,1)S(1)}, bf16[2,64,8192]{2,1,0:T(8,128)(2,1)S(1)}, u32[]{:S(2)}, u32[]{:S(2)}) collective-permute-start(bf16[2,64,8192]{2,1,0:T(8,128)(2,1)S(1)} %get-tuple-element.51), channel_id=1, source_target_pairs={{0,3},{1,0},{2,1},{3,2},{4,7},{5,4},{6,5},{7,6},{8,11},{9,8},{10,9... | collective-permute-start | bytes 6291464 | tf_op jit(solution)/shard_map/ppermute | solution.py:148
  218.5 128.3 %collective-permute-start.4 = (bf16[2,64,8192]{2,1,0:T(8,128)(2,1)}, bf16[2,64,8192]{2,1,0:T(8,128)(2,1)S(1)}, u32[]{:S(2)}, u32[]{:S(2)}) collective-permute-start(bf16[2,64,8192]{2,1,0:T(8,128)(2,1)} %get-tuple-element.56), channel_id=1, source_target_pairs={{0,1},{1,2},{2,3},{3,0},{4,5},{5,6},{6,7},{7,4},{8,9},{9,10},{10,1... | collective-permute-start | bytes 6291464 | tf_op jit(solution)/shard_map/ppermute | solution.py:148
  256.9 91.4 %collective-permute-start.9 = (bf16[2,64,8192]{2,1,0:T(8,128)(2,1)S(1)}, bf16[2,64,8192]{2,1,0:T(8,128)(2,1)S(1)}, u32[]{:S(2)}, u32[]{:S(2)}) collective-permute-start(bf16[2,64,8192]{2,1,0:T(8,128)(2,1)S(1)} %get-tuple-element.55), channel_id=1, source_target_pairs={{0,3},{1,0},{2,1},{3,2},{4,7},{5,4},{6,5},{7,6},{8,11},{9,8},{10,9... | collective-permute-start | bytes 6291464 | tf_op jit(solution)/shard_map/ppermute | solution.py:148
  263.9 128.0 %collective-permute-start.30 = (bf16[2,1024,512]{2,1,0:T(8,128)(2,1)}, bf16[2,1024,512]{2,1,0:T(8,128)(2,1)}, u32[]{:S(2)}, u32[]{:S(2)}) collective-permute-start(bf16[2,1024,512]{2,1,0:T(8,128)(2,1)} %get-tuple-element.44), channel_id=1, source_target_pairs={{0,1},{1,2},{2,3},{3,0},{4,5},{5,6},{6,7},{7,4},{8,9},{9,10},{10,1... | collective-permute-start | bytes 6291464 | tf_op jit(solution)/shard_map/ppermute | solution.py:148
  301.8 90.0 %collective-permute-start.33 = (bf16[2,1024,512]{2,1,0:T(8,128)(2,1)}, bf16[2,1024,512]{2,1,0:T(8,128)(2,1)}, u32[]{:S(2)}, u32[]{:S(2)}) collective-permute-start(bf16[2,1024,512]{2,1,0:T(8,128)(2,1)} %get-tuple-element.43), channel_id=1, source_target_pairs={{0,3},{1,0},{2,1},{3,2},{4,7},{5,4},{6,5},{7,6},{8,11},{9,8},{10,9... | collective-permute-start | bytes 6291464 | tf_op jit(solution)/shard_map/ppermute | solution.py:148
  309.1 127.7 %collective-permute-start.18 = (bf16[2,64,8192]{2,1,0:T(8,128)(2,1)}, bf16[2,64,8192]{2,1,0:T(8,128)(2,1)}, u32[]{:S(2)}, u32[]{:S(2)}) collective-permute-start(bf16[2,64,8192]{2,1,0:T(8,128)(2,1)} %get-tuple-element.50), channel_id=1, source_target_pairs={{0,1},{1,2},{2,3},{3,0},{4,5},{5,6},{6,7},{7,4},{8,9},{9,10},{10,1... | collective-permute-start | bytes 6291464 | tf_op jit(solution)/shard_map/ppermute | solution.py:148
  346.8 2.8 copy-start.5
  346.8 91.5 %collective-permute-start.21 = (bf16[2,64,8192]{2,1,0:T(8,128)(2,1)}, bf16[2,64,8192]{2,1,0:T(8,128)(2,1)}, u32[]{:S(2)}, u32[]{:S(2)}) collective-permute-start(bf16[2,64,8192]{2,1,0:T(8,128)(2,1)} %get-tuple-element.49), channel_id=1, source_target_pairs={{0,3},{1,0},{2,1},{3,2},{4,7},{5,4},{6,5},{7,6},{8,11},{9,8},{10,9... | collective-permute-start | bytes 6291464 | tf_op jit(solution)/shard_map/ppermute | solution.py:148
  348.3 1.3 copy-start.6
  370.1 111.6 %collective-permute-start.10 = (bf16[2,64,8192]{2,1,0:T(8,128)(2,1)}, bf16[2,64,8192]{2,1,0:T(8,128)(2,1)S(1)}, u32[]{:S(2)}, u32[]{:S(2)}) collective-permute-start(bf16[2,64,8192]{2,1,0:T(8,128)(2,1)} %get-tuple-element.28), channel_id=1, source_target_pairs={{0,1},{1,2},{2,3},{3,0},{4,5},{5,6},{6,7},{7,4},{8,9},{9,10},{10,1... | collective-permute-start | bytes 6291464 | tf_op jit(solution)/shard_map/ppermute | solution.py:148
  412.4 114.2 %collective-permute-start.34 = (bf16[2,1024,512]{2,1,0:T(8,128)(2,1)}, bf16[2,1024,512]{2,1,0:T(8,128)(2,1)}, u32[]{:S(2)}, u32[]{:S(2)}) collective-permute-start(bf16[2,1024,512]{2,1,0:T(8,128)(2,1)} %get-tuple-element.34), channel_id=1, source_target_pairs={{0,1},{1,2},{2,3},{3,0},{4,5},{5,6},{6,7},{7,4},{8,9},{9,10},{10,1... | collective-permute-start | bytes 6291464 | tf_op jit(solution)/shard_map/ppermute | solution.py:148
  413.3 113.4 %collective-permute-start.37 = (bf16[2,1024,512]{2,1,0:T(8,128)(2,1)}, bf16[2,1024,512]{2,1,0:T(8,128)(2,1)}, u32[]{:S(2)}, u32[]{:S(2)}) collective-permute-start(bf16[2,1024,512]{2,1,0:T(8,128)(2,1)} %get-tuple-element.35), channel_id=1, source_target_pairs={{0,3},{1,0},{2,1},{3,2},{4,7},{5,4},{6,5},{7,6},{8,11},{9,8},{10,9... | collective-permute-start | bytes 6291464 | tf_op jit(solution)/shard_map/ppermute | solution.py:148
  436.8 93.1 %collective-permute-start.13 = (bf16[2,64,8192]{2,1,0:T(8,128)(2,1)}, bf16[2,64,8192]{2,1,0:T(8,128)(2,1)}, u32[]{:S(2)}, u32[]{:S(2)}) collective-permute-start(bf16[2,64,8192]{2,1,0:T(8,128)(2,1)} %get-tuple-element.29), channel_id=1, source_target_pairs={{0,3},{1,0},{2,1},{3,2},{4,7},{5,4},{6,5},{7,6},{8,11},{9,8},{10,9... | collective-permute-start | bytes 6291464 | tf_op jit(solution)/shard_map/ppermute | solution.py:148
  458.7 112.8 %collective-permute-start.22 = (bf16[2,64,8192]{2,1,0:T(8,128)(2,1)}, bf16[2,64,8192]{2,1,0:T(8,128)(2,1)S(1)}, u32[]{:S(2)}, u32[]{:S(2)}) collective-permute-start(bf16[2,64,8192]{2,1,0:T(8,128)(2,1)} %get-tuple-element.31), channel_id=1, source_target_pairs={{0,1},{1,2},{2,3},{3,0},{4,5},{5,6},{6,7},{7,4},{8,9},{9,10},{10,1... | collective-permute-start | bytes 6291464 | tf_op jit(solution)/shard_map/ppermute | solution.py:148
  481.6 361.5 %copy-start.2 = (bf16[2,64,8192]{2,1,0:T(8,128)(2,1)}, bf16[2,64,8192]{2,1,0:T(8,128)(2,1)S(1)}, u32[]{:S(2)}) copy-start(bf16[2,64,8192]{2,1,0:T(8,128)(2,1)S(1)} %collective-permute-done.10.up_ref) | copy-start | bytes 6291460
  481.6 91.3 %collective-permute-start.25 = (bf16[2,64,8192]{2,1,0:T(8,128)(2,1)}, bf16[2,64,8192]{2,1,0:T(8,128)(2,1)S(1)}, u32[]{:S(2)}, u32[]{:S(2)}) collective-permute-start(bf16[2,64,8192]{2,1,0:T(8,128)(2,1)} %get-tuple-element.32), channel_id=1, source_target_pairs={{0,3},{1,0},{2,1},{3,2},{4,7},{5,4},{6,5},{7,6},{8,11},{9,8},{10,9... | collective-permute-start | bytes 6291464 | tf_op jit(solution)/shard_map/ppermute | solution.py:148
  526.7 89.8 %collective-permute-start.35 = (bf16[2,1024,512]{2,1,0:T(8,128)(2,1)}, bf16[2,1024,512]{2,1,0:T(8,128)(2,1)S(1)}, u32[]{:S(2)}, u32[]{:S(2)}) collective-permute-start(bf16[2,1024,512]{2,1,0:T(8,128)(2,1)} %collective-permute-done.34.up_ref), channel_id=1, source_target_pairs={{0,1},{1,2},{2,3},{3,0},{4,5},{5,6},{6,7},{7,4},{8,9},{9,10},{10,1... | collective-permute-start | bytes 6291464 | tf_op jit(solution)/shard_map/ppermute | solution.py:148
  526.7 91.3 %collective-permute-start.38 = (bf16[2,1024,512]{2,1,0:T(8,128)(2,1)}, bf16[2,1024,512]{2,1,0:T(8,128)(2,1)S(1)}, u32[]{:S(2)}, u32[]{:S(2)}) collective-permute-start(bf16[2,1024,512]{2,1,0:T(8,128)(2,1)} %collective-permute-done.37.down_ref), channel_id=1, source_target_pairs={{0,3},{1,0},{2,1},{3,2},{4,7},{5,4},{6,5},{7,6},{8,11},{9,8},{10,9... | collective-permute-start | bytes 6291464 | tf_op jit(solution)/shard_map/ppermute | solution.py:148
  529.9 131.6 %collective-permute-start.11 = (bf16[2,64,8192]{2,1,0:T(8,128)(2,1)S(1)}, bf16[2,64,8192]{2,1,0:T(8,128)(2,1)}, u32[]{:S(2)}, u32[]{:S(2)}) collective-permute-start(bf16[2,64,8192]{2,1,0:T(8,128)(2,1)S(1)} %collective-permute-done.10.up_ref), channel_id=1, source_target_pairs={{0,1},{1,2},{2,3},{3,0},{4,5},{5,6},{6,7},{7,4},{8,9},{9,10},{10,1... | collective-permute-start | bytes 6291464 | tf_op jit(solution)/shard_map/ppermute | solution.py:148
  571.5 181.9 %copy-start.3 = (bf16[2,64,8192]{2,1,0:T(8,128)(2,1)}, bf16[2,64,8192]{2,1,0:T(8,128)(2,1)S(1)}, u32[]{:S(2)}) copy-start(bf16[2,64,8192]{2,1,0:T(8,128)(2,1)S(1)} %collective-permute-done.22.up_ref) | copy-start | bytes 6291460
  571.5 91.5 %collective-permute-start.14 = (bf16[2,64,8192]{2,1,0:T(8,128)(2,1)}, bf16[2,64,8192]{2,1,0:T(8,128)(2,1)}, u32[]{:S(2)}, u32[]{:S(2)}) collective-permute-start(bf16[2,64,8192]{2,1,0:T(8,128)(2,1)} %collective-permute-done.13.down_ref), channel_id=1, source_target_pairs={{0,3},{1,0},{2,1},{3,2},{4,7},{5,4},{6,5},{7,6},{8,11},{9,8},{10,9... | collective-permute-start | bytes 6291464 | tf_op jit(solution)/shard_map/ppermute | solution.py:148
  573.0 266.4 %copy-start.4 = (bf16[2,64,8192]{2,1,0:T(8,128)(2,1)}, bf16[2,64,8192]{2,1,0:T(8,128)(2,1)S(1)}, u32[]{:S(2)}) copy-start(bf16[2,64,8192]{2,1,0:T(8,128)(2,1)S(1)} %collective-permute-done.25.down_ref) | copy-start | bytes 6291460
  573.0 133.5 %collective-permute-start.23 = (bf16[2,64,8192]{2,1,0:T(8,128)(2,1)S(1)}, bf16[2,64,8192]{2,1,0:T(8,128)(2,1)}, u32[]{:S(2)}, u32[]{:S(2)}) collective-permute-start(bf16[2,64,8192]{2,1,0:T(8,128)(2,1)S(1)} %collective-permute-done.22.up_ref), channel_id=1, source_target_pairs={{0,1},{1,2},{2,3},{3,0},{4,5},{5,6},{6,7},{7,4},{8,9},{9,10},{10,1... | collective-permute-start | bytes 6291464 | tf_op jit(solution)/shard_map/ppermute | solution.py:148
  616.4 93.3 %copy-start = (bf16[2,1024,512]{2,1,0:T(8,128)(2,1)}, bf16[2,1024,512]{2,1,0:T(8,128)(2,1)S(1)}, u32[]{:S(2)}) copy-start(bf16[2,1024,512]{2,1,0:T(8,128)(2,1)S(1)} %collective-permute-done.35.up_ref) | copy-start | bytes 6291460
  616.4 90.0 %collective-permute-start.26 = (bf16[2,64,8192]{2,1,0:T(8,128)(2,1)S(1)}, bf16[2,64,8192]{2,1,0:T(8,128)(2,1)}, u32[]{:S(2)}, u32[]{:S(2)}) collective-permute-start(bf16[2,64,8192]{2,1,0:T(8,128)(2,1)S(1)} %collective-permute-done.25.down_ref), channel_id=1, source_target_pairs={{0,3},{1,0},{2,1},{3,2},{4,7},{5,4},{6,5},{7,6},{8,11},{9,8},{10,9... | collective-permute-start | bytes 6291464 | tf_op jit(solution)/shard_map/ppermute | solution.py:148
  618.0 134.8 %copy-start.1 = (bf16[2,1024,512]{2,1,0:T(8,128)(2,1)}, bf16[2,1024,512]{2,1,0:T(8,128)(2,1)S(1)}, u32[]{:S(2)}) copy-start(bf16[2,1024,512]{2,1,0:T(8,128)(2,1)S(1)} %collective-permute-done.38.down_ref) | copy-start | bytes 6291460
  618.0 114.1 %collective-permute-start.42 = (bf16[1,640,512]{2,1,0:T(8,128)(2,1)S(1)}, bf16[1,640,512]{2,1,0:T(8,128)(2,1)S(1)}, u32[]{:S(2)}, u32[]{:S(2)}) collective-permute-start(bf16[1,640,512]{2,1,0:T(8,128)(2,1)S(1)} %slice.36), channel_id=1, source_target_pairs={{0,1},{1,2},{2,3},{3,0},{4,5},{5,6},{6,7},{7,4},{8,9},{9,10},{10,1... | collective-permute-start | bytes 1966088 | tf_op jit(solution)/shard_map/ppermute | solution.py:148
  661.5 70.6 %collective-permute-start.43 = (bf16[1,640,512]{2,1,0:T(8,128)(2,1)S(1)}, bf16[1,640,512]{2,1,0:T(8,128)(2,1)S(1)}, u32[]{:S(2)}, u32[]{:S(2)}) collective-permute-start(bf16[1,640,512]{2,1,0:T(8,128)(2,1)S(1)} %slice.37), channel_id=1, source_target_pairs={{0,3},{1,0},{2,1},{3,2},{4,7},{5,4},{6,5},{7,6},{8,11},{9,8},{10,9... | collective-permute-start | bytes 1966088 | tf_op jit(solution)/shard_map/ppermute | solution.py:148
  663.0 60.2 %collective-permute-start.36 = (bf16[1,128,512]{2,1,0:T(8,128)(2,1)S(1)}, bf16[1,128,512]{2,1,0:T(8,128)(2,1)S(1)}, u32[]{:S(2)}, u32[]{:S(2)}) collective-permute-start(bf16[1,128,512]{2,1,0:T(8,128)(2,1)S(1)} %slice.32), channel_id=1, source_target_pairs={{0,1},{1,2},{2,3},{3,0},{4,5},{5,6},{6,7},{7,4},{8,9},{9,10},{10,1... | collective-permute-start | bytes 393224 | tf_op jit(solution)/shard_map/ppermute | solution.py:148
  706.4 22.4 %collective-permute-start.40 = (bf16[1,256,512]{2,1,0:T(8,128)(2,1)S(1)}, bf16[1,256,512]{2,1,0:T(8,128)(2,1)S(1)}, u32[]{:S(2)}, u32[]{:S(2)}) collective-permute-start(bf16[1,256,512]{2,1,0:T(8,128)(2,1)S(1)} %slice.34), channel_id=1, source_target_pairs={{0,1},{1,2},{2,3},{3,0},{4,5},{5,6},{6,7},{7,4},{8,9},{9,10},{10,1... | collective-permute-start | bytes 786440 | tf_op jit(solution)/shard_map/ppermute | solution.py:148
  706.4 22.4 %collective-permute-start.41 = (bf16[1,256,512]{2,1,0:T(8,128)(2,1)S(1)}, bf16[1,256,512]{2,1,0:T(8,128)(2,1)S(1)}, u32[]{:S(2)}, u32[]{:S(2)}) collective-permute-start(bf16[1,256,512]{2,1,0:T(8,128)(2,1)S(1)} %slice.35), channel_id=1, source_target_pairs={{0,3},{1,0},{2,1},{3,2},{4,7},{5,4},{6,5},{7,6},{8,11},{9,8},{10,9... | collective-permute-start | bytes 786440 | tf_op jit(solution)/shard_map/ppermute | solution.py:148
  723.2 28.1 %collective-permute-start.44 = (bf16[1,1024,512]{2,1,0:T(8,128)(2,1)S(1)}, bf16[1,1024,512]{2,1,0:T(8,128)(2,1)S(1)}, u32[]{:S(2)}, u32[]{:S(2)}) collective-permute-start(bf16[1,1024,512]{2,1,0:T(8,128)(2,1)S(1)} %slice.38), channel_id=1, source_target_pairs={{0,1},{1,2},{2,3},{3,0},{4,5},{5,6},{6,7},{7,4},{8,9},{9,10},{10,1... | collective-permute-start | bytes 3145736 | tf_op jit(solution)/shard_map/ppermute | solution.py:148
  728.8 140.6 %collective-permute-start.12 = (bf16[2,64,8192]{2,1,0:T(8,128)(2,1)}, bf16[2,64,8192]{2,1,0:T(8,128)(2,1)}, u32[]{:S(2)}, u32[]{:S(2)}) collective-permute-start(bf16[2,64,8192]{2,1,0:T(8,128)(2,1)} %collective-permute-done.11.up_ref), channel_id=1, source_target_pairs={{0,1},{1,2},{2,3},{3,0},{4,5},{5,6},{6,7},{7,4},{8,9},{9,10},{10,1... | collective-permute-start | bytes 6291464 | tf_op jit(solution)/shard_map/ppermute | solution.py:148
  728.8 140.6 %collective-permute-start.15 = (bf16[2,64,8192]{2,1,0:T(8,128)(2,1)}, bf16[2,64,8192]{2,1,0:T(8,128)(2,1)}, u32[]{:S(2)}, u32[]{:S(2)}) collective-permute-start(bf16[2,64,8192]{2,1,0:T(8,128)(2,1)} %collective-permute-done.14.down_ref), channel_id=1, source_target_pairs={{0,3},{1,0},{2,1},{3,2},{4,7},{5,4},{6,5},{7,6},{8,11},{9,8},{10,9... | collective-permute-start | bytes 6291464 | tf_op jit(solution)/shard_map/ppermute | solution.py:148
  732.0 114.4 %copy-start.10 = (bf16[1,640,512]{2,1,0:T(8,128)(2,1)}, bf16[1,640,512]{2,1,0:T(8,128)(2,1)S(1)}, u32[]{:S(2)}) copy-start(bf16[1,640,512]{2,1,0:T(8,128)(2,1)S(1)} %collective-permute-done.42.up_ref) | copy-start | bytes 1966084
  732.0 140.7 %collective-permute-start.24 = (bf16[2,64,8192]{2,1,0:T(8,128)(2,1)}, bf16[2,64,8192]{2,1,0:T(8,128)(2,1)}, u32[]{:S(2)}, u32[]{:S(2)}) collective-permute-start(bf16[2,64,8192]{2,1,0:T(8,128)(2,1)} %collective-permute-done.23.up_ref), channel_id=1, source_target_pairs={{0,1},{1,2},{2,3},{3,0},{4,5},{5,6},{6,7},{7,4},{8,9},{9,10},{10,1... | collective-permute-start | bytes 6291464 | tf_op jit(solution)/shard_map/ppermute | solution.py:148
  732.1 111.0 %copy-start.11 = (bf16[1,640,512]{2,1,0:T(8,128)(2,1)}, bf16[1,640,512]{2,1,0:T(8,128)(2,1)S(1)}, u32[]{:S(2)}) copy-start(bf16[1,640,512]{2,1,0:T(8,128)(2,1)S(1)} %collective-permute-done.43.down_ref) | copy-start | bytes 1966084
  732.1 140.6 %collective-permute-start.27 = (bf16[2,64,8192]{2,1,0:T(8,128)(2,1)}, bf16[2,64,8192]{2,1,0:T(8,128)(2,1)}, u32[]{:S(2)}, u32[]{:S(2)}) collective-permute-start(bf16[2,64,8192]{2,1,0:T(8,128)(2,1)} %collective-permute-done.26.down_ref), channel_id=1, source_target_pairs={{0,3},{1,0},{2,1},{3,2},{4,7},{5,4},{6,5},{7,6},{8,11},{9,8},{10,9... | collective-permute-start | bytes 6291464 | tf_op jit(solution)/shard_map/ppermute | solution.py:148
  751.3 91.8 %copy-start.7 = (bf16[1,1024,512]{2,1,0:T(8,128)(2,1)}, bf16[1,1024,512]{2,1,0:T(8,128)(2,1)S(1)}, u32[]{:S(2)}) copy-start(bf16[1,1024,512]{2,1,0:T(8,128)(2,1)S(1)} %collective-permute-done.44.up_ref) | copy-start | bytes 3145732
  751.3 88.1 %collective-permute-start.45 = (bf16[1,1024,512]{2,1,0:T(8,128)(2,1)S(1)}, bf16[1,1024,512]{2,1,0:T(8,128)(2,1)S(1)}, u32[]{:S(2)}, u32[]{:S(2)}) collective-permute-start(bf16[1,1024,512]{2,1,0:T(8,128)(2,1)S(1)} %slice.39), channel_id=1, source_target_pairs={{0,3},{1,0},{2,1},{3,2},{4,7},{5,4},{6,5},{7,6},{8,11},{9,8},{10,9... | collective-permute-start | bytes 3145736 | tf_op jit(solution)/shard_map/ppermute | solution.py:148
  839.4 3.7 copy-start.8
  839.4 29.2 %collective-permute-start.39 = (bf16[1,128,512]{2,1,0:T(8,128)(2,1)}, bf16[1,128,512]{2,1,0:T(8,128)(2,1)S(1)}, u32[]{:S(2)}, u32[]{:S(2)}) collective-permute-start(bf16[1,128,512]{2,1,0:T(8,128)(2,1)} %slice.33), channel_id=1, source_target_pairs={{0,3},{1,0},{2,1},{3,2},{4,7},{5,4},{6,5},{7,6},{8,11},{9,8},{10,9... | collective-permute-start | bytes 393224 | tf_op jit(solution)/shard_map/ppermute | solution.py:148

commit v3 on v2

--- a/solution.py
+++ b/solution.py
@@ -96,7 +96,7 @@
     )(*pieces, whole)
 
 
-def first_slice(axis, hops, term, half, rows):
+def first_slice(axis, hops, term, half, row, rows):
     columns = term.shape[3]
     count = term.shape[2] // (2 * half)
 
@@ -105,7 +105,7 @@
         copies = []
         for side, ref in enumerate((up_ref, down_ref)):
             block = lax.rem(me + (hops, count - hops)[side], count)
-            start = pl.multiple_of((block * 2 + side) * half, half)
+            start = pl.multiple_of((block * 2 + side) * half, half) + row
             copies.append(pltpu.make_async_copy(term_ref.at[0, 0, pl.ds(start, rows)], ref.at[0], sems.at[side]))
         for copy in copies:
             copy.start()
@@ -175,8 +175,8 @@
         for k in order:
             if k == order[0]:
                 half, parts = m[k].shape[1] // 2, small_first(m[k])
-                sent = [send(first_slice("dp", n - 1, terms[k], half, parts[0][3]))]
-                sent += [send(own(terms[k], m[k], n - 1, part)) for part in parts[1:]]
+                sent = [send(first_slice("dp", n - 1, terms[k], half, row, rows)) for _, _, row, rows in parts[:2]]
+                sent += [send(own(terms[k], m[k], n - 1, part)) for part in parts[2:]]
                 moving[k] = [join(parts) for parts in zip(*sent, strict=True)]
             else:
                 moving[k] = send(own(terms[k], m[k], n - 1, all_of_it(m[k])[0]))

time: 876 us -> 875 us (level)
  no operation moved by 1% of the time
where the time goes in v3:
time: 875 us
  waiting for transfers between devices  673 us (77%)
  Pallas kernels  96.8 us (11%)
  starting transfers between devices  58.1 us (7%)
  other arithmetic  30.2 us (3%)
  local copies, waits for them, and re-layouts  15.5 us (2%)
    ppermute x46, waiting for transfers between devices, send(): moved.append(lax.ppermute(p, 'dp', way))  673 us
    pallas_call x3, Pallas kernels, update(): pl.pallas_call(kernel, out_shape=(jax.ShapeDtypeStruct(w.shape, jnp.bfloa...  61.6 us
    ppermute x46, starting transfers between devices, send(): moved.append(lax.ppermute(p, 'dp', way))  58.1 us
    pallas_call x12, Pallas kernels, place(): pl.pallas_call(kernel, out_shape=jax.ShapeDtypeStruct(whole.shape, whole....  32.8 us
    convert_element_type x6, other arithmetic, add(): return (a.astype(jnp.float32) + b.astype(jnp.float32)).astype(jnp.bfloat16)  30.2 us
  transfers between devices with their start and end apart: 46, of which 19 were waited for; matrix products, arithmetic and copies ran while one was open for 5% of the time, Pallas kernels for 11%

profile of v3, /device:TPU:112, one launch (start us, length us, event | category | flops | bytes accessed | tf_op | source)
XLA Modules:
  0.0 874.7 jit_solution(3706434989211318571)
XLA Ops:
  2.0 2.4 collective-permute-start.1
  5.5 1.7 collective-permute-start
  7.2 1.6 collective-permute-start.5
  8.8 3.0 dynamic-slice_bitcast_fusion.4
  12.3 4.5 dynamic-slice_bitcast_fusion
  18.1 11.9 %collective-permute-done = bf16[1,16,8192]{2,1,0:T(8,128)(2,1)S(1)} collective-permute-done((bf16[1,16,8192]{2,1,0:T(8,128)(2,1)S(1)}, bf16[1,16,8192]{2,1,0:T(8,128)(2,1)S(1)}, u32[]{:S(2)}, u32[]{:S(2)}) %collective-permute-start) | collective-permute-done | bytes 262176 | tf_op jit(solution)/shard_map/ppermute | solution.py:148
  30.0 2.0 collective-permute-start.31
  34.0 3.9 dynamic-slice_bitcast_fusion.2
  37.9 77.7 %collective-permute-done.6 = bf16[1,48,8192]{2,1,0:T(8,128)(2,1)S(1)} collective-permute-done((bf16[1,48,8192]{2,1,0:T(8,128)(2,1)S(1)}, bf16[1,48,8192]{2,1,0:T(8,128)(2,1)S(1)}, u32[]{:S(2)}, u32[]{:S(2)}) %collective-permute-start.6) | collective-permute-done | bytes 786464 | tf_op jit(solution)/shard_map/ppermute | solution.py:148
  116.5 2.7 collective-permute-start.19
  119.2 4.0 fusion.9
  123.3 3.2 collective-permute-start.8
  126.5 4.7 fusion.1
  131.4 34.3 %collective-permute-done.16 = bf16[2,64,8192]{2,1,0:T(8,128)(2,1)} collective-permute-done((bf16[2,64,8192]{2,1,0:T(8,128)(2,1)}, bf16[2,64,8192]{2,1,0:T(8,128)(2,1)}, u32[]{:S(2)}, u32[]{:S(2)}) %collective-permute-start.16) | collective-permute-done | bytes 2097184 | tf_op jit(solution)/shard_map/ppermute | solution.py:148
  165.7 1.4 collective-permute-start.32
  167.1 5.0 fusion.5
  172.8 37.7 %collective-permute-done.3 = bf16[2,64,8192]{2,1,0:T(8,128)(2,1)S(1)} collective-permute-done((bf16[2,64,8192]{2,1,0:T(8,128)(2,1)S(1)}, bf16[2,64,8192]{2,1,0:T(8,128)(2,1)S(1)}, u32[]{:S(2)}, u32[]{:S(2)}) %collective-permute-start.3) | collective-permute-done | bytes 2097184 | tf_op jit(solution)/shard_map/ppermute | solution.py:148
  210.5 1.4 collective-permute-start.20
  212.0 5.1 fusion.8
  217.6 37.8 %collective-permute-done.29 = bf16[2,1024,512]{2,1,0:T(8,128)(2,1)S(1)} collective-permute-done((bf16[2,1024,512]{2,1,0:T(8,128)(2,1)S(1)}, bf16[2,1024,512]{2,1,0:T(8,128)(2,1)S(1)}, u32[]{:S(2)}, u32[]{:S(2)}) %collective-permute-start.29) | collective-permute-done | bytes 2097184 | tf_op jit(solution)/shard_map/ppermute | solution.py:148
  255.5 1.4 collective-permute-start.9
  256.9 5.5 fusion
  263.0 37.4 %collective-permute-done.17 = bf16[2,64,8192]{2,1,0:T(8,128)(2,1)S(1)} collective-permute-done((bf16[2,64,8192]{2,1,0:T(8,128)(2,1)S(1)}, bf16[2,64,8192]{2,1,0:T(8,128)(2,1)S(1)}, u32[]{:S(2)}, u32[]{:S(2)}) %collective-permute-start.17) | collective-permute-done | bytes 2097184 | tf_op jit(solution)/shard_map/ppermute | solution.py:148
  300.4 1.4 collective-permute-start.33
  301.8 5.8 fusion.4
  308.2 37.1 %collective-permute-done.4.up_ref = bf16[2,64,8192]{2,1,0:T(8,128)(2,1)S(1)} collective-permute-done((bf16[2,64,8192]{2,1,0:T(8,128)(2,1)}, bf16[2,64,8192]{2,1,0:T(8,128)(2,1)S(1)}, u32[]{:S(2)}, u32[]{:S(2)}) %collective-permute-start.4) | collective-permute-done | bytes 2097184 | tf_op jit(solution)/shard_map/ppermute | solution.py:148
  345.3 1.4 collective-permute-start.21
  348.1 20.5 %update.3 = (bf16[2,512,8192]{2,1,0:T(8,128)(2,1)}, f32[2,128,8192]{2,1,0:T(8,128)}, f32[2,128,8192]{2,1,0:T(8,128)}, bf16[2,64,8192]{2,1,0:T(8,128)(2,1)}, bf16[2,64,8192]{2,1,0:T(8,128)(2,1)}) custom-call(s32[1]{0:T(128)} %bitcast.me_ref, bf16[2,64,8192]{2,1,0:T(8,128)(2,1)} %copy-done.5, bf16[2,64,8192]{2,1,0:T(8,128)(2,1)} %copy-done.6, ...), custom_call_target="tpu_custom_call" | custom-call | flops 41943040 | bytes 54525952 | tf_op jit(solution)/shard_map/update/pallas_call | solution.py:42
  369.2 21.2 %collective-permute-done.30.up_ref = bf16[2,1024,512]{2,1,0:T(8,128)(2,1)} collective-permute-done((bf16[2,1024,512]{2,1,0:T(8,128)(2,1)}, bf16[2,1024,512]{2,1,0:T(8,128)(2,1)}, u32[]{:S(2)}, u32[]{:S(2)}) %collective-permute-start.30) | collective-permute-done | bytes 2097184 | tf_op jit(solution)/shard_map/ppermute | solution.py:148
  390.4 20.6 %update.5 = (bf16[2,8192,512]{2,1,0:T(8,128)(2,1)}, f32[2,2048,512]{2,1,0:T(8,128)}, f32[2,2048,512]{2,1,0:T(8,128)}, bf16[2,1024,512]{2,1,0:T(8,128)(2,1)}, bf16[2,1024,512]{2,1,0:T(8,128)(2,1)}) custom-call(s32[1]{0:T(128)} %bitcast.me_ref, bf16[2,1024,512]{2,1,0:T(8,128)(2,1)} %collective-permute-done.30.up_ref, ...), custom_call_target="tpu_custom_call" | custom-call | flops 41943040 | bytes 54525952 | tf_op jit(solution)/shard_map/update/pallas_call | solution.py:42
  411.6 2.8 collective-permute-start.37
  414.4 20.9 %collective-permute-done.18.up_ref = bf16[2,64,8192]{2,1,0:T(8,128)(2,1)} collective-permute-done((bf16[2,64,8192]{2,1,0:T(8,128)(2,1)}, bf16[2,64,8192]{2,1,0:T(8,128)(2,1)}, u32[]{:S(2)}, u32[]{:S(2)}) %collective-permute-start.18) | collective-permute-done | bytes 2097184 | tf_op jit(solution)/shard_map/ppermute | solution.py:148
  435.3 1.4 collective-permute-start.13
  436.8 20.5 %update.4 = (bf16[2,512,8192]{2,1,0:T(8,128)(2,1)}, f32[2,128,8192]{2,1,0:T(8,128)}, f32[2,128,8192]{2,1,0:T(8,128)}, bf16[2,64,8192]{2,1,0:T(8,128)(2,1)}, bf16[2,64,8192]{2,1,0:T(8,128)(2,1)}) custom-call(s32[1]{0:T(128)} %bitcast.me_ref, bf16[2,64,8192]{2,1,0:T(8,128)(2,1)} %collective-permute-done.18.up_ref, ...), custom_call_target="tpu_custom_call" | custom-call | flops 41943040 | bytes 54525952 | tf_op jit(solution)/shard_map/update/pallas_call | solution.py:42
  457.8 22.3 %collective-permute-done.10.up_ref = bf16[2,64,8192]{2,1,0:T(8,128)(2,1)S(1)} collective-permute-done((bf16[2,64,8192]{2,1,0:T(8,128)(2,1)}, bf16[2,64,8192]{2,1,0:T(8,128)(2,1)S(1)}, u32[]{:S(2)}, u32[]{:S(2)}) %collective-permute-start.10) | collective-permute-done | bytes 2097184 | tf_op jit(solution)/shard_map/ppermute | solution.py:148
  480.2 1.4 collective-permute-start.25
  481.6 43.6 %collective-permute-done.34.up_ref = bf16[2,1024,512]{2,1,0:T(8,128)(2,1)} collective-permute-done((bf16[2,1024,512]{2,1,0:T(8,128)(2,1)}, bf16[2,1024,512]{2,1,0:T(8,128)(2,1)}, u32[]{:S(2)}, u32[]{:S(2)}) %collective-permute-start.34) | collective-permute-done | bytes 2097184 | tf_op jit(solution)/shard_map/ppermute | solution.py:148
  525.2 3.2 collective-permute-start.38
  528.5 41.6 %collective-permute-done.22.up_ref = bf16[2,64,8192]{2,1,0:T(8,128)(2,1)S(1)} collective-permute-done((bf16[2,64,8192]{2,1,0:T(8,128)(2,1)}, bf16[2,64,8192]{2,1,0:T(8,128)(2,1)S(1)}, u32[]{:S(2)}, u32[]{:S(2)}) %collective-permute-start.22) | collective-permute-done | bytes 2097184 | tf_op jit(solution)/shard_map/ppermute | solution.py:148
  570.0 1.4 collective-permute-start.14
  572.1 42.9 %collective-permute-done.35.up_ref = bf16[2,1024,512]{2,1,0:T(8,128)(2,1)S(1)} collective-permute-done((bf16[2,1024,512]{2,1,0:T(8,128)(2,1)}, bf16[2,1024,512]{2,1,0:T(8,128)(2,1)S(1)}, u32[]{:S(2)}, u32[]{:S(2)}) %collective-permute-start.35) | collective-permute-done | bytes 2097184 | tf_op jit(solution)/shard_map/ppermute | solution.py:148
  615.0 1.4 collective-permute-start.26
  617.2 42.8 %collective-permute-done.11.up_ref = bf16[2,64,8192]{2,1,0:T(8,128)(2,1)} collective-permute-done((bf16[2,64,8192]{2,1,0:T(8,128)(2,1)S(1)}, bf16[2,64,8192]{2,1,0:T(8,128)(2,1)}, u32[]{:S(2)}, u32[]{:S(2)}) %collective-permute-start.11) | collective-permute-done | bytes 2097184 | tf_op jit(solution)/shard_map/ppermute | solution.py:148
  660.0 1.4 collective-permute-start.43
  662.2 42.8 %collective-permute-done.23.up_ref = bf16[2,64,8192]{2,1,0:T(8,128)(2,1)} collective-permute-done((bf16[2,64,8192]{2,1,0:T(8,128)(2,1)S(1)}, bf16[2,64,8192]{2,1,0:T(8,128)(2,1)}, u32[]{:S(2)}, u32[]{:S(2)}) %collective-permute-start.23) | collective-permute-done | bytes 2097184 | tf_op jit(solution)/shard_map/ppermute | solution.py:148
  705.0 3.3 collective-permute-start.41
  708.4 13.3 %collective-permute-done.36.up_ref = bf16[1,128,512]{2,1,0:T(8,128)(2,1)S(1)} collective-permute-done((bf16[1,128,512]{2,1,0:T(8,128)(2,1)S(1)}, bf16[1,128,512]{2,1,0:T(8,128)(2,1)S(1)}, u32[]{:S(2)}, u32[]{:S(2)}) %collective-permute-start.36) | collective-permute-done | bytes 131104 | tf_op jit(solution)/shard_map/ppermute | solution.py:148
  721.7 5.6 collective-permute-done.40.up_ref
  727.3 3.2 collective-permute-start.15
  730.6 3.2 collective-permute-start.27
  733.9 15.9 %collective-permute-done.44.up_ref = bf16[1,1024,512]{2,1,0:T(8,128)(2,1)S(1)} collective-permute-done((bf16[1,1024,512]{2,1,0:T(8,128)(2,1)S(1)}, bf16[1,1024,512]{2,1,0:T(8,128)(2,1)S(1)}, u32[]{:S(2)}, u32[]{:S(2)}) %collective-permute-start.44) | collective-permute-done | bytes 1048608 | tf_op jit(solution)/shard_map/ppermute | solution.py:148
  749.8 1.4 collective-permute-start.45
  751.9 86.0 %collective-permute-done.45.down_ref = bf16[1,1024,512]{2,1,0:T(8,128)(2,1)S(1)} collective-permute-done((bf16[1,1024,512]{2,1,0:T(8,128)(2,1)S(1)}, bf16[1,1024,512]{2,1,0:T(8,128)(2,1)S(1)}, u32[]{:S(2)}, u32[]{:S(2)}) %collective-permute-start.45) | collective-permute-done | bytes 1048608 | tf_op jit(solution)/shard_map/ppermute | solution.py:148
  837.9 3.7 collective-permute-start.39
  841.6 3.3 place.12.whole_ref
  845.0 3.3 place.18.whole_ref
  848.3 3.3 place.15.whole_ref
  851.6 3.3 place.13.whole_ref
  854.9 3.3 place.19.whole_ref
  858.2 2.6 place.20.whole_ref
  860.8 2.2 place.21.whole_ref
  863.0 3.3 place.16.whole_ref
  867.9 3.3 place.14
  871.3 3.3 place.17
  (88 shorter events, 17.3 us)
Async XLA Ops:
  2.0 30.7 %collective-permute-start.1 = (bf16[1,48,8192]{2,1,0:T(8,128)(2,1)S(1)}, bf16[1,48,8192]{2,1,0:T(8,128)(2,1)S(1)}, u32[]{:S(2)}, u32[]{:S(2)}) collective-permute-start(bf16[1,48,8192]{2,1,0:T(8,128)(2,1)S(1)} %get-tuple-element.29), channel_id=1, source_target_pairs={{0,1},{1,2},{2,3},{3,0},{4,5},{5,6},{6,7},{7,4},{8,9},{9,10},{10,1... | collective-permute-start | bytes 2359304 | tf_op jit(solution)/shard_map/ppermute | solution.py:148
  5.5 24.5 %collective-permute-start = (bf16[1,16,8192]{2,1,0:T(8,128)(2,1)S(1)}, bf16[1,16,8192]{2,1,0:T(8,128)(2,1)S(1)}, u32[]{:S(2)}, u32[]{:S(2)}) collective-permute-start(bf16[1,16,8192]{2,1,0:T(8,128)(2,1)S(1)} %get-tuple-element.28), channel_id=1, source_target_pairs={{0,1},{1,2},{2,3},{3,0},{4,5},{5,6},{6,7},{7,4},{8,9},{9,10},{10,1... | collective-permute-start | bytes 786440 | tf_op jit(solution)/shard_map/ppermute | solution.py:148
  7.2 24.8 %collective-permute-start.5 = (bf16[1,16,8192]{2,1,0:T(8,128)(2,1)S(1)}, bf16[1,16,8192]{2,1,0:T(8,128)(2,1)S(1)}, u32[]{:S(2)}, u32[]{:S(2)}) collective-permute-start(bf16[1,16,8192]{2,1,0:T(8,128)(2,1)S(1)} %get-tuple-element.30), channel_id=1, source_target_pairs={{0,3},{1,0},{2,1},{3,2},{4,7},{5,4},{6,5},{7,6},{8,11},{9,8},{10,9... | collective-permute-start | bytes 786440 | tf_op jit(solution)/shard_map/ppermute | solution.py:148
  11.9 103.8 %collective-permute-start.2 = (bf16[1,64,8192]{2,1,0:T(8,128)(2,1)}, bf16[1,64,8192]{2,1,0:T(8,128)(2,1)}, u32[]{:S(2)}, u32[]{:S(2)}) collective-permute-start(bf16[1,64,8192]{2,1,0:T(8,128)(2,1)} %get-tuple-element.64), channel_id=1, source_target_pairs={{0,1},{1,2},{2,3},{3,0},{4,5},{5,6},{6,7},{7,4},{8,9},{9,10},{10,1... | collective-permute-start | bytes 3145736 | tf_op jit(solution)/shard_map/ppermute | solution.py:148
  16.8 106.5 %collective-permute-start.28 = (bf16[2,1024,512]{2,1,0:T(8,128)(2,1)}, bf16[2,1024,512]{2,1,0:T(8,128)(2,1)}, u32[]{:S(2)}, u32[]{:S(2)}) collective-permute-start(bf16[2,1024,512]{2,1,0:T(8,128)(2,1)} %get-tuple-element.52), channel_id=1, source_target_pairs={{0,1},{1,2},{2,3},{3,0},{4,5},{5,6},{6,7},{7,4},{8,9},{9,10},{10,1... | collective-permute-start | bytes 6291464 | tf_op jit(solution)/shard_map/ppermute | solution.py:148
  30.0 96.5 %collective-permute-start.31 = (bf16[2,1024,512]{2,1,0:T(8,128)(2,1)}, bf16[2,1024,512]{2,1,0:T(8,128)(2,1)}, u32[]{:S(2)}, u32[]{:S(2)}) collective-permute-start(bf16[2,1024,512]{2,1,0:T(8,128)(2,1)} %get-tuple-element.51), channel_id=1, source_target_pairs={{0,3},{1,0},{2,1},{3,2},{4,7},{5,4},{6,5},{7,6},{8,11},{9,8},{10,9... | collective-permute-start | bytes 6291464 | tf_op jit(solution)/shard_map/ppermute | solution.py:148
  32.0 87.1 %collective-permute-start.7 = (bf16[1,64,8192]{2,1,0:T(8,128)(2,1)}, bf16[1,64,8192]{2,1,0:T(8,128)(2,1)}, u32[]{:S(2)}, u32[]{:S(2)}) collective-permute-start(bf16[1,64,8192]{2,1,0:T(8,128)(2,1)} %get-tuple-element.63), channel_id=1, source_target_pairs={{0,3},{1,0},{2,1},{3,2},{4,7},{5,4},{6,5},{7,6},{8,11},{9,8},{10,9... | collective-permute-start | bytes 3145736 | tf_op jit(solution)/shard_map/ppermute | solution.py:148
  32.7 0.9 copy-start.9
  33.6 82.0 %collective-permute-start.6 = (bf16[1,48,8192]{2,1,0:T(8,128)(2,1)S(1)}, bf16[1,48,8192]{2,1,0:T(8,128)(2,1)S(1)}, u32[]{:S(2)}, u32[]{:S(2)}) collective-permute-start(bf16[1,48,8192]{2,1,0:T(8,128)(2,1)S(1)} %get-tuple-element.31), channel_id=1, source_target_pairs={{0,3},{1,0},{2,1},{3,2},{4,7},{5,4},{6,5},{7,6},{8,11},{9,8},{10,9... | collective-permute-start | bytes 2359304 | tf_op jit(solution)/shard_map/ppermute | solution.py:148
  115.6 0.9 copy-start.10
  115.6 50.0 %collective-permute-start.16 = (bf16[2,64,8192]{2,1,0:T(8,128)(2,1)}, bf16[2,64,8192]{2,1,0:T(8,128)(2,1)}, u32[]{:S(2)}, u32[]{:S(2)}) collective-permute-start(bf16[2,64,8192]{2,1,0:T(8,128)(2,1)} %get-tuple-element.58), channel_id=1, source_target_pairs={{0,1},{1,2},{2,3},{3,0},{4,5},{5,6},{6,7},{7,4},{8,9},{9,10},{10,1... | collective-permute-start | bytes 6291464 | tf_op jit(solution)/shard_map/ppermute | solution.py:148
  116.5 50.6 %collective-permute-start.19 = (bf16[2,64,8192]{2,1,0:T(8,128)(2,1)S(1)}, bf16[2,64,8192]{2,1,0:T(8,128)(2,1)}, u32[]{:S(2)}, u32[]{:S(2)}) collective-permute-start(bf16[2,64,8192]{2,1,0:T(8,128)(2,1)S(1)} %get-tuple-element.57), channel_id=1, source_target_pairs={{0,3},{1,0},{2,1},{3,2},{4,7},{5,4},{6,5},{7,6},{8,11},{9,8},{10,9... | collective-permute-start | bytes 6291464 | tf_op jit(solution)/shard_map/ppermute | solution.py:148
  123.2 87.3 %collective-permute-start.3 = (bf16[2,64,8192]{2,1,0:T(8,128)(2,1)S(1)}, bf16[2,64,8192]{2,1,0:T(8,128)(2,1)S(1)}, u32[]{:S(2)}, u32[]{:S(2)}) collective-permute-start(bf16[2,64,8192]{2,1,0:T(8,128)(2,1)S(1)} %get-tuple-element.62), channel_id=1, source_target_pairs={{0,1},{1,2},{2,3},{3,0},{4,5},{5,6},{6,7},{7,4},{8,9},{9,10},{10,1... | collective-permute-start | bytes 6291464 | tf_op jit(solution)/shard_map/ppermute | solution.py:148
  123.3 88.6 %collective-permute-start.8 = (bf16[2,64,8192]{2,1,0:T(8,128)(2,1)S(1)}, bf16[2,64,8192]{2,1,0:T(8,128)(2,1)S(1)}, u32[]{:S(2)}, u32[]{:S(2)}) collective-permute-start(bf16[2,64,8192]{2,1,0:T(8,128)(2,1)S(1)} %get-tuple-element.61), channel_id=1, source_target_pairs={{0,3},{1,0},{2,1},{3,2},{4,7},{5,4},{6,5},{7,6},{8,11},{9,8},{10,9... | collective-permute-start | bytes 6291464 | tf_op jit(solution)/shard_map/ppermute | solution.py:148
  131.3 124.2 %collective-permute-start.29 = (bf16[2,1024,512]{2,1,0:T(8,128)(2,1)S(1)}, bf16[2,1024,512]{2,1,0:T(8,128)(2,1)S(1)}, u32[]{:S(2)}, u32[]{:S(2)}) collective-permute-start(bf16[2,1024,512]{2,1,0:T(8,128)(2,1)S(1)} %get-tuple-element.50), channel_id=1, source_target_pairs={{0,1},{1,2},{2,3},{3,0},{4,5},{5,6},{6,7},{7,4},{8,9},{9,10},{10,1... | collective-permute-start | bytes 6291464 | tf_op jit(solution)/shard_map/ppermute | solution.py:148
  165.7 91.2 %collective-permute-start.32 = (bf16[2,1024,512]{2,1,0:T(8,128)(2,1)S(1)}, bf16[2,1024,512]{2,1,0:T(8,128)(2,1)S(1)}, u32[]{:S(2)}, u32[]{:S(2)}) collective-permute-start(bf16[2,1024,512]{2,1,0:T(8,128)(2,1)S(1)} %get-tuple-element.49), channel_id=1, source_target_pairs={{0,3},{1,0},{2,1},{3,2},{4,7},{5,4},{6,5},{7,6},{8,11},{9,8},{10,9... | collective-permute-start | bytes 6291464 | tf_op jit(solution)/shard_map/ppermute | solution.py:148
  172.2 128.2 %collective-permute-start.17 = (bf16[2,64,8192]{2,1,0:T(8,128)(2,1)S(1)}, bf16[2,64,8192]{2,1,0:T(8,128)(2,1)S(1)}, u32[]{:S(2)}, u32[]{:S(2)}) collective-permute-start(bf16[2,64,8192]{2,1,0:T(8,128)(2,1)S(1)} %get-tuple-element.56), channel_id=1, source_target_pairs={{0,1},{1,2},{2,3},{3,0},{4,5},{5,6},{6,7},{7,4},{8,9},{9,10},{10,1... | collective-permute-start | bytes 6291464 | tf_op jit(solution)/shard_map/ppermute | solution.py:148
  210.5 91.3 %collective-permute-start.20 = (bf16[2,64,8192]{2,1,0:T(8,128)(2,1)S(1)}, bf16[2,64,8192]{2,1,0:T(8,128)(2,1)S(1)}, u32[]{:S(2)}, u32[]{:S(2)}) collective-permute-start(bf16[2,64,8192]{2,1,0:T(8,128)(2,1)S(1)} %get-tuple-element.55), channel_id=1, source_target_pairs={{0,3},{1,0},{2,1},{3,2},{4,7},{5,4},{6,5},{7,6},{8,11},{9,8},{10,9... | collective-permute-start | bytes 6291464 | tf_op jit(solution)/shard_map/ppermute | solution.py:148
  217.1 128.3 %collective-permute-start.4 = (bf16[2,64,8192]{2,1,0:T(8,128)(2,1)}, bf16[2,64,8192]{2,1,0:T(8,128)(2,1)S(1)}, u32[]{:S(2)}, u32[]{:S(2)}) collective-permute-start(bf16[2,64,8192]{2,1,0:T(8,128)(2,1)} %get-tuple-element.60), channel_id=1, source_target_pairs={{0,1},{1,2},{2,3},{3,0},{4,5},{5,6},{6,7},{7,4},{8,9},{9,10},{10,1... | collective-permute-start | bytes 6291464 | tf_op jit(solution)/shard_map/ppermute | solution.py:148
  255.5 91.3 %collective-permute-start.9 = (bf16[2,64,8192]{2,1,0:T(8,128)(2,1)S(1)}, bf16[2,64,8192]{2,1,0:T(8,128)(2,1)S(1)}, u32[]{:S(2)}, u32[]{:S(2)}) collective-permute-start(bf16[2,64,8192]{2,1,0:T(8,128)(2,1)S(1)} %get-tuple-element.59), channel_id=1, source_target_pairs={{0,3},{1,0},{2,1},{3,2},{4,7},{5,4},{6,5},{7,6},{8,11},{9,8},{10,9... | collective-permute-start | bytes 6291464 | tf_op jit(solution)/shard_map/ppermute | solution.py:148
  262.4 128.0 %collective-permute-start.30 = (bf16[2,1024,512]{2,1,0:T(8,128)(2,1)}, bf16[2,1024,512]{2,1,0:T(8,128)(2,1)}, u32[]{:S(2)}, u32[]{:S(2)}) collective-permute-start(bf16[2,1024,512]{2,1,0:T(8,128)(2,1)} %get-tuple-element.48), channel_id=1, source_target_pairs={{0,1},{1,2},{2,3},{3,0},{4,5},{5,6},{6,7},{7,4},{8,9},{9,10},{10,1... | collective-permute-start | bytes 6291464 | tf_op jit(solution)/shard_map/ppermute | solution.py:148
  300.4 90.0 %collective-permute-start.33 = (bf16[2,1024,512]{2,1,0:T(8,128)(2,1)}, bf16[2,1024,512]{2,1,0:T(8,128)(2,1)}, u32[]{:S(2)}, u32[]{:S(2)}) collective-permute-start(bf16[2,1024,512]{2,1,0:T(8,128)(2,1)} %get-tuple-element.47), channel_id=1, source_target_pairs={{0,3},{1,0},{2,1},{3,2},{4,7},{5,4},{6,5},{7,6},{8,11},{9,8},{10,9... | collective-permute-start | bytes 6291464 | tf_op jit(solution)/shard_map/ppermute | solution.py:148
  307.6 127.7 %collective-permute-start.18 = (bf16[2,64,8192]{2,1,0:T(8,128)(2,1)}, bf16[2,64,8192]{2,1,0:T(8,128)(2,1)}, u32[]{:S(2)}, u32[]{:S(2)}) collective-permute-start(bf16[2,64,8192]{2,1,0:T(8,128)(2,1)} %get-tuple-element.54), channel_id=1, source_target_pairs={{0,1},{1,2},{2,3},{3,0},{4,5},{5,6},{6,7},{7,4},{8,9},{9,10},{10,1... | collective-permute-start | bytes 6291464 | tf_op jit(solution)/shard_map/ppermute | solution.py:148
  345.3 2.8 copy-start.5
  345.3 91.4 %collective-permute-start.21 = (bf16[2,64,8192]{2,1,0:T(8,128)(2,1)}, bf16[2,64,8192]{2,1,0:T(8,128)(2,1)}, u32[]{:S(2)}, u32[]{:S(2)}) collective-permute-start(bf16[2,64,8192]{2,1,0:T(8,128)(2,1)} %get-tuple-element.53), channel_id=1, source_target_pairs={{0,3},{1,0},{2,1},{3,2},{4,7},{5,4},{6,5},{7,6},{8,11},{9,8},{10,9... | collective-permute-start | bytes 6291464 | tf_op jit(solution)/shard_map/ppermute | solution.py:148
  346.8 1.3 copy-start.6
  368.6 111.6 %collective-permute-start.10 = (bf16[2,64,8192]{2,1,0:T(8,128)(2,1)}, bf16[2,64,8192]{2,1,0:T(8,128)(2,1)S(1)}, u32[]{:S(2)}, u32[]{:S(2)}) collective-permute-start(bf16[2,64,8192]{2,1,0:T(8,128)(2,1)} %get-tuple-element.32), channel_id=1, source_target_pairs={{0,1},{1,2},{2,3},{3,0},{4,5},{5,6},{6,7},{7,4},{8,9},{9,10},{10,1... | collective-permute-start | bytes 6291464 | tf_op jit(solution)/shard_map/ppermute | solution.py:148
  411.0 114.2 %collective-permute-start.34 = (bf16[2,1024,512]{2,1,0:T(8,128)(2,1)}, bf16[2,1024,512]{2,1,0:T(8,128)(2,1)}, u32[]{:S(2)}, u32[]{:S(2)}) collective-permute-start(bf16[2,1024,512]{2,1,0:T(8,128)(2,1)} %get-tuple-element.38), channel_id=1, source_target_pairs={{0,1},{1,2},{2,3},{3,0},{4,5},{5,6},{6,7},{7,4},{8,9},{9,10},{10,1... | collective-permute-start | bytes 6291464 | tf_op jit(solution)/shard_map/ppermute | solution.py:148
  411.6 113.6 %collective-permute-start.37 = (bf16[2,1024,512]{2,1,0:T(8,128)(2,1)}, bf16[2,1024,512]{2,1,0:T(8,128)(2,1)}, u32[]{:S(2)}, u32[]{:S(2)}) collective-permute-start(bf16[2,1024,512]{2,1,0:T(8,128)(2,1)} %get-tuple-element.39), channel_id=1, source_target_pairs={{0,3},{1,0},{2,1},{3,2},{4,7},{5,4},{6,5},{7,6},{8,11},{9,8},{10,9... | collective-permute-start | bytes 6291464 | tf_op jit(solution)/shard_map/ppermute | solution.py:148
  435.3 93.1 %collective-permute-start.13 = (bf16[2,64,8192]{2,1,0:T(8,128)(2,1)}, bf16[2,64,8192]{2,1,0:T(8,128)(2,1)}, u32[]{:S(2)}, u32[]{:S(2)}) collective-permute-start(bf16[2,64,8192]{2,1,0:T(8,128)(2,1)} %get-tuple-element.33), channel_id=1, source_target_pairs={{0,3},{1,0},{2,1},{3,2},{4,7},{5,4},{6,5},{7,6},{8,11},{9,8},{10,9... | collective-permute-start | bytes 6291464 | tf_op jit(solution)/shard_map/ppermute | solution.py:148
  457.3 112.8 %collective-permute-start.22 = (bf16[2,64,8192]{2,1,0:T(8,128)(2,1)}, bf16[2,64,8192]{2,1,0:T(8,128)(2,1)S(1)}, u32[]{:S(2)}, u32[]{:S(2)}) collective-permute-start(bf16[2,64,8192]{2,1,0:T(8,128)(2,1)} %get-tuple-element.35), channel_id=1, source_target_pairs={{0,1},{1,2},{2,3},{3,0},{4,5},{5,6},{6,7},{7,4},{8,9},{9,10},{10,1... | collective-permute-start | bytes 6291464 | tf_op jit(solution)/shard_map/ppermute | solution.py:148
  480.2 361.5 %copy-start.2 = (bf16[2,64,8192]{2,1,0:T(8,128)(2,1)}, bf16[2,64,8192]{2,1,0:T(8,128)(2,1)S(1)}, u32[]{:S(2)}) copy-start(bf16[2,64,8192]{2,1,0:T(8,128)(2,1)S(1)} %collective-permute-done.10.up_ref) | copy-start | bytes 6291460
  480.2 91.3 %collective-permute-start.25 = (bf16[2,64,8192]{2,1,0:T(8,128)(2,1)}, bf16[2,64,8192]{2,1,0:T(8,128)(2,1)S(1)}, u32[]{:S(2)}, u32[]{:S(2)}) collective-permute-start(bf16[2,64,8192]{2,1,0:T(8,128)(2,1)} %get-tuple-element.36), channel_id=1, source_target_pairs={{0,3},{1,0},{2,1},{3,2},{4,7},{5,4},{6,5},{7,6},{8,11},{9,8},{10,9... | collective-permute-start | bytes 6291464 | tf_op jit(solution)/shard_map/ppermute | solution.py:148
  525.2 89.8 %collective-permute-start.35 = (bf16[2,1024,512]{2,1,0:T(8,128)(2,1)}, bf16[2,1024,512]{2,1,0:T(8,128)(2,1)S(1)}, u32[]{:S(2)}, u32[]{:S(2)}) collective-permute-start(bf16[2,1024,512]{2,1,0:T(8,128)(2,1)} %collective-permute-done.34.up_ref), channel_id=1, source_target_pairs={{0,1},{1,2},{2,3},{3,0},{4,5},{5,6},{6,7},{7,4},{8,9},{9,10},{10,1... | collective-permute-start | bytes 6291464 | tf_op jit(solution)/shard_map/ppermute | solution.py:148
  525.2 91.3 %collective-permute-start.38 = (bf16[2,1024,512]{2,1,0:T(8,128)(2,1)}, bf16[2,1024,512]{2,1,0:T(8,128)(2,1)S(1)}, u32[]{:S(2)}, u32[]{:S(2)}) collective-permute-start(bf16[2,1024,512]{2,1,0:T(8,128)(2,1)} %collective-permute-done.37.down_ref), channel_id=1, source_target_pairs={{0,3},{1,0},{2,1},{3,2},{4,7},{5,4},{6,5},{7,6},{8,11},{9,8},{10,9... | collective-permute-start | bytes 6291464 | tf_op jit(solution)/shard_map/ppermute | solution.py:148
  528.5 131.6 %collective-permute-start.11 = (bf16[2,64,8192]{2,1,0:T(8,128)(2,1)S(1)}, bf16[2,64,8192]{2,1,0:T(8,128)(2,1)}, u32[]{:S(2)}, u32[]{:S(2)}) collective-permute-start(bf16[2,64,8192]{2,1,0:T(8,128)(2,1)S(1)} %collective-permute-done.10.up_ref), channel_id=1, source_target_pairs={{0,1},{1,2},{2,3},{3,0},{4,5},{5,6},{6,7},{7,4},{8,9},{9,10},{10,1... | collective-permute-start | bytes 6291464 | tf_op jit(solution)/shard_map/ppermute | solution.py:148
  570.0 181.9 %copy-start.3 = (bf16[2,64,8192]{2,1,0:T(8,128)(2,1)}, bf16[2,64,8192]{2,1,0:T(8,128)(2,1)S(1)}, u32[]{:S(2)}) copy-start(bf16[2,64,8192]{2,1,0:T(8,128)(2,1)S(1)} %collective-permute-done.22.up_ref) | copy-start | bytes 6291460
  570.0 91.5 %collective-permute-start.14 = (bf16[2,64,8192]{2,1,0:T(8,128)(2,1)}, bf16[2,64,8192]{2,1,0:T(8,128)(2,1)}, u32[]{:S(2)}, u32[]{:S(2)}) collective-permute-start(bf16[2,64,8192]{2,1,0:T(8,128)(2,1)} %collective-permute-done.13.down_ref), channel_id=1, source_target_pairs={{0,3},{1,0},{2,1},{3,2},{4,7},{5,4},{6,5},{7,6},{8,11},{9,8},{10,9... | collective-permute-start | bytes 6291464 | tf_op jit(solution)/shard_map/ppermute | solution.py:148
  571.5 266.4 %copy-start.4 = (bf16[2,64,8192]{2,1,0:T(8,128)(2,1)}, bf16[2,64,8192]{2,1,0:T(8,128)(2,1)S(1)}, u32[]{:S(2)}) copy-start(bf16[2,64,8192]{2,1,0:T(8,128)(2,1)S(1)} %collective-permute-done.25.down_ref) | copy-start | bytes 6291460
  571.5 133.5 %collective-permute-start.23 = (bf16[2,64,8192]{2,1,0:T(8,128)(2,1)S(1)}, bf16[2,64,8192]{2,1,0:T(8,128)(2,1)}, u32[]{:S(2)}, u32[]{:S(2)}) collective-permute-start(bf16[2,64,8192]{2,1,0:T(8,128)(2,1)S(1)} %collective-permute-done.22.up_ref), channel_id=1, source_target_pairs={{0,1},{1,2},{2,3},{3,0},{4,5},{5,6},{6,7},{7,4},{8,9},{9,10},{10,1... | collective-permute-start | bytes 6291464 | tf_op jit(solution)/shard_map/ppermute | solution.py:148
  615.0 93.4 %copy-start = (bf16[2,1024,512]{2,1,0:T(8,128)(2,1)}, bf16[2,1024,512]{2,1,0:T(8,128)(2,1)S(1)}, u32[]{:S(2)}) copy-start(bf16[2,1024,512]{2,1,0:T(8,128)(2,1)S(1)} %collective-permute-done.35.up_ref) | copy-start | bytes 6291460
  615.0 90.0 %collective-permute-start.26 = (bf16[2,64,8192]{2,1,0:T(8,128)(2,1)S(1)}, bf16[2,64,8192]{2,1,0:T(8,128)(2,1)}, u32[]{:S(2)}, u32[]{:S(2)}) collective-permute-start(bf16[2,64,8192]{2,1,0:T(8,128)(2,1)S(1)} %collective-permute-done.25.down_ref), channel_id=1, source_target_pairs={{0,3},{1,0},{2,1},{3,2},{4,7},{5,4},{6,5},{7,6},{8,11},{9,8},{10,9... | collective-permute-start | bytes 6291464 | tf_op jit(solution)/shard_map/ppermute | solution.py:148
  616.5 134.8 %copy-start.1 = (bf16[2,1024,512]{2,1,0:T(8,128)(2,1)}, bf16[2,1024,512]{2,1,0:T(8,128)(2,1)S(1)}, u32[]{:S(2)}) copy-start(bf16[2,1024,512]{2,1,0:T(8,128)(2,1)S(1)} %collective-permute-done.38.down_ref) | copy-start | bytes 6291460
  616.5 114.1 %collective-permute-start.42 = (bf16[1,640,512]{2,1,0:T(8,128)(2,1)S(1)}, bf16[1,640,512]{2,1,0:T(8,128)(2,1)S(1)}, u32[]{:S(2)}, u32[]{:S(2)}) collective-permute-start(bf16[1,640,512]{2,1,0:T(8,128)(2,1)S(1)} %slice.36), channel_id=1, source_target_pairs={{0,1},{1,2},{2,3},{3,0},{4,5},{5,6},{6,7},{7,4},{8,9},{9,10},{10,1... | collective-permute-start | bytes 1966088 | tf_op jit(solution)/shard_map/ppermute | solution.py:148
  660.0 70.6 %collective-permute-start.43 = (bf16[1,640,512]{2,1,0:T(8,128)(2,1)S(1)}, bf16[1,640,512]{2,1,0:T(8,128)(2,1)S(1)}, u32[]{:S(2)}, u32[]{:S(2)}) collective-permute-start(bf16[1,640,512]{2,1,0:T(8,128)(2,1)S(1)} %slice.37), channel_id=1, source_target_pairs={{0,3},{1,0},{2,1},{3,2},{4,7},{5,4},{6,5},{7,6},{8,11},{9,8},{10,9... | collective-permute-start | bytes 1966088 | tf_op jit(solution)/shard_map/ppermute | solution.py:148
  661.5 60.2 %collective-permute-start.36 = (bf16[1,128,512]{2,1,0:T(8,128)(2,1)S(1)}, bf16[1,128,512]{2,1,0:T(8,128)(2,1)S(1)}, u32[]{:S(2)}, u32[]{:S(2)}) collective-permute-start(bf16[1,128,512]{2,1,0:T(8,128)(2,1)S(1)} %slice.32), channel_id=1, source_target_pairs={{0,1},{1,2},{2,3},{3,0},{4,5},{5,6},{6,7},{7,4},{8,9},{9,10},{10,1... | collective-permute-start | bytes 393224 | tf_op jit(solution)/shard_map/ppermute | solution.py:148
  705.0 22.4 %collective-permute-start.40 = (bf16[1,256,512]{2,1,0:T(8,128)(2,1)S(1)}, bf16[1,256,512]{2,1,0:T(8,128)(2,1)S(1)}, u32[]{:S(2)}, u32[]{:S(2)}) collective-permute-start(bf16[1,256,512]{2,1,0:T(8,128)(2,1)S(1)} %slice.34), channel_id=1, source_target_pairs={{0,1},{1,2},{2,3},{3,0},{4,5},{5,6},{6,7},{7,4},{8,9},{9,10},{10,1... | collective-permute-start | bytes 786440 | tf_op jit(solution)/shard_map/ppermute | solution.py:148
  705.0 22.4 %collective-permute-start.41 = (bf16[1,256,512]{2,1,0:T(8,128)(2,1)S(1)}, bf16[1,256,512]{2,1,0:T(8,128)(2,1)S(1)}, u32[]{:S(2)}, u32[]{:S(2)}) collective-permute-start(bf16[1,256,512]{2,1,0:T(8,128)(2,1)S(1)} %slice.35), channel_id=1, source_target_pairs={{0,3},{1,0},{2,1},{3,2},{4,7},{5,4},{6,5},{7,6},{8,11},{9,8},{10,9... | collective-permute-start | bytes 786440 | tf_op jit(solution)/shard_map/ppermute | solution.py:148
  721.7 28.1 %collective-permute-start.44 = (bf16[1,1024,512]{2,1,0:T(8,128)(2,1)S(1)}, bf16[1,1024,512]{2,1,0:T(8,128)(2,1)S(1)}, u32[]{:S(2)}, u32[]{:S(2)}) collective-permute-start(bf16[1,1024,512]{2,1,0:T(8,128)(2,1)S(1)} %slice.38), channel_id=1, source_target_pairs={{0,1},{1,2},{2,3},{3,0},{4,5},{5,6},{6,7},{7,4},{8,9},{9,10},{10,1... | collective-permute-start | bytes 3145736 | tf_op jit(solution)/shard_map/ppermute | solution.py:148
  727.3 140.6 %collective-permute-start.12 = (bf16[2,64,8192]{2,1,0:T(8,128)(2,1)}, bf16[2,64,8192]{2,1,0:T(8,128)(2,1)}, u32[]{:S(2)}, u32[]{:S(2)}) collective-permute-start(bf16[2,64,8192]{2,1,0:T(8,128)(2,1)} %collective-permute-done.11.up_ref), channel_id=1, source_target_pairs={{0,1},{1,2},{2,3},{3,0},{4,5},{5,6},{6,7},{7,4},{8,9},{9,10},{10,1... | collective-permute-start | bytes 6291464 | tf_op jit(solution)/shard_map/ppermute | solution.py:148
  727.3 140.6 %collective-permute-start.15 = (bf16[2,64,8192]{2,1,0:T(8,128)(2,1)}, bf16[2,64,8192]{2,1,0:T(8,128)(2,1)}, u32[]{:S(2)}, u32[]{:S(2)}) collective-permute-start(bf16[2,64,8192]{2,1,0:T(8,128)(2,1)} %collective-permute-done.14.down_ref), channel_id=1, source_target_pairs={{0,3},{1,0},{2,1},{3,2},{4,7},{5,4},{6,5},{7,6},{8,11},{9,8},{10,9... | collective-permute-start | bytes 6291464 | tf_op jit(solution)/shard_map/ppermute | solution.py:148
  730.6 114.4 %copy-start.11 = (bf16[1,640,512]{2,1,0:T(8,128)(2,1)}, bf16[1,640,512]{2,1,0:T(8,128)(2,1)S(1)}, u32[]{:S(2)}) copy-start(bf16[1,640,512]{2,1,0:T(8,128)(2,1)S(1)} %collective-permute-done.42.up_ref) | copy-start | bytes 1966084
  730.6 140.7 %collective-permute-start.24 = (bf16[2,64,8192]{2,1,0:T(8,128)(2,1)}, bf16[2,64,8192]{2,1,0:T(8,128)(2,1)}, u32[]{:S(2)}, u32[]{:S(2)}) collective-permute-start(bf16[2,64,8192]{2,1,0:T(8,128)(2,1)} %collective-permute-done.23.up_ref), channel_id=1, source_target_pairs={{0,1},{1,2},{2,3},{3,0},{4,5},{5,6},{6,7},{7,4},{8,9},{9,10},{10,1... | collective-permute-start | bytes 6291464 | tf_op jit(solution)/shard_map/ppermute | solution.py:148
  730.6 111.0 %copy-start.12 = (bf16[1,640,512]{2,1,0:T(8,128)(2,1)}, bf16[1,640,512]{2,1,0:T(8,128)(2,1)S(1)}, u32[]{:S(2)}) copy-start(bf16[1,640,512]{2,1,0:T(8,128)(2,1)S(1)} %collective-permute-done.43.down_ref) | copy-start | bytes 1966084
  730.6 140.6 %collective-permute-start.27 = (bf16[2,64,8192]{2,1,0:T(8,128)(2,1)}, bf16[2,64,8192]{2,1,0:T(8,128)(2,1)}, u32[]{:S(2)}, u32[]{:S(2)}) collective-permute-start(bf16[2,64,8192]{2,1,0:T(8,128)(2,1)} %collective-permute-done.26.down_ref), channel_id=1, source_target_pairs={{0,3},{1,0},{2,1},{3,2},{4,7},{5,4},{6,5},{7,6},{8,11},{9,8},{10,9... | collective-permute-start | bytes 6291464 | tf_op jit(solution)/shard_map/ppermute | solution.py:148
  749.8 91.8 %copy-start.7 = (bf16[1,1024,512]{2,1,0:T(8,128)(2,1)}, bf16[1,1024,512]{2,1,0:T(8,128)(2,1)S(1)}, u32[]{:S(2)}) copy-start(bf16[1,1024,512]{2,1,0:T(8,128)(2,1)S(1)} %collective-permute-done.44.up_ref) | copy-start | bytes 3145732
  749.8 88.1 %collective-permute-start.45 = (bf16[1,1024,512]{2,1,0:T(8,128)(2,1)S(1)}, bf16[1,1024,512]{2,1,0:T(8,128)(2,1)S(1)}, u32[]{:S(2)}, u32[]{:S(2)}) collective-permute-start(bf16[1,1024,512]{2,1,0:T(8,128)(2,1)S(1)} %slice.39), channel_id=1, source_target_pairs={{0,3},{1,0},{2,1},{3,2},{4,7},{5,4},{6,5},{7,6},{8,11},{9,8},{10,9... | collective-permute-start | bytes 3145736 | tf_op jit(solution)/shard_map/ppermute | solution.py:148
  837.9 3.7 copy-start.8
  837.9 29.2 %collective-permute-start.39 = (bf16[1,128,512]{2,1,0:T(8,128)(2,1)}, bf16[1,128,512]{2,1,0:T(8,128)(2,1)S(1)}, u32[]{:S(2)}, u32[]{:S(2)}) collective-permute-start(bf16[1,128,512]{2,1,0:T(8,128)(2,1)} %slice.33), channel_id=1, source_target_pairs={{0,3},{1,0},{2,1},{3,2},{4,7},{5,4},{6,5},{7,6},{8,11},{9,8},{10,9... | collective-permute-start | bytes 393224 | tf_op jit(solution)/shard_map/ppermute | solution.py:148

commit v4 on v3

--- a/solution.py
+++ b/solution.py
@@ -160,9 +160,8 @@
 
         def small_last(like):
             layers, half = like.shape[0], like.shape[1] // 2
-            quarter = half // 4
-            small = quarter // 2
-            ends = [(layers - 1, 1, 0, half - 3 * small), (layers - 1, 1, half - 3 * small, 2 * small), (layers - 1, 1, half - small, small)]
+            small = half // 64
+            ends = [(layers - 1, 1, 0, half - 20 * small), (layers - 1, 1, half - 20 * small, 15 * small), (layers - 1, 1, half - 5 * small, 5 * small)]
             return [(0, layers - 1, 0, half)] * (layers > 1) + ends
 
         def join(parts):

time: 875 us -> 874 us (level)
  transfers between devices with their start and end apart: 46 -> 46, of which waited for: 19 -> 18; matrix products, arithmetic and copies ran while one was open for 5% -> 5% of each run, Pallas kernels for 11% -> 11%
where the time goes in v4:
time: 874 us
  waiting for transfers between devices  675 us (77%)
  Pallas kernels  96.8 us (11%)
  starting transfers between devices  56.4 us (6%)
  other arithmetic  30.2 us (3%)
  local copies, waits for them, and re-layouts  14.8 us (2%)
    ppermute x46, waiting for transfers between devices, send(): moved.append(lax.ppermute(p, 'dp', way))  675 us
    pallas_call x3, Pallas kernels, update(): pl.pallas_call(kernel, out_shape=(jax.ShapeDtypeStruct(w.shape, jnp.bfloa...  61.6 us
    ppermute x46, starting transfers between devices, send(): moved.append(lax.ppermute(p, 'dp', way))  56.4 us
    pallas_call x12, Pallas kernels, place(): pl.pallas_call(kernel, out_shape=jax.ShapeDtypeStruct(whole.shape, whole....  32.8 us
    convert_element_type x6, other arithmetic, add(): return (a.astype(jnp.float32) + b.astype(jnp.float32)).astype(jnp.bfloat16)  30.2 us
  transfers between devices with their start and end apart: 46, of which 18 were waited for; matrix products, arithmetic and copies ran while one was open for 5% of the time, Pallas kernels for 11%

profile of v4, /device:TPU:112, one launch (start us, length us, event | category | flops | bytes accessed | tf_op | source)
XLA Modules:
  0.0 873.9 jit_solution(4342934047068430593)
XLA Ops:
  0.6 1.4 first_slice.3
  2.0 2.4 collective-permute-start.1
  5.5 1.7 collective-permute-start
  7.2 1.6 collective-permute-start.5
  8.8 3.0 dynamic-slice_bitcast_fusion.4
  12.3 4.5 dynamic-slice_bitcast_fusion
  16.8 1.3 collective-permute-start.28
  18.1 11.9 %collective-permute-done = bf16[1,16,8192]{2,1,0:T(8,128)(2,1)S(1)} collective-permute-done((bf16[1,16,8192]{2,1,0:T(8,128)(2,1)S(1)}, bf16[1,16,8192]{2,1,0:T(8,128)(2,1)S(1)}, u32[]{:S(2)}, u32[]{:S(2)}) %collective-permute-start) | collective-permute-done | bytes 262176 | tf_op jit(solution)/shard_map/ppermute | solution.py:148
  30.0 2.0 collective-permute-start.31
  34.0 3.9 dynamic-slice_bitcast_fusion.2
  37.9 77.7 %collective-permute-done.6 = bf16[1,48,8192]{2,1,0:T(8,128)(2,1)S(1)} collective-permute-done((bf16[1,48,8192]{2,1,0:T(8,128)(2,1)S(1)}, bf16[1,48,8192]{2,1,0:T(8,128)(2,1)S(1)}, u32[]{:S(2)}, u32[]{:S(2)}) %collective-permute-start.6) | collective-permute-done | bytes 786464 | tf_op jit(solution)/shard_map/ppermute | solution.py:148
  116.5 2.7 collective-permute-start.19
  119.2 4.0 fusion.9
  123.3 3.2 collective-permute-start.8
  126.5 4.7 fusion.1
  131.4 34.3 %collective-permute-done.16 = bf16[2,64,8192]{2,1,0:T(8,128)(2,1)} collective-permute-done((bf16[2,64,8192]{2,1,0:T(8,128)(2,1)}, bf16[2,64,8192]{2,1,0:T(8,128)(2,1)}, u32[]{:S(2)}, u32[]{:S(2)}) %collective-permute-start.16) | collective-permute-done | bytes 2097184 | tf_op jit(solution)/shard_map/ppermute | solution.py:148
  165.7 1.4 collective-permute-start.32
  167.1 5.0 fusion.5
  172.8 37.7 %collective-permute-done.3 = bf16[2,64,8192]{2,1,0:T(8,128)(2,1)S(1)} collective-permute-done((bf16[2,64,8192]{2,1,0:T(8,128)(2,1)S(1)}, bf16[2,64,8192]{2,1,0:T(8,128)(2,1)S(1)}, u32[]{:S(2)}, u32[]{:S(2)}) %collective-permute-start.3) | collective-permute-done | bytes 2097184 | tf_op jit(solution)/shard_map/ppermute | solution.py:148
  210.5 1.4 collective-permute-start.20
  212.0 5.1 fusion.8
  217.6 37.8 %collective-permute-done.29 = bf16[2,1024,512]{2,1,0:T(8,128)(2,1)S(1)} collective-permute-done((bf16[2,1024,512]{2,1,0:T(8,128)(2,1)S(1)}, bf16[2,1024,512]{2,1,0:T(8,128)(2,1)S(1)}, u32[]{:S(2)}, u32[]{:S(2)}) %collective-permute-start.29) | collective-permute-done | bytes 2097184 | tf_op jit(solution)/shard_map/ppermute | solution.py:148
  255.5 1.4 collective-permute-start.9
  256.9 5.5 fusion
  263.0 37.4 %collective-permute-done.17 = bf16[2,64,8192]{2,1,0:T(8,128)(2,1)S(1)} collective-permute-done((bf16[2,64,8192]{2,1,0:T(8,128)(2,1)S(1)}, bf16[2,64,8192]{2,1,0:T(8,128)(2,1)S(1)}, u32[]{:S(2)}, u32[]{:S(2)}) %collective-permute-start.17) | collective-permute-done | bytes 2097184 | tf_op jit(solution)/shard_map/ppermute | solution.py:148
  300.4 1.4 collective-permute-start.33
  301.8 5.8 fusion.4
  308.2 37.1 %collective-permute-done.4.up_ref = bf16[2,64,8192]{2,1,0:T(8,128)(2,1)S(1)} collective-permute-done((bf16[2,64,8192]{2,1,0:T(8,128)(2,1)}, bf16[2,64,8192]{2,1,0:T(8,128)(2,1)S(1)}, u32[]{:S(2)}, u32[]{:S(2)}) %collective-permute-start.4) | collective-permute-done | bytes 2097184 | tf_op jit(solution)/shard_map/ppermute | solution.py:148
  345.3 1.4 collective-permute-start.21
  348.1 20.5 %update.3 = (bf16[2,512,8192]{2,1,0:T(8,128)(2,1)}, f32[2,128,8192]{2,1,0:T(8,128)}, f32[2,128,8192]{2,1,0:T(8,128)}, bf16[2,64,8192]{2,1,0:T(8,128)(2,1)}, bf16[2,64,8192]{2,1,0:T(8,128)(2,1)}) custom-call(s32[1]{0:T(128)} %bitcast.me_ref, bf16[2,64,8192]{2,1,0:T(8,128)(2,1)} %copy-done.5, bf16[2,64,8192]{2,1,0:T(8,128)(2,1)} %copy-done.6, ...), custom_call_target="tpu_custom_call" | custom-call | flops 41943040 | bytes 54525952 | tf_op jit(solution)/shard_map/update/pallas_call | solution.py:42
  369.2 21.2 %collective-permute-done.30.up_ref = bf16[2,1024,512]{2,1,0:T(8,128)(2,1)} collective-permute-done((bf16[2,1024,512]{2,1,0:T(8,128)(2,1)}, bf16[2,1024,512]{2,1,0:T(8,128)(2,1)}, u32[]{:S(2)}, u32[]{:S(2)}) %collective-permute-start.30) | collective-permute-done | bytes 2097184 | tf_op jit(solution)/shard_map/ppermute | solution.py:148
  390.4 20.6 %update.5 = (bf16[2,8192,512]{2,1,0:T(8,128)(2,1)}, f32[2,2048,512]{2,1,0:T(8,128)}, f32[2,2048,512]{2,1,0:T(8,128)}, bf16[2,1024,512]{2,1,0:T(8,128)(2,1)}, bf16[2,1024,512]{2,1,0:T(8,128)(2,1)}) custom-call(s32[1]{0:T(128)} %bitcast.me_ref, bf16[2,1024,512]{2,1,0:T(8,128)(2,1)} %collective-permute-done.30.up_ref, ...), custom_call_target="tpu_custom_call" | custom-call | flops 41943040 | bytes 54525952 | tf_op jit(solution)/shard_map/update/pallas_call | solution.py:42
  411.6 2.8 collective-permute-start.37
  414.4 20.9 %collective-permute-done.18.up_ref = bf16[2,64,8192]{2,1,0:T(8,128)(2,1)} collective-permute-done((bf16[2,64,8192]{2,1,0:T(8,128)(2,1)}, bf16[2,64,8192]{2,1,0:T(8,128)(2,1)}, u32[]{:S(2)}, u32[]{:S(2)}) %collective-permute-start.18) | collective-permute-done | bytes 2097184 | tf_op jit(solution)/shard_map/ppermute | solution.py:148
  435.3 1.4 collective-permute-start.13
  436.8 20.5 %update.4 = (bf16[2,512,8192]{2,1,0:T(8,128)(2,1)}, f32[2,128,8192]{2,1,0:T(8,128)}, f32[2,128,8192]{2,1,0:T(8,128)}, bf16[2,64,8192]{2,1,0:T(8,128)(2,1)}, bf16[2,64,8192]{2,1,0:T(8,128)(2,1)}) custom-call(s32[1]{0:T(128)} %bitcast.me_ref, bf16[2,64,8192]{2,1,0:T(8,128)(2,1)} %collective-permute-done.18.up_ref, ...), custom_call_target="tpu_custom_call" | custom-call | flops 41943040 | bytes 54525952 | tf_op jit(solution)/shard_map/update/pallas_call | solution.py:42
  457.8 22.3 %collective-permute-done.10.up_ref = bf16[2,64,8192]{2,1,0:T(8,128)(2,1)S(1)} collective-permute-done((bf16[2,64,8192]{2,1,0:T(8,128)(2,1)}, bf16[2,64,8192]{2,1,0:T(8,128)(2,1)S(1)}, u32[]{:S(2)}, u32[]{:S(2)}) %collective-permute-start.10) | collective-permute-done | bytes 2097184 | tf_op jit(solution)/shard_map/ppermute | solution.py:148
  480.2 1.4 collective-permute-start.25
  481.6 43.6 %collective-permute-done.34.up_ref = bf16[2,1024,512]{2,1,0:T(8,128)(2,1)} collective-permute-done((bf16[2,1024,512]{2,1,0:T(8,128)(2,1)}, bf16[2,1024,512]{2,1,0:T(8,128)(2,1)}, u32[]{:S(2)}, u32[]{:S(2)}) %collective-permute-start.34) | collective-permute-done | bytes 2097184 | tf_op jit(solution)/shard_map/ppermute | solution.py:148
  525.2 3.2 collective-permute-start.38
  528.5 41.6 %collective-permute-done.22.up_ref = bf16[2,64,8192]{2,1,0:T(8,128)(2,1)S(1)} collective-permute-done((bf16[2,64,8192]{2,1,0:T(8,128)(2,1)}, bf16[2,64,8192]{2,1,0:T(8,128)(2,1)S(1)}, u32[]{:S(2)}, u32[]{:S(2)}) %collective-permute-start.22) | collective-permute-done | bytes 2097184 | tf_op jit(solution)/shard_map/ppermute | solution.py:148
  570.0 1.4 collective-permute-start.14
  572.1 42.9 %collective-permute-done.35.up_ref = bf16[2,1024,512]{2,1,0:T(8,128)(2,1)S(1)} collective-permute-done((bf16[2,1024,512]{2,1,0:T(8,128)(2,1)}, bf16[2,1024,512]{2,1,0:T(8,128)(2,1)S(1)}, u32[]{:S(2)}, u32[]{:S(2)}) %collective-permute-start.35) | collective-permute-done | bytes 2097184 | tf_op jit(solution)/shard_map/ppermute | solution.py:148
  615.0 1.4 collective-permute-start.26
  617.2 42.8 %collective-permute-done.11.up_ref = bf16[2,64,8192]{2,1,0:T(8,128)(2,1)} collective-permute-done((bf16[2,64,8192]{2,1,0:T(8,128)(2,1)S(1)}, bf16[2,64,8192]{2,1,0:T(8,128)(2,1)}, u32[]{:S(2)}, u32[]{:S(2)}) %collective-permute-start.11) | collective-permute-done | bytes 2097184 | tf_op jit(solution)/shard_map/ppermute | solution.py:148
  660.0 1.4 collective-permute-start.43
  662.2 42.8 %collective-permute-done.23.up_ref = bf16[2,64,8192]{2,1,0:T(8,128)(2,1)} collective-permute-done((bf16[2,64,8192]{2,1,0:T(8,128)(2,1)S(1)}, bf16[2,64,8192]{2,1,0:T(8,128)(2,1)}, u32[]{:S(2)}, u32[]{:S(2)}) %collective-permute-start.23) | collective-permute-done | bytes 2097184 | tf_op jit(solution)/shard_map/ppermute | solution.py:148
  705.0 1.4 collective-permute-start.41
  707.2 16.9 %collective-permute-done.36.up_ref = bf16[1,80,512]{2,1,0:T(8,128)(2,1)S(1)} collective-permute-done((bf16[1,80,512]{2,1,0:T(8,128)(2,1)S(1)}, bf16[1,80,512]{2,1,0:T(8,128)(2,1)S(1)}, u32[]{:S(2)}, u32[]{:S(2)}) %collective-permute-start.36) | collective-permute-done | bytes 81952 | tf_op jit(solution)/shard_map/ppermute | solution.py:148
  725.0 2.4 collective-permute-start.15
  727.6 3.0 collective-permute-start.27
  730.7 20.6 %collective-permute-done.44.up_ref = bf16[1,1024,512]{2,1,0:T(8,128)(2,1)S(1)} collective-permute-done((bf16[1,1024,512]{2,1,0:T(8,128)(2,1)S(1)}, bf16[1,1024,512]{2,1,0:T(8,128)(2,1)S(1)}, u32[]{:S(2)}, u32[]{:S(2)}) %collective-permute-start.44) | collective-permute-done | bytes 1048608 | tf_op jit(solution)/shard_map/ppermute | solution.py:148
  752.1 85.0 %collective-permute-done.45.down_ref = bf16[1,1024,512]{2,1,0:T(8,128)(2,1)S(1)} collective-permute-done((bf16[1,1024,512]{2,1,0:T(8,128)(2,1)S(1)}, bf16[1,1024,512]{2,1,0:T(8,128)(2,1)S(1)}, u32[]{:S(2)}, u32[]{:S(2)}) %collective-permute-start.45) | collective-permute-done | bytes 1048608 | tf_op jit(solution)/shard_map/ppermute | solution.py:148
  837.1 3.7 collective-permute-start.39
  840.8 3.3 place.12.whole_ref
  844.1 3.3 place.18.whole_ref
  847.4 3.3 place.15.whole_ref
  850.8 3.3 place.13.whole_ref
  854.1 3.3 place.19.whole_ref
  857.4 2.6 place.20.whole_ref
  860.0 2.2 place.21.whole_ref
  862.2 3.3 place.16.whole_ref
  867.1 3.3 place.14
  870.4 3.3 place.17
  (88 shorter events, 16.5 us)
Async XLA Ops:
  2.0 30.7 %collective-permute-start.1 = (bf16[1,48,8192]{2,1,0:T(8,128)(2,1)S(1)}, bf16[1,48,8192]{2,1,0:T(8,128)(2,1)S(1)}, u32[]{:S(2)}, u32[]{:S(2)}) collective-permute-start(bf16[1,48,8192]{2,1,0:T(8,128)(2,1)S(1)} %get-tuple-element.29), channel_id=1, source_target_pairs={{0,1},{1,2},{2,3},{3,0},{4,5},{5,6},{6,7},{7,4},{8,9},{9,10},{10,1... | collective-permute-start | bytes 2359304 | tf_op jit(solution)/shard_map/ppermute | solution.py:148
  5.5 24.5 %collective-permute-start = (bf16[1,16,8192]{2,1,0:T(8,128)(2,1)S(1)}, bf16[1,16,8192]{2,1,0:T(8,128)(2,1)S(1)}, u32[]{:S(2)}, u32[]{:S(2)}) collective-permute-start(bf16[1,16,8192]{2,1,0:T(8,128)(2,1)S(1)} %get-tuple-element.28), channel_id=1, source_target_pairs={{0,1},{1,2},{2,3},{3,0},{4,5},{5,6},{6,7},{7,4},{8,9},{9,10},{10,1... | collective-permute-start | bytes 786440 | tf_op jit(solution)/shard_map/ppermute | solution.py:148
  7.2 24.8 %collective-permute-start.5 = (bf16[1,16,8192]{2,1,0:T(8,128)(2,1)S(1)}, bf16[1,16,8192]{2,1,0:T(8,128)(2,1)S(1)}, u32[]{:S(2)}, u32[]{:S(2)}) collective-permute-start(bf16[1,16,8192]{2,1,0:T(8,128)(2,1)S(1)} %get-tuple-element.30), channel_id=1, source_target_pairs={{0,3},{1,0},{2,1},{3,2},{4,7},{5,4},{6,5},{7,6},{8,11},{9,8},{10,9... | collective-permute-start | bytes 786440 | tf_op jit(solution)/shard_map/ppermute | solution.py:148
  11.9 103.8 %collective-permute-start.2 = (bf16[1,64,8192]{2,1,0:T(8,128)(2,1)}, bf16[1,64,8192]{2,1,0:T(8,128)(2,1)}, u32[]{:S(2)}, u32[]{:S(2)}) collective-permute-start(bf16[1,64,8192]{2,1,0:T(8,128)(2,1)} %get-tuple-element.64), channel_id=1, source_target_pairs={{0,1},{1,2},{2,3},{3,0},{4,5},{5,6},{6,7},{7,4},{8,9},{9,10},{10,1... | collective-permute-start | bytes 3145736 | tf_op jit(solution)/shard_map/ppermute | solution.py:148
  16.8 106.5 %collective-permute-start.28 = (bf16[2,1024,512]{2,1,0:T(8,128)(2,1)}, bf16[2,1024,512]{2,1,0:T(8,128)(2,1)}, u32[]{:S(2)}, u32[]{:S(2)}) collective-permute-start(bf16[2,1024,512]{2,1,0:T(8,128)(2,1)} %get-tuple-element.52), channel_id=1, source_target_pairs={{0,1},{1,2},{2,3},{3,0},{4,5},{5,6},{6,7},{7,4},{8,9},{9,10},{10,1... | collective-permute-start | bytes 6291464 | tf_op jit(solution)/shard_map/ppermute | solution.py:148
  30.0 96.5 %collective-permute-start.31 = (bf16[2,1024,512]{2,1,0:T(8,128)(2,1)}, bf16[2,1024,512]{2,1,0:T(8,128)(2,1)}, u32[]{:S(2)}, u32[]{:S(2)}) collective-permute-start(bf16[2,1024,512]{2,1,0:T(8,128)(2,1)} %get-tuple-element.51), channel_id=1, source_target_pairs={{0,3},{1,0},{2,1},{3,2},{4,7},{5,4},{6,5},{7,6},{8,11},{9,8},{10,9... | collective-permute-start | bytes 6291464 | tf_op jit(solution)/shard_map/ppermute | solution.py:148
  32.0 87.1 %collective-permute-start.7 = (bf16[1,64,8192]{2,1,0:T(8,128)(2,1)}, bf16[1,64,8192]{2,1,0:T(8,128)(2,1)}, u32[]{:S(2)}, u32[]{:S(2)}) collective-permute-start(bf16[1,64,8192]{2,1,0:T(8,128)(2,1)} %get-tuple-element.63), channel_id=1, source_target_pairs={{0,3},{1,0},{2,1},{3,2},{4,7},{5,4},{6,5},{7,6},{8,11},{9,8},{10,9... | collective-permute-start | bytes 3145736 | tf_op jit(solution)/shard_map/ppermute | solution.py:148
  32.7 0.9 copy-start.9
  33.6 82.0 %collective-permute-start.6 = (bf16[1,48,8192]{2,1,0:T(8,128)(2,1)S(1)}, bf16[1,48,8192]{2,1,0:T(8,128)(2,1)S(1)}, u32[]{:S(2)}, u32[]{:S(2)}) collective-permute-start(bf16[1,48,8192]{2,1,0:T(8,128)(2,1)S(1)} %get-tuple-element.31), channel_id=1, source_target_pairs={{0,3},{1,0},{2,1},{3,2},{4,7},{5,4},{6,5},{7,6},{8,11},{9,8},{10,9... | collective-permute-start | bytes 2359304 | tf_op jit(solution)/shard_map/ppermute | solution.py:148
  115.6 0.9 copy-start.10
  115.6 50.0 %collective-permute-start.16 = (bf16[2,64,8192]{2,1,0:T(8,128)(2,1)}, bf16[2,64,8192]{2,1,0:T(8,128)(2,1)}, u32[]{:S(2)}, u32[]{:S(2)}) collective-permute-start(bf16[2,64,8192]{2,1,0:T(8,128)(2,1)} %get-tuple-element.58), channel_id=1, source_target_pairs={{0,1},{1,2},{2,3},{3,0},{4,5},{5,6},{6,7},{7,4},{8,9},{9,10},{10,1... | collective-permute-start | bytes 6291464 | tf_op jit(solution)/shard_map/ppermute | solution.py:148
  116.5 50.6 %collective-permute-start.19 = (bf16[2,64,8192]{2,1,0:T(8,128)(2,1)S(1)}, bf16[2,64,8192]{2,1,0:T(8,128)(2,1)}, u32[]{:S(2)}, u32[]{:S(2)}) collective-permute-start(bf16[2,64,8192]{2,1,0:T(8,128)(2,1)S(1)} %get-tuple-element.57), channel_id=1, source_target_pairs={{0,3},{1,0},{2,1},{3,2},{4,7},{5,4},{6,5},{7,6},{8,11},{9,8},{10,9... | collective-permute-start | bytes 6291464 | tf_op jit(solution)/shard_map/ppermute | solution.py:148
  123.2 87.3 %collective-permute-start.3 = (bf16[2,64,8192]{2,1,0:T(8,128)(2,1)S(1)}, bf16[2,64,8192]{2,1,0:T(8,128)(2,1)S(1)}, u32[]{:S(2)}, u32[]{:S(2)}) collective-permute-start(bf16[2,64,8192]{2,1,0:T(8,128)(2,1)S(1)} %get-tuple-element.62), channel_id=1, source_target_pairs={{0,1},{1,2},{2,3},{3,0},{4,5},{5,6},{6,7},{7,4},{8,9},{9,10},{10,1... | collective-permute-start | bytes 6291464 | tf_op jit(solution)/shard_map/ppermute | solution.py:148
  123.3 88.6 %collective-permute-start.8 = (bf16[2,64,8192]{2,1,0:T(8,128)(2,1)S(1)}, bf16[2,64,8192]{2,1,0:T(8,128)(2,1)S(1)}, u32[]{:S(2)}, u32[]{:S(2)}) collective-permute-start(bf16[2,64,8192]{2,1,0:T(8,128)(2,1)S(1)} %get-tuple-element.61), channel_id=1, source_target_pairs={{0,3},{1,0},{2,1},{3,2},{4,7},{5,4},{6,5},{7,6},{8,11},{9,8},{10,9... | collective-permute-start | bytes 6291464 | tf_op jit(solution)/shard_map/ppermute | solution.py:148
  131.3 124.2 %collective-permute-start.29 = (bf16[2,1024,512]{2,1,0:T(8,128)(2,1)S(1)}, bf16[2,1024,512]{2,1,0:T(8,128)(2,1)S(1)}, u32[]{:S(2)}, u32[]{:S(2)}) collective-permute-start(bf16[2,1024,512]{2,1,0:T(8,128)(2,1)S(1)} %get-tuple-element.50), channel_id=1, source_target_pairs={{0,1},{1,2},{2,3},{3,0},{4,5},{5,6},{6,7},{7,4},{8,9},{9,10},{10,1... | collective-permute-start | bytes 6291464 | tf_op jit(solution)/shard_map/ppermute | solution.py:148
  165.7 91.2 %collective-permute-start.32 = (bf16[2,1024,512]{2,1,0:T(8,128)(2,1)S(1)}, bf16[2,1024,512]{2,1,0:T(8,128)(2,1)S(1)}, u32[]{:S(2)}, u32[]{:S(2)}) collective-permute-start(bf16[2,1024,512]{2,1,0:T(8,128)(2,1)S(1)} %get-tuple-element.49), channel_id=1, source_target_pairs={{0,3},{1,0},{2,1},{3,2},{4,7},{5,4},{6,5},{7,6},{8,11},{9,8},{10,9... | collective-permute-start | bytes 6291464 | tf_op jit(solution)/shard_map/ppermute | solution.py:148
  172.2 128.2 %collective-permute-start.17 = (bf16[2,64,8192]{2,1,0:T(8,128)(2,1)S(1)}, bf16[2,64,8192]{2,1,0:T(8,128)(2,1)S(1)}, u32[]{:S(2)}, u32[]{:S(2)}) collective-permute-start(bf16[2,64,8192]{2,1,0:T(8,128)(2,1)S(1)} %get-tuple-element.56), channel_id=1, source_target_pairs={{0,1},{1,2},{2,3},{3,0},{4,5},{5,6},{6,7},{7,4},{8,9},{9,10},{10,1... | collective-permute-start | bytes 6291464 | tf_op jit(solution)/shard_map/ppermute | solution.py:148
  210.5 91.3 %collective-permute-start.20 = (bf16[2,64,8192]{2,1,0:T(8,128)(2,1)S(1)}, bf16[2,64,8192]{2,1,0:T(8,128)(2,1)S(1)}, u32[]{:S(2)}, u32[]{:S(2)}) collective-permute-start(bf16[2,64,8192]{2,1,0:T(8,128)(2,1)S(1)} %get-tuple-element.55), channel_id=1, source_target_pairs={{0,3},{1,0},{2,1},{3,2},{4,7},{5,4},{6,5},{7,6},{8,11},{9,8},{10,9... | collective-permute-start | bytes 6291464 | tf_op jit(solution)/shard_map/ppermute | solution.py:148
  217.1 128.3 %collective-permute-start.4 = (bf16[2,64,8192]{2,1,0:T(8,128)(2,1)}, bf16[2,64,8192]{2,1,0:T(8,128)(2,1)S(1)}, u32[]{:S(2)}, u32[]{:S(2)}) collective-permute-start(bf16[2,64,8192]{2,1,0:T(8,128)(2,1)} %get-tuple-element.60), channel_id=1, source_target_pairs={{0,1},{1,2},{2,3},{3,0},{4,5},{5,6},{6,7},{7,4},{8,9},{9,10},{10,1... | collective-permute-start | bytes 6291464 | tf_op jit(solution)/shard_map/ppermute | solution.py:148
  255.5 91.3 %collective-permute-start.9 = (bf16[2,64,8192]{2,1,0:T(8,128)(2,1)S(1)}, bf16[2,64,8192]{2,1,0:T(8,128)(2,1)S(1)}, u32[]{:S(2)}, u32[]{:S(2)}) collective-permute-start(bf16[2,64,8192]{2,1,0:T(8,128)(2,1)S(1)} %get-tuple-element.59), channel_id=1, source_target_pairs={{0,3},{1,0},{2,1},{3,2},{4,7},{5,4},{6,5},{7,6},{8,11},{9,8},{10,9... | collective-permute-start | bytes 6291464 | tf_op jit(solution)/shard_map/ppermute | solution.py:148
  262.4 128.0 %collective-permute-start.30 = (bf16[2,1024,512]{2,1,0:T(8,128)(2,1)}, bf16[2,1024,512]{2,1,0:T(8,128)(2,1)}, u32[]{:S(2)}, u32[]{:S(2)}) collective-permute-start(bf16[2,1024,512]{2,1,0:T(8,128)(2,1)} %get-tuple-element.48), channel_id=1, source_target_pairs={{0,1},{1,2},{2,3},{3,0},{4,5},{5,6},{6,7},{7,4},{8,9},{9,10},{10,1... | collective-permute-start | bytes 6291464 | tf_op jit(solution)/shard_map/ppermute | solution.py:148
  300.4 90.0 %collective-permute-start.33 = (bf16[2,1024,512]{2,1,0:T(8,128)(2,1)}, bf16[2,1024,512]{2,1,0:T(8,128)(2,1)}, u32[]{:S(2)}, u32[]{:S(2)}) collective-permute-start(bf16[2,1024,512]{2,1,0:T(8,128)(2,1)} %get-tuple-element.47), channel_id=1, source_target_pairs={{0,3},{1,0},{2,1},{3,2},{4,7},{5,4},{6,5},{7,6},{8,11},{9,8},{10,9... | collective-permute-start | bytes 6291464 | tf_op jit(solution)/shard_map/ppermute | solution.py:148
  307.6 127.7 %collective-permute-start.18 = (bf16[2,64,8192]{2,1,0:T(8,128)(2,1)}, bf16[2,64,8192]{2,1,0:T(8,128)(2,1)}, u32[]{:S(2)}, u32[]{:S(2)}) collective-permute-start(bf16[2,64,8192]{2,1,0:T(8,128)(2,1)} %get-tuple-element.54), channel_id=1, source_target_pairs={{0,1},{1,2},{2,3},{3,0},{4,5},{5,6},{6,7},{7,4},{8,9},{9,10},{10,1... | collective-permute-start | bytes 6291464 | tf_op jit(solution)/shard_map/ppermute | solution.py:148
  345.3 2.8 copy-start.5
  345.3 91.4 %collective-permute-start.21 = (bf16[2,64,8192]{2,1,0:T(8,128)(2,1)}, bf16[2,64,8192]{2,1,0:T(8,128)(2,1)}, u32[]{:S(2)}, u32[]{:S(2)}) collective-permute-start(bf16[2,64,8192]{2,1,0:T(8,128)(2,1)} %get-tuple-element.53), channel_id=1, source_target_pairs={{0,3},{1,0},{2,1},{3,2},{4,7},{5,4},{6,5},{7,6},{8,11},{9,8},{10,9... | collective-permute-start | bytes 6291464 | tf_op jit(solution)/shard_map/ppermute | solution.py:148
  346.8 1.3 copy-start.6
  368.6 111.6 %collective-permute-start.10 = (bf16[2,64,8192]{2,1,0:T(8,128)(2,1)}, bf16[2,64,8192]{2,1,0:T(8,128)(2,1)S(1)}, u32[]{:S(2)}, u32[]{:S(2)}) collective-permute-start(bf16[2,64,8192]{2,1,0:T(8,128)(2,1)} %get-tuple-element.32), channel_id=1, source_target_pairs={{0,1},{1,2},{2,3},{3,0},{4,5},{5,6},{6,7},{7,4},{8,9},{9,10},{10,1... | collective-permute-start | bytes 6291464 | tf_op jit(solution)/shard_map/ppermute | solution.py:148
  411.0 114.2 %collective-permute-start.34 = (bf16[2,1024,512]{2,1,0:T(8,128)(2,1)}, bf16[2,1024,512]{2,1,0:T(8,128)(2,1)}, u32[]{:S(2)}, u32[]{:S(2)}) collective-permute-start(bf16[2,1024,512]{2,1,0:T(8,128)(2,1)} %get-tuple-element.38), channel_id=1, source_target_pairs={{0,1},{1,2},{2,3},{3,0},{4,5},{5,6},{6,7},{7,4},{8,9},{9,10},{10,1... | collective-permute-start | bytes 6291464 | tf_op jit(solution)/shard_map/ppermute | solution.py:148
  411.6 113.6 %collective-permute-start.37 = (bf16[2,1024,512]{2,1,0:T(8,128)(2,1)}, bf16[2,1024,512]{2,1,0:T(8,128)(2,1)}, u32[]{:S(2)}, u32[]{:S(2)}) collective-permute-start(bf16[2,1024,512]{2,1,0:T(8,128)(2,1)} %get-tuple-element.39), channel_id=1, source_target_pairs={{0,3},{1,0},{2,1},{3,2},{4,7},{5,4},{6,5},{7,6},{8,11},{9,8},{10,9... | collective-permute-start | bytes 6291464 | tf_op jit(solution)/shard_map/ppermute | solution.py:148
  435.3 93.1 %collective-permute-start.13 = (bf16[2,64,8192]{2,1,0:T(8,128)(2,1)}, bf16[2,64,8192]{2,1,0:T(8,128)(2,1)}, u32[]{:S(2)}, u32[]{:S(2)}) collective-permute-start(bf16[2,64,8192]{2,1,0:T(8,128)(2,1)} %get-tuple-element.33), channel_id=1, source_target_pairs={{0,3},{1,0},{2,1},{3,2},{4,7},{5,4},{6,5},{7,6},{8,11},{9,8},{10,9... | collective-permute-start | bytes 6291464 | tf_op jit(solution)/shard_map/ppermute | solution.py:148
  457.3 112.8 %collective-permute-start.22 = (bf16[2,64,8192]{2,1,0:T(8,128)(2,1)}, bf16[2,64,8192]{2,1,0:T(8,128)(2,1)S(1)}, u32[]{:S(2)}, u32[]{:S(2)}) collective-permute-start(bf16[2,64,8192]{2,1,0:T(8,128)(2,1)} %get-tuple-element.35), channel_id=1, source_target_pairs={{0,1},{1,2},{2,3},{3,0},{4,5},{5,6},{6,7},{7,4},{8,9},{9,10},{10,1... | collective-permute-start | bytes 6291464 | tf_op jit(solution)/shard_map/ppermute | solution.py:148
  480.2 360.7 %copy-start.2 = (bf16[2,64,8192]{2,1,0:T(8,128)(2,1)}, bf16[2,64,8192]{2,1,0:T(8,128)(2,1)S(1)}, u32[]{:S(2)}) copy-start(bf16[2,64,8192]{2,1,0:T(8,128)(2,1)S(1)} %collective-permute-done.10.up_ref) | copy-start | bytes 6291460
  480.2 91.3 %collective-permute-start.25 = (bf16[2,64,8192]{2,1,0:T(8,128)(2,1)}, bf16[2,64,8192]{2,1,0:T(8,128)(2,1)S(1)}, u32[]{:S(2)}, u32[]{:S(2)}) collective-permute-start(bf16[2,64,8192]{2,1,0:T(8,128)(2,1)} %get-tuple-element.36), channel_id=1, source_target_pairs={{0,3},{1,0},{2,1},{3,2},{4,7},{5,4},{6,5},{7,6},{8,11},{9,8},{10,9... | collective-permute-start | bytes 6291464 | tf_op jit(solution)/shard_map/ppermute | solution.py:148
  525.2 89.8 %collective-permute-start.35 = (bf16[2,1024,512]{2,1,0:T(8,128)(2,1)}, bf16[2,1024,512]{2,1,0:T(8,128)(2,1)S(1)}, u32[]{:S(2)}, u32[]{:S(2)}) collective-permute-start(bf16[2,1024,512]{2,1,0:T(8,128)(2,1)} %collective-permute-done.34.up_ref), channel_id=1, source_target_pairs={{0,1},{1,2},{2,3},{3,0},{4,5},{5,6},{6,7},{7,4},{8,9},{9,10},{10,1... | collective-permute-start | bytes 6291464 | tf_op jit(solution)/shard_map/ppermute | solution.py:148
  525.2 91.3 %collective-permute-start.38 = (bf16[2,1024,512]{2,1,0:T(8,128)(2,1)}, bf16[2,1024,512]{2,1,0:T(8,128)(2,1)S(1)}, u32[]{:S(2)}, u32[]{:S(2)}) collective-permute-start(bf16[2,1024,512]{2,1,0:T(8,128)(2,1)} %collective-permute-done.37.down_ref), channel_id=1, source_target_pairs={{0,3},{1,0},{2,1},{3,2},{4,7},{5,4},{6,5},{7,6},{8,11},{9,8},{10,9... | collective-permute-start | bytes 6291464 | tf_op jit(solution)/shard_map/ppermute | solution.py:148
  528.5 131.6 %collective-permute-start.11 = (bf16[2,64,8192]{2,1,0:T(8,128)(2,1)S(1)}, bf16[2,64,8192]{2,1,0:T(8,128)(2,1)}, u32[]{:S(2)}, u32[]{:S(2)}) collective-permute-start(bf16[2,64,8192]{2,1,0:T(8,128)(2,1)S(1)} %collective-permute-done.10.up_ref), channel_id=1, source_target_pairs={{0,1},{1,2},{2,3},{3,0},{4,5},{5,6},{6,7},{7,4},{8,9},{9,10},{10,1... | collective-permute-start | bytes 6291464 | tf_op jit(solution)/shard_map/ppermute | solution.py:148
  570.0 182.1 %copy-start.3 = (bf16[2,64,8192]{2,1,0:T(8,128)(2,1)}, bf16[2,64,8192]{2,1,0:T(8,128)(2,1)S(1)}, u32[]{:S(2)}) copy-start(bf16[2,64,8192]{2,1,0:T(8,128)(2,1)S(1)} %collective-permute-done.22.up_ref) | copy-start | bytes 6291460
  570.0 91.5 %collective-permute-start.14 = (bf16[2,64,8192]{2,1,0:T(8,128)(2,1)}, bf16[2,64,8192]{2,1,0:T(8,128)(2,1)}, u32[]{:S(2)}, u32[]{:S(2)}) collective-permute-start(bf16[2,64,8192]{2,1,0:T(8,128)(2,1)} %collective-permute-done.13.down_ref), channel_id=1, source_target_pairs={{0,3},{1,0},{2,1},{3,2},{4,7},{5,4},{6,5},{7,6},{8,11},{9,8},{10,9... | collective-permute-start | bytes 6291464 | tf_op jit(solution)/shard_map/ppermute | solution.py:148
  571.5 265.6 %copy-start.4 = (bf16[2,64,8192]{2,1,0:T(8,128)(2,1)}, bf16[2,64,8192]{2,1,0:T(8,128)(2,1)S(1)}, u32[]{:S(2)}) copy-start(bf16[2,64,8192]{2,1,0:T(8,128)(2,1)S(1)} %collective-permute-done.25.down_ref) | copy-start | bytes 6291460
  571.5 133.5 %collective-permute-start.23 = (bf16[2,64,8192]{2,1,0:T(8,128)(2,1)S(1)}, bf16[2,64,8192]{2,1,0:T(8,128)(2,1)}, u32[]{:S(2)}, u32[]{:S(2)}) collective-permute-start(bf16[2,64,8192]{2,1,0:T(8,128)(2,1)S(1)} %collective-permute-done.22.up_ref), channel_id=1, source_target_pairs={{0,1},{1,2},{2,3},{3,0},{4,5},{5,6},{6,7},{7,4},{8,9},{9,10},{10,1... | collective-permute-start | bytes 6291464 | tf_op jit(solution)/shard_map/ppermute | solution.py:148
  615.0 92.2 %copy-start = (bf16[2,1024,512]{2,1,0:T(8,128)(2,1)}, bf16[2,1024,512]{2,1,0:T(8,128)(2,1)S(1)}, u32[]{:S(2)}) copy-start(bf16[2,1024,512]{2,1,0:T(8,128)(2,1)S(1)} %collective-permute-done.35.up_ref) | copy-start | bytes 6291460
  615.0 91.4 %collective-permute-start.26 = (bf16[2,64,8192]{2,1,0:T(8,128)(2,1)S(1)}, bf16[2,64,8192]{2,1,0:T(8,128)(2,1)}, u32[]{:S(2)}, u32[]{:S(2)}) collective-permute-start(bf16[2,64,8192]{2,1,0:T(8,128)(2,1)S(1)} %collective-permute-done.25.down_ref), channel_id=1, source_target_pairs={{0,3},{1,0},{2,1},{3,2},{4,7},{5,4},{6,5},{7,6},{8,11},{9,8},{10,9... | collective-permute-start | bytes 6291464 | tf_op jit(solution)/shard_map/ppermute | solution.py:148
  616.5 135.6 %copy-start.1 = (bf16[2,1024,512]{2,1,0:T(8,128)(2,1)}, bf16[2,1024,512]{2,1,0:T(8,128)(2,1)S(1)}, u32[]{:S(2)}) copy-start(bf16[2,1024,512]{2,1,0:T(8,128)(2,1)S(1)} %collective-permute-done.38.down_ref) | copy-start | bytes 6291460
  616.5 110.9 %collective-permute-start.42 = (bf16[1,704,512]{2,1,0:T(8,128)(2,1)S(1)}, bf16[1,704,512]{2,1,0:T(8,128)(2,1)S(1)}, u32[]{:S(2)}, u32[]{:S(2)}) collective-permute-start(bf16[1,704,512]{2,1,0:T(8,128)(2,1)S(1)} %slice.36), channel_id=1, source_target_pairs={{0,1},{1,2},{2,3},{3,0},{4,5},{5,6},{6,7},{7,4},{8,9},{9,10},{10,1... | collective-permute-start | bytes 2162696 | tf_op jit(solution)/shard_map/ppermute | solution.py:148
  660.0 67.6 %collective-permute-start.43 = (bf16[1,704,512]{2,1,0:T(8,128)(2,1)S(1)}, bf16[1,704,512]{2,1,0:T(8,128)(2,1)S(1)}, u32[]{:S(2)}, u32[]{:S(2)}) collective-permute-start(bf16[1,704,512]{2,1,0:T(8,128)(2,1)S(1)} %slice.37), channel_id=1, source_target_pairs={{0,3},{1,0},{2,1},{3,2},{4,7},{5,4},{6,5},{7,6},{8,11},{9,8},{10,9... | collective-permute-start | bytes 2162696 | tf_op jit(solution)/shard_map/ppermute | solution.py:148
  661.5 62.5 %collective-permute-start.40 = (bf16[1,240,512]{2,1,0:T(8,128)(2,1)S(1)}, bf16[1,240,512]{2,1,0:T(8,128)(2,1)S(1)}, u32[]{:S(2)}, u32[]{:S(2)}) collective-permute-start(bf16[1,240,512]{2,1,0:T(8,128)(2,1)S(1)} %slice.34), channel_id=1, source_target_pairs={{0,1},{1,2},{2,3},{3,0},{4,5},{5,6},{6,7},{7,4},{8,9},{9,10},{10,1... | collective-permute-start | bytes 737288 | tf_op jit(solution)/shard_map/ppermute | solution.py:148
  705.0 20.1 %collective-permute-start.41 = (bf16[1,240,512]{2,1,0:T(8,128)(2,1)S(1)}, bf16[1,240,512]{2,1,0:T(8,128)(2,1)S(1)}, u32[]{:S(2)}, u32[]{:S(2)}) collective-permute-start(bf16[1,240,512]{2,1,0:T(8,128)(2,1)S(1)} %slice.35), channel_id=1, source_target_pairs={{0,3},{1,0},{2,1},{3,2},{4,7},{5,4},{6,5},{7,6},{8,11},{9,8},{10,9... | collective-permute-start | bytes 737288 | tf_op jit(solution)/shard_map/ppermute | solution.py:148
  706.4 17.6 %collective-permute-start.36 = (bf16[1,80,512]{2,1,0:T(8,128)(2,1)S(1)}, bf16[1,80,512]{2,1,0:T(8,128)(2,1)S(1)}, u32[]{:S(2)}, u32[]{:S(2)}) collective-permute-start(bf16[1,80,512]{2,1,0:T(8,128)(2,1)S(1)} %slice.32), channel_id=1, source_target_pairs={{0,1},{1,2},{2,3},{3,0},{4,5},{5,6},{6,7},{7,4},{8,9},{9,10},{10,1... | collective-permute-start | bytes 245768 | tf_op jit(solution)/shard_map/ppermute | solution.py:148
  724.1 27.2 %collective-permute-start.44 = (bf16[1,1024,512]{2,1,0:T(8,128)(2,1)S(1)}, bf16[1,1024,512]{2,1,0:T(8,128)(2,1)S(1)}, u32[]{:S(2)}, u32[]{:S(2)}) collective-permute-start(bf16[1,1024,512]{2,1,0:T(8,128)(2,1)S(1)} %slice.38), channel_id=1, source_target_pairs={{0,1},{1,2},{2,3},{3,0},{4,5},{5,6},{6,7},{7,4},{8,9},{9,10},{10,1... | collective-permute-start | bytes 3145736 | tf_op jit(solution)/shard_map/ppermute | solution.py:148
  724.1 143.0 %collective-permute-start.12 = (bf16[2,64,8192]{2,1,0:T(8,128)(2,1)}, bf16[2,64,8192]{2,1,0:T(8,128)(2,1)}, u32[]{:S(2)}, u32[]{:S(2)}) collective-permute-start(bf16[2,64,8192]{2,1,0:T(8,128)(2,1)} %collective-permute-done.11.up_ref), channel_id=1, source_target_pairs={{0,1},{1,2},{2,3},{3,0},{4,5},{5,6},{6,7},{7,4},{8,9},{9,10},{10,1... | collective-permute-start | bytes 6291464 | tf_op jit(solution)/shard_map/ppermute | solution.py:148
  725.0 142.1 %collective-permute-start.15 = (bf16[2,64,8192]{2,1,0:T(8,128)(2,1)}, bf16[2,64,8192]{2,1,0:T(8,128)(2,1)}, u32[]{:S(2)}, u32[]{:S(2)}) collective-permute-start(bf16[2,64,8192]{2,1,0:T(8,128)(2,1)} %collective-permute-done.14.down_ref), channel_id=1, source_target_pairs={{0,3},{1,0},{2,1},{3,2},{4,7},{5,4},{6,5},{7,6},{8,11},{9,8},{10,9... | collective-permute-start | bytes 6291464 | tf_op jit(solution)/shard_map/ppermute | solution.py:148
  727.4 116.7 %copy-start.11 = (bf16[1,704,512]{2,1,0:T(8,128)(2,1)}, bf16[1,704,512]{2,1,0:T(8,128)(2,1)S(1)}, u32[]{:S(2)}) copy-start(bf16[1,704,512]{2,1,0:T(8,128)(2,1)S(1)} %collective-permute-done.42.up_ref) | copy-start | bytes 2162692
  727.4 143.0 %collective-permute-start.24 = (bf16[2,64,8192]{2,1,0:T(8,128)(2,1)}, bf16[2,64,8192]{2,1,0:T(8,128)(2,1)}, u32[]{:S(2)}, u32[]{:S(2)}) collective-permute-start(bf16[2,64,8192]{2,1,0:T(8,128)(2,1)} %collective-permute-done.23.up_ref), channel_id=1, source_target_pairs={{0,1},{1,2},{2,3},{3,0},{4,5},{5,6},{6,7},{7,4},{8,9},{9,10},{10,1... | collective-permute-start | bytes 6291464 | tf_op jit(solution)/shard_map/ppermute | solution.py:148
  727.6 113.2 %copy-start.12 = (bf16[1,704,512]{2,1,0:T(8,128)(2,1)}, bf16[1,704,512]{2,1,0:T(8,128)(2,1)S(1)}, u32[]{:S(2)}) copy-start(bf16[1,704,512]{2,1,0:T(8,128)(2,1)S(1)} %collective-permute-done.43.down_ref) | copy-start | bytes 2162692
  727.6 142.8 %collective-permute-start.27 = (bf16[2,64,8192]{2,1,0:T(8,128)(2,1)}, bf16[2,64,8192]{2,1,0:T(8,128)(2,1)}, u32[]{:S(2)}, u32[]{:S(2)}) collective-permute-start(bf16[2,64,8192]{2,1,0:T(8,128)(2,1)} %collective-permute-done.26.down_ref), channel_id=1, source_target_pairs={{0,3},{1,0},{2,1},{3,2},{4,7},{5,4},{6,5},{7,6},{8,11},{9,8},{10,9... | collective-permute-start | bytes 6291464 | tf_op jit(solution)/shard_map/ppermute | solution.py:148
  751.3 89.5 %copy-start.7 = (bf16[1,1024,512]{2,1,0:T(8,128)(2,1)}, bf16[1,1024,512]{2,1,0:T(8,128)(2,1)S(1)}, u32[]{:S(2)}) copy-start(bf16[1,1024,512]{2,1,0:T(8,128)(2,1)S(1)} %collective-permute-done.44.up_ref) | copy-start | bytes 3145732
  751.3 85.8 %collective-permute-start.45 = (bf16[1,1024,512]{2,1,0:T(8,128)(2,1)S(1)}, bf16[1,1024,512]{2,1,0:T(8,128)(2,1)S(1)}, u32[]{:S(2)}, u32[]{:S(2)}) collective-permute-start(bf16[1,1024,512]{2,1,0:T(8,128)(2,1)S(1)} %slice.39), channel_id=1, source_target_pairs={{0,3},{1,0},{2,1},{3,2},{4,7},{5,4},{6,5},{7,6},{8,11},{9,8},{10,9... | collective-permute-start | bytes 3145736 | tf_op jit(solution)/shard_map/ppermute | solution.py:148
  837.1 3.7 copy-start.8
  837.1 29.3 %collective-permute-start.39 = (bf16[1,80,512]{2,1,0:T(8,128)(2,1)S(1)}, bf16[1,80,512]{2,1,0:T(8,128)(2,1)S(1)}, u32[]{:S(2)}, u32[]{:S(2)}) collective-permute-start(bf16[1,80,512]{2,1,0:T(8,128)(2,1)S(1)} %slice.33), channel_id=1, source_target_pairs={{0,3},{1,0},{2,1},{3,2},{4,7},{5,4},{6,5},{7,6},{8,11},{9,8},{10,9... | collective-permute-start | bytes 245768 | tf_op jit(solution)/shard_map/ppermute | solution.py:148
